TPU v7x, 768 devices: a whole 4x8x12 slice. The times are simulated.
768 devices in a mesh: gx: 96 (over z_hi, x, y), gy: 8 (over z_lo, core).
Axes of the slice: x: 4, y: 8, z: 12 (z_hi: 3, z_lo: 4; z = z_hi * 4 + z_lo), core: 2. Of those that a mesh axis runs over, the one named last changes fastest.
Arguments:
- right_side: float32 [384, 512, 256], P('gx', 'gy'), may hold values from -40 to 40
- kappa_sq: float32 [384, 512, 256], P('gx', 'gy'), may hold values from 0.5 to 4
Outputs:
- solution_field: float32 [384, 512, 256], P('gx', 'gy')
- residual: float32 [384, 512, 256], P('gx', 'gy')
- residual_rms: float32 [3], replicated
All inputs are finite; a program needn't handle non-finite values.
Results may differ from a plain program's by a relative error of at most 0.00016.
Values sent between devices are 32-bit elements; how exact they have to be, the bound alone decides.
No kernel may reach another device: no remote copies, remote signals or barrier semaphores. Data moves between devices by JAX's collectives and lax.ppermute only.
A program may use at most 32 MiB of HBM per device.

v0:
```python
import jax
import jax.numpy as jnp
from jax import lax
from jax.sharding import Mesh
from jax.sharding import PartitionSpec as P

ITERS = 3
GX_GY = ("gx_0", "gx_1", "gx_2", "gy_0", "gy_1")
GX = ("gx_0", "gx_1", "gx_2")
GY = ("gy_0", "gy_1")


def extended(x, sides, width):
    for axis, dim in sides:
        size, length = (lax.axis_size(axis), x.shape[dim])
        up = [(i, (i + 1) % size) for i in range(size)]
        down = [(j, i) for i, j in up]
        last = lax.slice_in_dim(x, length - width, length, axis=dim)
        first = lax.slice_in_dim(x, 0, width, axis=dim)
        before = lax.ppermute(last, axis, up)
        after = lax.ppermute(first, axis, down)
        x = jnp.concatenate([before, x, after], axis=dim)
    return x


def extended_2(x, sides, width):
    edges = {}
    for axis, dim in sides:
        size, length = (lax.axis_size(axis), x.shape[dim])
        up = [(i, (i + 1) % size) for i in range(size)]
        last = lax.slice_in_dim(x, length - width, length, axis=dim)
        first = lax.slice_in_dim(x, 0, width, axis=dim)
        edges[dim] = (
            lax.ppermute(last, axis, up),
            lax.ppermute(first, axis, [(b, a) for a, b in up]),
        )
    done = []
    for _, dim in sides:
        low, high = edges[dim]
        around = [(width, width) if d in done else (0, 0) for d in range(x.ndim)]
        x = jnp.concatenate([jnp.pad(low, around), x, jnp.pad(high, around)], axis=dim)
        done.append(dim)
    return x


def by_axis(x, axes):
    for axis in axes:
        x = lax.psum(x, axis)
    return x


def zbeside(field):
    return jnp.roll(field, 1, 2) + jnp.roll(field, -1, 2)


def operate_double(field, kappa_wide, kappa_sq):
    padded = extended(field, ((GX, 0), (GY, 1)), 2)
    center = padded[1:-1, 1:-1]
    beside = padded[2:, 1:-1] + padded[:-2, 1:-1]
    beside = beside + padded[1:-1, 2:] + padded[1:-1, :-2]
    beside = beside + zbeside(center)
    middle = (6.0 + kappa_wide) * center - beside
    inner = middle[1:-1, 1:-1]
    outer = middle[2:, 1:-1] + middle[:-2, 1:-1]
    outer = outer + middle[1:-1, 2:] + middle[1:-1, :-2]
    outer = outer + zbeside(inner)
    return (6.0 + kappa_sq) * inner - outer


def body(right_side, kappa_sq):
    shifted = 6.0 + kappa_sq
    precond = 1.0 / (shifted * shifted + 6.0)
    cells = (
        right_side.shape[0]
        * lax.axis_size(GX)
        * right_side.shape[1]
        * lax.axis_size(GY)
        * right_side.shape[2]
    )
    kappa_wide = extended_2(kappa_sq, ((GX, 0), (GY, 1)), 1)

    def operate(field):
        return operate_double(field, kappa_wide, kappa_sq)

    solution_field = jnp.zeros_like(right_side)
    residual = right_side
    u_vec = precond * residual
    w_vec = operate(u_vec)
    p_vec = jnp.zeros_like(right_side)
    s_vec = jnp.zeros_like(right_side)
    q_vec = jnp.zeros_like(right_side)
    z_vec = jnp.zeros_like(right_side)
    norms = []
    gamma_old = jnp.float32(1.0)
    alpha_old = jnp.float32(1.0)
    for step in range(ITERS):
        gamma, delta, norm_sq = (
            by_axis(jnp.sum(residual * u_vec), GX_GY),
            by_axis(jnp.sum(w_vec * u_vec), GX_GY),
            by_axis(jnp.sum(residual * residual), GX_GY),
        )
        norms.append(jnp.sqrt(norm_sq / cells))
        m_vec = precond * w_vec
        n_vec = operate(m_vec)
        if step == 0:
            beta = jnp.float32(0.0)
            alpha = gamma / delta
        else:
            beta = gamma / gamma_old
            alpha = gamma / (delta - beta * gamma / alpha_old)
        z_vec = n_vec + beta * z_vec
        q_vec = m_vec + beta * q_vec
        s_vec = w_vec + beta * s_vec
        p_vec = u_vec + beta * p_vec
        solution_field = solution_field + alpha * p_vec
        residual = residual - alpha * s_vec
        u_vec = u_vec - alpha * q_vec
        w_vec = w_vec - alpha * z_vec
        gamma_old = gamma
        alpha_old = alpha
    return (solution_field, residual, jnp.stack(norms))


def solution(mesh):
    finer = Mesh(mesh.devices.reshape(3, 4, 8, 4, 2), ("gx_0", "gx_1", "gx_2", "gy_0", "gy_1"))
    in_specs = (P(GX, GY, None), P(GX, GY, None))
    out_specs = (P(GX, GY, None), P(GX, GY, None), P())
    return jax.shard_map(body, mesh=finer, in_specs=in_specs, out_specs=out_specs, check_vma=False)
```

profile of v0, /device:TPU:1, one launch (start us, length us, event | category | flops | bytes accessed | tf_op | source)
XLA Modules:
  0.0 293.2 jit_solution(4108338896056886561)
XLA Ops:
  0.6 1.1 fusion.24
  1.7 0.0 copy-start
  1.8 4.2 %collective-permute-start.4 = (f32[2,64,256]{2,1,0:T(8,128)S(1)}, f32[2,64,256]{2,1,0:T(8,128)S(1)}, u32[]{:S(2)}, u32[]{:S(2)}) collective-permute-start(f32[2,64,256]{2,1,0:T(8,128)S(1)} %get-tuple-element.99), channel_id=1, source_target_pairs={{0,8},{8,16},{16,24},{24,32},{32,40},{40,48},{48,56},{56,64},{64,7... | collective-permute-start | bytes 393224 | tf_op jit(solution)/shard_map/ppermute | solution.py:20
  5.9 18.1 %collective-permute-start.5 = (f32[2,64,256]{2,1,0:T(8,128)S(1)}, f32[2,64,256]{2,1,0:T(8,128)S(1)}, u32[]{:S(2)}, u32[]{:S(2)}) collective-permute-start(f32[2,64,256]{2,1,0:T(8,128)S(1)} %get-tuple-element.100), channel_id=1, source_target_pairs={{8,0},{16,8},{24,16},{32,24},{40,32},{48,40},{56,48},{64,56},{72,6... | collective-permute-start | bytes 393224 | tf_op jit(solution)/shard_map/ppermute | solution.py:21
  24.0 3.9 %collective-permute-start = (f32[4,1,256]{2,1,0:T(1,128)S(1)}, f32[4,1,256]{2,1,0:T(1,128)S(1)}, u32[]{:S(2)}, u32[]{:S(2)}) collective-permute-start(f32[4,1,256]{2,1,0:T(1,128)S(1)} %get-tuple-element.95), channel_id=1, source_target_pairs={{0,1},{1,2},{2,3},{3,4},{4,5},{5,6},{6,7},{7,0},{8,9},{9,10},{10,1... | collective-permute-start | bytes 12296 | tf_op jit(solution)/shard_map/ppermute | solution.py:34
  28.0 2.2 collective-permute-start.3
  30.3 8.8 %collective-permute-start.7 = (f32[8,2,256]{2,1,0:T(2,128)S(1)}, f32[8,2,256]{2,1,0:T(2,128)S(1)}, u32[]{:S(2)}, u32[]{:S(2)}) collective-permute-start(f32[8,2,256]{2,1,0:T(2,128)S(1)} %get-tuple-element.77), channel_id=1, source_target_pairs={{1,0},{2,1},{3,2},{4,3},{5,4},{6,5},{7,6},{0,7},{9,8},{10,9},{11,1... | collective-permute-start | bytes 49160 | tf_op jit(solution)/shard_map/ppermute | solution.py:21
  39.0 1.9 collective-permute-start.6
  41.0 1.9 collective-permute-start.1
  42.9 12.2 %collective-permute-start.2 = (f32[1,64,256]{2,1,0:T(8,128)S(1)}, f32[1,64,256]{2,1,0:T(8,128)S(1)}, u32[]{:S(2)}, u32[]{:S(2)}) collective-permute-start(f32[1,64,256]{2,1,0:T(8,128)S(1)} %get-tuple-element.98), channel_id=1, source_target_pairs={{8,0},{16,8},{24,16},{32,24},{40,32},{48,40},{56,48},{64,56},{72,6... | collective-permute-start | bytes 196616 | tf_op jit(solution)/shard_map/ppermute | solution.py:35
  55.2 0.1 pad_maximum_fusion
  55.2 0.2 fusion.32
  55.4 0.1 fusion.33
  55.6 5.4 %collective-permute-done.2 = f32[1,64,256]{2,1,0:T(8,128)S(1)} collective-permute-done((f32[1,64,256]{2,1,0:T(8,128)S(1)}, f32[1,64,256]{2,1,0:T(8,128)S(1)}, u32[]{:S(2)}, u32[]{:S(2)}) %collective-permute-start.2) | collective-permute-done | bytes 65568 | tf_op jit(solution)/shard_map/ppermute | solution.py:35
  61.0 0.4 fusion.10
  61.3 0.1 fusion.38
  61.5 0.1 fusion.39
  61.6 0.8 copy-done.1
  62.4 0.8 multiply_reduce_fusion.7
  63.2 0.1 fusion.23
  63.3 1.9 collective-permute-start.8
  65.2 12.4 %collective-permute-start.9 = (f32[2,64,256]{2,1,0:T(8,128)S(1)}, f32[2,64,256]{2,1,0:T(8,128)S(1)}, u32[]{:S(2)}, u32[]{:S(2)}) collective-permute-start(f32[2,64,256]{2,1,0:T(8,128)S(1)} %get-tuple-element.94), channel_id=1, source_target_pairs={{8,0},{16,8},{24,16},{32,24},{40,32},{48,40},{56,48},{64,56},{72,6... | collective-permute-start | bytes 393224 | tf_op jit(solution)/shard_map/ppermute | solution.py:21
  77.6 5.5 %collective-permute-done.8 = f32[2,64,256]{2,1,0:T(8,128)S(1)} collective-permute-done((f32[2,64,256]{2,1,0:T(8,128)S(1)}, f32[2,64,256]{2,1,0:T(8,128)S(1)}, u32[]{:S(2)}, u32[]{:S(2)}) %collective-permute-start.8) | collective-permute-done | bytes 131104 | tf_op jit(solution)/shard_map/ppermute | solution.py:20
  83.2 2.4 collective-permute-done.9
  85.6 2.6 collective-permute-start.11
  88.2 3.0 %collective-permute-start.10 = (f32[8,2,256]{2,1,0:T(2,128)S(1)}, f32[8,2,256]{2,1,0:T(2,128)S(1)}, u32[]{:S(2)}, u32[]{:S(2)}) collective-permute-start(f32[8,2,256]{2,1,0:T(2,128)S(1)} %get-tuple-element.76), channel_id=1, source_target_pairs={{0,1},{1,2},{2,3},{3,4},{4,5},{5,6},{6,7},{7,0},{8,9},{9,10},{10,1... | collective-permute-start | bytes 49160 | tf_op jit(solution)/shard_map/ppermute | solution.py:20
  91.2 9.5 %all-reduce.13 = (f32[]{:T(128)}, f32[]{:T(128)}) all-reduce(f32[]{:T(128)} %get-tuple-element.11, f32[]{:T(128)} %get-tuple-element.10), channel_id=1, replica_groups=mesh['gx_0'=3,'gx_1'=4,'gx_2'=8,'gy_0'=4,'gy_1'=2] {'gx_0'}, use_global_device_ids=true, to_apply=%region_1.2 | all-reduce | flops 2 | bytes 16 | tf_op jit(solution)/shard_map/psum | solution.py:48
  100.7 6.8 %all-reduce.10 = (f32[]{:T(128)}, f32[]{:T(128)}) all-reduce(f32[]{:T(128)} %get-tuple-element.46, f32[]{:T(128)} %get-tuple-element.47), channel_id=1, replica_groups=mesh['gx_0'=3,'gx_1'=4,'gx_2'=8,'gy_0'=4,'gy_1'=2] {'gx_1'}, use_global_device_ids=true, to_apply=%region_2.3 | all-reduce | flops 2 | bytes 16 | tf_op jit(solution)/shard_map/psum | solution.py:48
  107.4 19.5 %all-reduce.4 = (f32[]{:T(128)}, f32[]{:T(128)}) all-reduce(f32[]{:T(128)} %get-tuple-element.37, f32[]{:T(128)} %get-tuple-element.38), channel_id=1, replica_groups=mesh['gx_0'=3,'gx_1'=4,'gx_2'=8,'gy_0'=4,'gy_1'=2] {'gx_2'}, use_global_device_ids=true, to_apply=%region_3.4 | all-reduce | flops 2 | bytes 16 | tf_op jit(solution)/shard_map/psum | solution.py:48
  126.9 9.4 %all-reduce.7 = (f32[]{:T(128)}, f32[]{:T(128)}) all-reduce(f32[]{:T(128)} %get-tuple-element.19, f32[]{:T(128)} %get-tuple-element.20), channel_id=1, replica_groups=mesh['gx_0'=3,'gx_1'=4,'gx_2'=8,'gy_0'=4,'gy_1'=2] {'gy_0'}, use_global_device_ids=true, to_apply=%region_4.5 | all-reduce | flops 2 | bytes 16 | tf_op jit(solution)/shard_map/psum | solution.py:48
  136.2 9.6 %all-reduce.16 = (f32[]{:T(128)}, f32[]{:T(128)}) all-reduce(f32[]{:T(128)} %get-tuple-element.28, f32[]{:T(128)} %get-tuple-element.29), channel_id=1, replica_groups=mesh['gx_0'=3,'gx_1'=4,'gx_2'=8,'gy_0'=4,'gy_1'=2] {'gy_1'}, use_global_device_ids=true, to_apply=%region_5.6 | all-reduce | flops 2 | bytes 16 | tf_op jit(solution)/shard_map/psum | solution.py:48
  147.2 0.1 pad_maximum_fusion.1
  147.3 0.1 fusion.31
  147.4 0.2 fusion.30
  147.6 0.4 fusion.6
  148.0 0.1 fusion.36
  148.1 0.1 fusion.37
  148.2 1.0 multiply_reduce_fusion.5
  149.2 0.1 fusion.22
  149.3 1.9 collective-permute-start.12
  151.2 11.5 %collective-permute-start.13 = (f32[2,64,256]{2,1,0:T(8,128)S(1)}, f32[2,64,256]{2,1,0:T(8,128)S(1)}, u32[]{:S(2)}, u32[]{:S(2)}) collective-permute-start(f32[2,64,256]{2,1,0:T(8,128)S(1)} %get-tuple-element.92), channel_id=1, source_target_pairs={{8,0},{16,8},{24,16},{32,24},{40,32},{48,40},{56,48},{64,56},{72,6... | collective-permute-start | bytes 393224 | tf_op jit(solution)/shard_map/ppermute | solution.py:21
  162.7 8.5 %collective-permute-done.12 = f32[2,64,256]{2,1,0:T(8,128)S(1)} collective-permute-done((f32[2,64,256]{2,1,0:T(8,128)S(1)}, f32[2,64,256]{2,1,0:T(8,128)S(1)}, u32[]{:S(2)}, u32[]{:S(2)}) %collective-permute-start.12) | collective-permute-done | bytes 131104 | tf_op jit(solution)/shard_map/ppermute | solution.py:20
  171.2 2.2 collective-permute-done.13
  173.4 2.4 collective-permute-start.15
  175.8 3.2 %collective-permute-start.14 = (f32[8,2,256]{2,1,0:T(2,128)S(1)}, f32[8,2,256]{2,1,0:T(2,128)S(1)}, u32[]{:S(2)}, u32[]{:S(2)}) collective-permute-start(f32[8,2,256]{2,1,0:T(2,128)S(1)} %get-tuple-element.74), channel_id=1, source_target_pairs={{0,1},{1,2},{2,3},{3,4},{4,5},{5,6},{6,7},{7,0},{8,9},{9,10},{10,1... | collective-permute-start | bytes 49160 | tf_op jit(solution)/shard_map/ppermute | solution.py:20
  179.0 8.5 %all-reduce.12 = (f32[]{:T(128)}, f32[]{:T(128)}) all-reduce(f32[]{:T(128)} %get-tuple-element.6, f32[]{:T(128)} %get-tuple-element.5), channel_id=1, replica_groups=mesh['gx_0'=3,'gx_1'=4,'gx_2'=8,'gy_0'=4,'gy_1'=2] {'gx_0'}, use_global_device_ids=true, to_apply=%region_13.14 | all-reduce | flops 2 | bytes 16 | tf_op jit(solution)/shard_map/psum | solution.py:48
  187.5 6.8 %all-reduce.9 = (f32[]{:T(128)}, f32[]{:T(128)}) all-reduce(f32[]{:T(128)} %get-tuple-element.44, f32[]{:T(128)} %get-tuple-element.45), channel_id=1, replica_groups=mesh['gx_0'=3,'gx_1'=4,'gx_2'=8,'gy_0'=4,'gy_1'=2] {'gx_1'}, use_global_device_ids=true, to_apply=%region_14.15 | all-reduce | flops 2 | bytes 16 | tf_op jit(solution)/shard_map/psum | solution.py:48
  194.3 19.6 %all-reduce.3 = (f32[]{:T(128)}, f32[]{:T(128)}) all-reduce(f32[]{:T(128)} %get-tuple-element.35, f32[]{:T(128)} %get-tuple-element.36), channel_id=1, replica_groups=mesh['gx_0'=3,'gx_1'=4,'gx_2'=8,'gy_0'=4,'gy_1'=2] {'gx_2'}, use_global_device_ids=true, to_apply=%region_15.16 | all-reduce | flops 2 | bytes 16 | tf_op jit(solution)/shard_map/psum | solution.py:48
  213.9 9.1 %all-reduce.6 = (f32[]{:T(128)}, f32[]{:T(128)}) all-reduce(f32[]{:T(128)} %get-tuple-element.17, f32[]{:T(128)} %get-tuple-element.18), channel_id=1, replica_groups=mesh['gx_0'=3,'gx_1'=4,'gx_2'=8,'gy_0'=4,'gy_1'=2] {'gy_0'}, use_global_device_ids=true, to_apply=%region_16.17 | all-reduce | flops 2 | bytes 16 | tf_op jit(solution)/shard_map/psum | solution.py:48
  222.9 9.9 %all-reduce.15 = (f32[]{:T(128)}, f32[]{:T(128)}) all-reduce(f32[]{:T(128)} %get-tuple-element.26, f32[]{:T(128)} %get-tuple-element.27), channel_id=1, replica_groups=mesh['gx_0'=3,'gx_1'=4,'gx_2'=8,'gy_0'=4,'gy_1'=2] {'gy_1'}, use_global_device_ids=true, to_apply=%region_17.18 | all-reduce | flops 2 | bytes 16 | tf_op jit(solution)/shard_map/psum | solution.py:48
  237.6 0.1 pad_maximum_fusion.2
  237.7 0.1 fusion.29
  237.8 0.2 fusion.28
  238.0 0.4 fusion.2
  238.4 0.1 fusion.34
  238.5 0.1 fusion.35
  238.6 1.0 multiply_reduce_fusion
  239.7 8.4 %all-reduce.11 = (f32[]{:T(128)}, f32[]{:T(128)}, f32[]{:T(128)}, f32[]{:T(128)}, f32[]{:T(128)}) all-reduce(f32[]{:T(128)} %get-tuple-element.4, f32[]{:T(128)} %get-tuple-element.9, f32[]{:T(128)} %get-tuple-element.3, f32[]{:T(128)} %get-tuple-element.7, ...), channel_id=1, replica_groups=mesh['gx_0'=3,'gx_1'=4,'gx_2'=8,'gy_0'=4,'gy_1'=2] {'gx_0'}, use_global_device_ids=true, to_apply=%region_25.26 | all-reduce | flops 5 | bytes 40 | tf_op jit(solution)/shard_map/psum | solution.py:48
  248.0 6.7 %all-reduce.8 = (f32[]{:T(128)}, f32[]{:T(128)}, f32[]{:T(128)}, f32[]{:T(128)}, f32[]{:T(128)}) all-reduce(f32[]{:T(128)} %get-tuple-element.39, f32[]{:T(128)} %get-tuple-element.40, f32[]{:T(128)} %get-tuple-element.41, f32[]{:T(128)} %get-tuple-element.42, ...), channel_id=1, replica_groups=mesh['gx_0'=3,'gx_1'=4,'gx_2'=8,'gy_0'=4,'gy_1'=2] {'gx_1'}, use_global_device_ids=true, to_apply=%region_26.27 | all-reduce | flops 5 | bytes 40 | tf_op jit(solution)/shard_map/psum | solution.py:48
  254.7 11.4 %all-reduce.2 = (f32[]{:T(128)}, f32[]{:T(128)}, f32[]{:T(128)}, f32[]{:T(128)}, f32[]{:T(128)}) all-reduce(f32[]{:T(128)} %get-tuple-element.30, f32[]{:T(128)} %get-tuple-element.31, f32[]{:T(128)} %get-tuple-element.32, f32[]{:T(128)} %get-tuple-element.33, ...), channel_id=1, replica_groups=mesh['gx_0'=3,'gx_1'=4,'gx_2'=8,'gy_0'=4,'gy_1'=2] {'gx_2'}, use_global_device_ids=true, to_apply=%region_27.28 | all-reduce | flops 5 | bytes 40 | tf_op jit(solution)/shard_map/psum | solution.py:48
  266.1 7.9 %all-reduce.5 = (f32[]{:T(128)}, f32[]{:T(128)}, f32[]{:T(128)}, f32[]{:T(128)}, f32[]{:T(128)}) all-reduce(f32[]{:T(128)} %get-tuple-element.12, f32[]{:T(128)} %get-tuple-element.13, f32[]{:T(128)} %get-tuple-element.14, f32[]{:T(128)} %get-tuple-element.15, ...), channel_id=1, replica_groups=mesh['gx_0'=3,'gx_1'=4,'gx_2'=8,'gy_0'=4,'gy_1'=2] {'gy_0'}, use_global_device_ids=true, to_apply=%region_28.29 | all-reduce | flops 5 | bytes 40 | tf_op jit(solution)/shard_map/psum | solution.py:48
  274.0 11.5 %all-reduce.14 = (f32[]{:T(128)}, f32[]{:T(128)}, f32[]{:T(128)}, f32[]{:T(128)}, f32[]{:T(128)}) all-reduce(f32[]{:T(128)} %get-tuple-element.21, f32[]{:T(128)} %get-tuple-element.22, f32[]{:T(128)} %get-tuple-element.23, f32[]{:T(128)} %get-tuple-element.24, ...), channel_id=1, replica_groups=mesh['gx_0'=3,'gx_1'=4,'gx_2'=8,'gy_0'=4,'gy_1'=2] {'gy_1'}, use_global_device_ids=true, to_apply=%region_29.30 | all-reduce | flops 5 | bytes 40 | tf_op jit(solution)/shard_map/psum | solution.py:48
  291.6 1.0 multiply_subtract_fusion
  292.6 0.6 pad_maximum_fusion.30
  (21 shorter events, 0.2 us)
Async XLA Ops:
  1.7 22.3 %copy-start = (f32[4,64,256]{2,1,0:T(8,128)S(1)}, f32[4,64,256]{2,1,0:T(8,128)}, u32[]{:S(2)}) copy-start(f32[4,64,256]{2,1,0:T(8,128)} %param.3) | copy-start | bytes 786436
  1.8 28.5 %collective-permute-start.4 = (f32[2,64,256]{2,1,0:T(8,128)S(1)}, f32[2,64,256]{2,1,0:T(8,128)S(1)}, u32[]{:S(2)}, u32[]{:S(2)}) collective-permute-start(f32[2,64,256]{2,1,0:T(8,128)S(1)} %get-tuple-element.99), channel_id=1, source_target_pairs={{0,8},{8,16},{16,24},{24,32},{32,40},{40,48},{48,56},{56,64},{64,7... | collective-permute-start | bytes 393224 | tf_op jit(solution)/shard_map/ppermute | solution.py:20
  5.9 24.3 %collective-permute-start.5 = (f32[2,64,256]{2,1,0:T(8,128)S(1)}, f32[2,64,256]{2,1,0:T(8,128)S(1)}, u32[]{:S(2)}, u32[]{:S(2)}) collective-permute-start(f32[2,64,256]{2,1,0:T(8,128)S(1)} %get-tuple-element.100), channel_id=1, source_target_pairs={{8,0},{16,8},{24,16},{32,24},{40,32},{48,40},{56,48},{64,56},{72,6... | collective-permute-start | bytes 393224 | tf_op jit(solution)/shard_map/ppermute | solution.py:21
  24.0 31.5 %collective-permute-start = (f32[4,1,256]{2,1,0:T(1,128)S(1)}, f32[4,1,256]{2,1,0:T(1,128)S(1)}, u32[]{:S(2)}, u32[]{:S(2)}) collective-permute-start(f32[4,1,256]{2,1,0:T(1,128)S(1)} %get-tuple-element.95), channel_id=1, source_target_pairs={{0,1},{1,2},{2,3},{3,4},{4,5},{5,6},{6,7},{7,0},{8,9},{9,10},{10,1... | collective-permute-start | bytes 12296 | tf_op jit(solution)/shard_map/ppermute | solution.py:34
  28.0 27.6 %collective-permute-start.3 = (f32[4,1,256]{2,1,0:T(1,128)S(1)}, f32[4,1,256]{2,1,0:T(1,128)S(1)}, u32[]{:S(2)}, u32[]{:S(2)}) collective-permute-start(f32[4,1,256]{2,1,0:T(1,128)S(1)} %get-tuple-element.96), channel_id=1, source_target_pairs={{1,0},{2,1},{3,2},{4,3},{5,4},{6,5},{7,6},{0,7},{9,8},{10,9},{11,1... | collective-permute-start | bytes 12296 | tf_op jit(solution)/shard_map/ppermute | solution.py:35
  30.3 12.7 %collective-permute-start.7 = (f32[8,2,256]{2,1,0:T(2,128)S(1)}, f32[8,2,256]{2,1,0:T(2,128)S(1)}, u32[]{:S(2)}, u32[]{:S(2)}) collective-permute-start(f32[8,2,256]{2,1,0:T(2,128)S(1)} %get-tuple-element.77), channel_id=1, source_target_pairs={{1,0},{2,1},{3,2},{4,3},{5,4},{6,5},{7,6},{0,7},{9,8},{10,9},{11,1... | collective-permute-start | bytes 49160 | tf_op jit(solution)/shard_map/ppermute | solution.py:21
  39.0 16.1 %collective-permute-start.6 = (f32[8,2,256]{2,1,0:T(2,128)S(1)}, f32[8,2,256]{2,1,0:T(2,128)S(1)}, u32[]{:S(2)}, u32[]{:S(2)}) collective-permute-start(f32[8,2,256]{2,1,0:T(2,128)S(1)} %get-tuple-element.78), channel_id=1, source_target_pairs={{0,1},{1,2},{2,3},{3,4},{4,5},{5,6},{6,7},{7,0},{8,9},{9,10},{10,1... | collective-permute-start | bytes 49160 | tf_op jit(solution)/shard_map/ppermute | solution.py:20
  41.0 14.6 %collective-permute-start.1 = (f32[1,64,256]{2,1,0:T(8,128)S(1)}, f32[1,64,256]{2,1,0:T(8,128)S(1)}, u32[]{:S(2)}, u32[]{:S(2)}) collective-permute-start(f32[1,64,256]{2,1,0:T(8,128)S(1)} %get-tuple-element.97), channel_id=1, source_target_pairs={{0,8},{8,16},{16,24},{24,32},{32,40},{40,48},{48,56},{56,64},{64,7... | collective-permute-start | bytes 196616 | tf_op jit(solution)/shard_map/ppermute | solution.py:34
  42.9 18.0 %collective-permute-start.2 = (f32[1,64,256]{2,1,0:T(8,128)S(1)}, f32[1,64,256]{2,1,0:T(8,128)S(1)}, u32[]{:S(2)}, u32[]{:S(2)}) collective-permute-start(f32[1,64,256]{2,1,0:T(8,128)S(1)} %get-tuple-element.98), channel_id=1, source_target_pairs={{8,0},{16,8},{24,16},{32,24},{40,32},{48,40},{56,48},{64,56},{72,6... | collective-permute-start | bytes 196616 | tf_op jit(solution)/shard_map/ppermute | solution.py:35
  61.4 1.0 copy-start.1
  63.3 19.8 %collective-permute-start.8 = (f32[2,64,256]{2,1,0:T(8,128)S(1)}, f32[2,64,256]{2,1,0:T(8,128)S(1)}, u32[]{:S(2)}, u32[]{:S(2)}) collective-permute-start(f32[2,64,256]{2,1,0:T(8,128)S(1)} %get-tuple-element.93), channel_id=1, source_target_pairs={{0,8},{8,16},{16,24},{24,32},{32,40},{40,48},{48,56},{56,64},{64,7... | collective-permute-start | bytes 393224 | tf_op jit(solution)/shard_map/ppermute | solution.py:20
  65.2 20.3 %collective-permute-start.9 = (f32[2,64,256]{2,1,0:T(8,128)S(1)}, f32[2,64,256]{2,1,0:T(8,128)S(1)}, u32[]{:S(2)}, u32[]{:S(2)}) collective-permute-start(f32[2,64,256]{2,1,0:T(8,128)S(1)} %get-tuple-element.94), channel_id=1, source_target_pairs={{8,0},{16,8},{24,16},{32,24},{40,32},{48,40},{56,48},{64,56},{72,6... | collective-permute-start | bytes 393224 | tf_op jit(solution)/shard_map/ppermute | solution.py:21
  85.6 61.6 %collective-permute-start.11 = (f32[8,2,256]{2,1,0:T(2,128)S(1)}, f32[8,2,256]{2,1,0:T(2,128)S(1)}, u32[]{:S(2)}, u32[]{:S(2)}) collective-permute-start(f32[8,2,256]{2,1,0:T(2,128)S(1)} %get-tuple-element.75), channel_id=1, source_target_pairs={{1,0},{2,1},{3,2},{4,3},{5,4},{6,5},{7,6},{0,7},{9,8},{10,9},{11,1... | collective-permute-start | bytes 49160 | tf_op jit(solution)/shard_map/ppermute | solution.py:21
  88.2 59.0 %collective-permute-start.10 = (f32[8,2,256]{2,1,0:T(2,128)S(1)}, f32[8,2,256]{2,1,0:T(2,128)S(1)}, u32[]{:S(2)}, u32[]{:S(2)}) collective-permute-start(f32[8,2,256]{2,1,0:T(2,128)S(1)} %get-tuple-element.76), channel_id=1, source_target_pairs={{0,1},{1,2},{2,3},{3,4},{4,5},{5,6},{6,7},{7,0},{8,9},{9,10},{10,1... | collective-permute-start | bytes 49160 | tf_op jit(solution)/shard_map/ppermute | solution.py:20
  149.3 21.9 %collective-permute-start.12 = (f32[2,64,256]{2,1,0:T(8,128)S(1)}, f32[2,64,256]{2,1,0:T(8,128)S(1)}, u32[]{:S(2)}, u32[]{:S(2)}) collective-permute-start(f32[2,64,256]{2,1,0:T(8,128)S(1)} %get-tuple-element.91), channel_id=1, source_target_pairs={{0,8},{8,16},{16,24},{24,32},{32,40},{40,48},{48,56},{56,64},{64,7... | collective-permute-start | bytes 393224 | tf_op jit(solution)/shard_map/ppermute | solution.py:20
  151.2 22.2 %collective-permute-start.13 = (f32[2,64,256]{2,1,0:T(8,128)S(1)}, f32[2,64,256]{2,1,0:T(8,128)S(1)}, u32[]{:S(2)}, u32[]{:S(2)}) collective-permute-start(f32[2,64,256]{2,1,0:T(8,128)S(1)} %get-tuple-element.92), channel_id=1, source_target_pairs={{8,0},{16,8},{24,16},{32,24},{40,32},{48,40},{56,48},{64,56},{72,6... | collective-permute-start | bytes 393224 | tf_op jit(solution)/shard_map/ppermute | solution.py:21
  173.4 64.2 %collective-permute-start.15 = (f32[8,2,256]{2,1,0:T(2,128)S(1)}, f32[8,2,256]{2,1,0:T(2,128)S(1)}, u32[]{:S(2)}, u32[]{:S(2)}) collective-permute-start(f32[8,2,256]{2,1,0:T(2,128)S(1)} %get-tuple-element.73), channel_id=1, source_target_pairs={{1,0},{2,1},{3,2},{4,3},{5,4},{6,5},{7,6},{0,7},{9,8},{10,9},{11,1... | collective-permute-start | bytes 49160 | tf_op jit(solution)/shard_map/ppermute | solution.py:21
  175.8 61.8 %collective-permute-start.14 = (f32[8,2,256]{2,1,0:T(2,128)S(1)}, f32[8,2,256]{2,1,0:T(2,128)S(1)}, u32[]{:S(2)}, u32[]{:S(2)}) collective-permute-start(f32[8,2,256]{2,1,0:T(2,128)S(1)} %get-tuple-element.74), channel_id=1, source_target_pairs={{0,1},{1,2},{2,3},{3,4},{4,5},{5,6},{6,7},{7,0},{8,9},{9,10},{10,1... | collective-permute-start | bytes 49160 | tf_op jit(solution)/shard_map/ppermute | solution.py:20
where the time goes:
time: 294 us; the launch traced here: 293 us
  blocking collectives  154 us (52%)
  starting transfers between devices  92.1 us (31%)
  waiting for transfers between devices  24 us (8%)
  between operations  13.2 us (4%)
  other arithmetic  6.98 us (2%)
    psum x15, blocking collectives, by_axis(): x = lax.psum(x, axis)  154 us
    ppermute x6, starting transfers between devices, extended(): after = lax.ppermute(first, axis, down)  55.7 us
    ppermute x6, starting transfers between devices, extended(): before = lax.ppermute(last, axis, up)  16.1 us
    ppermute x2, starting transfers between devices, extended_2(): lax.ppermute(first, axis, [(b, a) for a, b in up])  14.4 us
    ppermute x6, waiting for transfers between devices, extended(): before = lax.ppermute(last, axis, up)  14.1 us
  transfers between devices with their start and end apart: 16, of which 5 were waited for; matrix products, arithmetic and copies ran while one was open for 0% of the time, Pallas kernels for 0%

commit v1 on v0

--- a/solution.py
+++ b/solution.py
@@ -5,7 +5,6 @@
 from jax.sharding import PartitionSpec as P
 
 ITERS = 3
-GX_GY = ("gx_0", "gx_1", "gx_2", "gy_0", "gy_1")
 GX = ("gx_0", "gx_1", "gx_2")
 GY = ("gy_0", "gy_1")
 
@@ -43,10 +42,15 @@
     return x
 
 
-def by_axis(x, axes):
-    for axis in axes:
-        x = lax.psum(x, axis)
-    return x
+def stage(x, axes):
+    n = lax.axis_size(axes)
+    return jnp.sum(lax.all_to_all(jnp.broadcast_to(x, (n, 1, 128)), axes, 0, 0), axis=0)
+
+
+def totals(*sums):
+    packed = jnp.pad(jnp.stack(sums), (0, 128 - len(sums))).reshape(1, 128)
+    packed = stage(stage(packed, ("gx_1", "gx_2")), ("gx_0", "gy_0", "gy_1"))
+    return [packed[0, i] for i in range(len(sums))]
 
 
 def zbeside(field):
@@ -94,10 +98,8 @@
     gamma_old = jnp.float32(1.0)
     alpha_old = jnp.float32(1.0)
     for step in range(ITERS):
-        gamma, delta, norm_sq = (
-            by_axis(jnp.sum(residual * u_vec), GX_GY),
-            by_axis(jnp.sum(w_vec * u_vec), GX_GY),
-            by_axis(jnp.sum(residual * residual), GX_GY),
+        gamma, delta, norm_sq = totals(
+            jnp.sum(residual * u_vec), jnp.sum(w_vec * u_vec), jnp.sum(residual * residual)
         )
         norms.append(jnp.sqrt(norm_sq / cells))
         m_vec = precond * w_vec

time: 294 us -> 212 us (0.72)
  blocking collectives: 154 us -> 69.1 us
  waiting for transfers between devices: 24 us -> 13.5 us
  other arithmetic: 6.98 us -> 13 us
  starting transfers between devices: 92.1 us -> 97.2 us
    psum x15 -> x0, blocking collectives: 154 us -> none  [by_axis(): x = lax.psum(x, axis)]
    all_to_all x0 -> x5, blocking collectives: none -> 69.1 us  [stage(): lax.all_to_all(jnp.broadcast_to(x, (n, 1, 128)), axes, 0, 0)]
    ppermute x6, waiting for transfers between devices: 14.1 us -> 0.02 us  [extended(): before = lax.ppermute(last, axis, up)]
    all_to_all x0 -> x1, waiting for transfers between devices: none -> 8.03 us  [stage(): lax.all_to_all(jnp.broadcast_to(x, (n, 1, 128)), axes, 0, 0)]
    another operation x0 -> x3, other arithmetic: none -> 5.93 us  [totals(): packed = jnp.pad(jnp.stack(sums), (0, 128 - len(sums))).reshape(1, 128)]
    all_to_all x0 -> x1, starting transfers between devices: none -> 5.19 us  [stage(): lax.all_to_all(jnp.broadcast_to(x, (n, 1, 128)), axes, 0, 0)]
    ppermute x6, waiting for transfers between devices: 4.6 us -> 0.02 us  [extended(): after = lax.ppermute(first, axis, down)]
  transfers between devices with their start and end apart: 16 -> 17, of which waited for: 5 -> 2; matrix products, arithmetic and copies ran while one was open for 0% -> 3% of each run, Pallas kernels for 0% -> 0%
where the time goes in v1:
time: 212 us; the launch traced here: 211 us
  starting transfers between devices  97.2 us (46%)
  blocking collectives  69.1 us (33%)
  waiting for transfers between devices  13.5 us (6%)
  other arithmetic  13 us (6%)
  between operations  12.9 us (6%)
  local copies, waits for them, and re-layouts  5.05 us (2%)
    all_to_all x5, blocking collectives, stage(): lax.all_to_all(jnp.broadcast_to(x, (n, 1, 128)), axes, 0, 0)  69.1 us
    ppermute x6, starting transfers between devices, extended(): after = lax.ppermute(first, axis, down)  55.5 us
    ppermute x6, starting transfers between devices, extended(): before = lax.ppermute(last, axis, up)  16.3 us
    ppermute x2, starting transfers between devices, extended_2(): lax.ppermute(first, axis, [(b, a) for a, b in up])  14.4 us
    all_to_all x1, waiting for transfers between devices, stage(): lax.all_to_all(jnp.broadcast_to(x, (n, 1, 128)), axes, 0, 0)  8.03 us
    another operation x3, other arithmetic, totals(): packed = jnp.pad(jnp.stack(sums), (0, 128 - len(sums))).reshape(1, 128)  5.93 us
    ppermute x2, starting transfers between devices, extended_2(): lax.ppermute(last, axis, up)  5.86 us
    ppermute x2, waiting for transfers between devices, extended_2(): lax.ppermute(first, axis, [(b, a) for a, b in up])  5.4 us
  transfers between devices with their start and end apart: 17, of which 2 were waited for; matrix products, arithmetic and copies ran while one was open for 3% of the time, Pallas kernels for 0%

profile of v1, /device:TPU:1, one launch (start us, length us, event | category | flops | bytes accessed | tf_op | source)
XLA Modules:
  0.0 210.8 jit_solution(17434135808790042851)
XLA Ops:
  0.6 1.1 fusion.24
  1.7 0.0 copy-start
  1.8 4.2 %collective-permute-start.4 = (f32[2,64,256]{2,1,0:T(8,128)S(1)}, f32[2,64,256]{2,1,0:T(8,128)S(1)}, u32[]{:S(2)}, u32[]{:S(2)}) collective-permute-start(f32[2,64,256]{2,1,0:T(8,128)S(1)} %get-tuple-element.54), channel_id=1, source_target_pairs={{0,8},{8,16},{16,24},{24,32},{32,40},{40,48},{48,56},{56,64},{64,7... | collective-permute-start | bytes 393224 | tf_op jit(solution)/shard_map/ppermute | solution.py:19
  5.9 18.1 %collective-permute-start.5 = (f32[2,64,256]{2,1,0:T(8,128)S(1)}, f32[2,64,256]{2,1,0:T(8,128)S(1)}, u32[]{:S(2)}, u32[]{:S(2)}) collective-permute-start(f32[2,64,256]{2,1,0:T(8,128)S(1)} %get-tuple-element.55), channel_id=1, source_target_pairs={{8,0},{16,8},{24,16},{32,24},{40,32},{48,40},{56,48},{64,56},{72,6... | collective-permute-start | bytes 393224 | tf_op jit(solution)/shard_map/ppermute | solution.py:20
  24.0 3.9 %collective-permute-start = (f32[4,1,256]{2,1,0:T(1,128)S(1)}, f32[4,1,256]{2,1,0:T(1,128)S(1)}, u32[]{:S(2)}, u32[]{:S(2)}) collective-permute-start(f32[4,1,256]{2,1,0:T(1,128)S(1)} %get-tuple-element.50), channel_id=1, source_target_pairs={{0,1},{1,2},{2,3},{3,4},{4,5},{5,6},{6,7},{7,0},{8,9},{9,10},{10,1... | collective-permute-start | bytes 12296 | tf_op jit(solution)/shard_map/ppermute | solution.py:33
  28.0 2.2 %collective-permute-start.3 = (f32[4,1,256]{2,1,0:T(1,128)S(1)}, f32[4,1,256]{2,1,0:T(1,128)S(1)}, u32[]{:S(2)}, u32[]{:S(2)}) collective-permute-start(f32[4,1,256]{2,1,0:T(1,128)S(1)} %get-tuple-element.51), channel_id=1, source_target_pairs={{1,0},{2,1},{3,2},{4,3},{5,4},{6,5},{7,6},{0,7},{9,8},{10,9},{11,1... | collective-permute-start | bytes 12296 | tf_op jit(solution)/shard_map/ppermute | solution.py:34
  30.2 0.0 collective-permute-done.4
  30.2 0.0 collective-permute-done.5
  30.3 8.8 %collective-permute-start.7 = (f32[8,2,256]{2,1,0:T(2,128)S(1)}, f32[8,2,256]{2,1,0:T(2,128)S(1)}, u32[]{:S(2)}, u32[]{:S(2)}) collective-permute-start(f32[8,2,256]{2,1,0:T(2,128)S(1)} %get-tuple-element.32), channel_id=1, source_target_pairs={{1,0},{2,1},{3,2},{4,3},{5,4},{6,5},{7,6},{0,7},{9,8},{10,9},{11,1... | collective-permute-start | bytes 49160 | tf_op jit(solution)/shard_map/ppermute | solution.py:20
  39.0 1.9 collective-permute-start.6
  41.0 1.9 collective-permute-start.1
  42.9 0.0 collective-permute-done.7
  42.9 12.2 %collective-permute-start.2 = (f32[1,64,256]{2,1,0:T(8,128)S(1)}, f32[1,64,256]{2,1,0:T(8,128)S(1)}, u32[]{:S(2)}, u32[]{:S(2)}) collective-permute-start(f32[1,64,256]{2,1,0:T(8,128)S(1)} %get-tuple-element.53), channel_id=1, source_target_pairs={{8,0},{16,8},{24,16},{32,24},{40,32},{48,40},{56,48},{64,56},{72,6... | collective-permute-start | bytes 196616 | tf_op jit(solution)/shard_map/ppermute | solution.py:34
  55.1 0.0 collective-permute-done.6
  55.2 0.1 pad_maximum_fusion
  55.2 0.2 fusion.32
  55.4 0.1 fusion.33
  55.6 5.4 %collective-permute-done.2 = f32[1,64,256]{2,1,0:T(8,128)S(1)} collective-permute-done((f32[1,64,256]{2,1,0:T(8,128)S(1)}, f32[1,64,256]{2,1,0:T(8,128)S(1)}, u32[]{:S(2)}, u32[]{:S(2)}) %collective-permute-start.2) | collective-permute-done | bytes 65568 | tf_op jit(solution)/shard_map/ppermute | solution.py:34
  61.0 0.4 fusion.10
  61.4 0.1 fusion.38
  61.5 0.0 copy-start.1
  61.5 0.1 fusion.39
  61.6 0.8 copy-done.1
  62.4 0.9 multiply_reduce_fusion.8
  63.3 0.1 fusion.23
  63.3 1.9 collective-permute-start.8
  65.3 12.4 %collective-permute-start.9 = (f32[2,64,256]{2,1,0:T(8,128)S(1)}, f32[2,64,256]{2,1,0:T(8,128)S(1)}, u32[]{:S(2)}, u32[]{:S(2)}) collective-permute-start(f32[2,64,256]{2,1,0:T(8,128)S(1)} %get-tuple-element.49), channel_id=1, source_target_pairs={{8,0},{16,8},{24,16},{32,24},{40,32},{48,40},{56,48},{64,56},{72,6... | collective-permute-start | bytes 393224 | tf_op jit(solution)/shard_map/ppermute | solution.py:20
  77.7 2.0 select_maximum_fusion.6
  79.7 11.6 %all_to_all.30 = f32[32,1,128]{2,1,0:T(1,128)S(1)} all-to-all(f32[32,1,128]{2,1,0:T(1,128)S(1)} %broadcast_in_dim.18), channel_id=1, replica_groups=mesh['gx_0'=3,'gx_1'=4,'gx_2'=8,'gy_0'=4,'gy_1'=2] {'gx_1','gx_2'}, dimensions={0} | all-to-all | bytes 32768 | tf_op jit(solution)/shard_map/all_to_all | solution.py:47
  91.4 16.1 %all_to_all.31 = f32[24,1,128]{2,1,0:T(1,128)S(1)} all-to-all(f32[24,1,128]{2,1,0:T(1,128)S(1)} %broadcast_in_dim.19), channel_id=1, replica_groups=mesh['gx_0'=3,'gx_1'=4,'gx_2'=8,'gy_0'=4,'gy_1'=2] {'gx_0','gy_0','gy_1'}, dimensions={0} | all-to-all | bytes 24576 | tf_op jit(solution)/shard_map/all_to_all | solution.py:47
  107.5 2.6 %collective-permute-start.11 = (f32[8,2,256]{2,1,0:T(2,128)S(1)}, f32[8,2,256]{2,1,0:T(2,128)S(1)}, u32[]{:S(2)}, u32[]{:S(2)}) collective-permute-start(f32[8,2,256]{2,1,0:T(2,128)S(1)} %get-tuple-element.30), channel_id=1, source_target_pairs={{1,0},{2,1},{3,2},{4,3},{5,4},{6,5},{7,6},{0,7},{9,8},{10,9},{11,1... | collective-permute-start | bytes 49160 | tf_op jit(solution)/shard_map/ppermute | solution.py:20
  110.1 3.0 %collective-permute-start.10 = (f32[8,2,256]{2,1,0:T(2,128)S(1)}, f32[8,2,256]{2,1,0:T(2,128)S(1)}, u32[]{:S(2)}, u32[]{:S(2)}) collective-permute-start(f32[8,2,256]{2,1,0:T(2,128)S(1)} %get-tuple-element.31), channel_id=1, source_target_pairs={{0,1},{1,2},{2,3},{3,4},{4,5},{5,6},{6,7},{7,0},{8,9},{9,10},{10,1... | collective-permute-start | bytes 49160 | tf_op jit(solution)/shard_map/ppermute | solution.py:19
  113.1 0.6 fusion.45
  115.1 0.1 pad_maximum_fusion.1
  115.1 0.1 fusion.31
  115.3 0.2 fusion.30
  115.5 0.4 fusion.6
  115.8 0.1 fusion.36
  115.9 0.1 fusion.37
  116.1 1.0 multiply_reduce_fusion.5
  117.0 0.1 fusion.22
  117.1 2.3 %collective-permute-start.12 = (f32[2,64,256]{2,1,0:T(8,128)S(1)}, f32[2,64,256]{2,1,0:T(8,128)S(1)}, u32[]{:S(2)}, u32[]{:S(2)}) collective-permute-start(f32[2,64,256]{2,1,0:T(8,128)S(1)} %get-tuple-element.46), channel_id=1, source_target_pairs={{0,8},{8,16},{16,24},{24,32},{32,40},{40,48},{48,56},{56,64},{64,7... | collective-permute-start | bytes 393224 | tf_op jit(solution)/shard_map/ppermute | solution.py:19
  119.4 11.1 %collective-permute-start.13 = (f32[2,64,256]{2,1,0:T(8,128)S(1)}, f32[2,64,256]{2,1,0:T(8,128)S(1)}, u32[]{:S(2)}, u32[]{:S(2)}) collective-permute-start(f32[2,64,256]{2,1,0:T(8,128)S(1)} %get-tuple-element.47), channel_id=1, source_target_pairs={{8,0},{16,8},{24,16},{32,24},{40,32},{48,40},{56,48},{64,56},{72,6... | collective-permute-start | bytes 393224 | tf_op jit(solution)/shard_map/ppermute | solution.py:20
  130.6 1.9 select_maximum_fusion.4
  132.5 11.6 %all_to_all.32 = f32[32,1,128]{2,1,0:T(1,128)S(1)} all-to-all(f32[32,1,128]{2,1,0:T(1,128)S(1)} %broadcast_in_dim.20), channel_id=1, replica_groups=mesh['gx_0'=3,'gx_1'=4,'gx_2'=8,'gy_0'=4,'gy_1'=2] {'gx_1','gx_2'}, dimensions={0} | all-to-all | bytes 32768 | tf_op jit(solution)/shard_map/all_to_all | solution.py:47
  144.2 18.0 %all_to_all.33 = f32[24,1,128]{2,1,0:T(1,128)S(1)} all-to-all(f32[24,1,128]{2,1,0:T(1,128)S(1)} %broadcast_in_dim.21), channel_id=1, replica_groups=mesh['gx_0'=3,'gx_1'=4,'gx_2'=8,'gy_0'=4,'gy_1'=2] {'gx_0','gy_0','gy_1'}, dimensions={0} | all-to-all | bytes 24576 | tf_op jit(solution)/shard_map/all_to_all | solution.py:47
  162.2 2.6 %collective-permute-start.15 = (f32[8,2,256]{2,1,0:T(2,128)S(1)}, f32[8,2,256]{2,1,0:T(2,128)S(1)}, u32[]{:S(2)}, u32[]{:S(2)}) collective-permute-start(f32[8,2,256]{2,1,0:T(2,128)S(1)} %get-tuple-element.28), channel_id=1, source_target_pairs={{1,0},{2,1},{3,2},{4,3},{5,4},{6,5},{7,6},{0,7},{9,8},{10,9},{11,1... | collective-permute-start | bytes 49160 | tf_op jit(solution)/shard_map/ppermute | solution.py:20
  164.8 3.0 %collective-permute-start.14 = (f32[8,2,256]{2,1,0:T(2,128)S(1)}, f32[8,2,256]{2,1,0:T(2,128)S(1)}, u32[]{:S(2)}, u32[]{:S(2)}) collective-permute-start(f32[8,2,256]{2,1,0:T(2,128)S(1)} %get-tuple-element.29), channel_id=1, source_target_pairs={{0,1},{1,2},{2,3},{3,4},{4,5},{5,6},{6,7},{7,0},{8,9},{9,10},{10,1... | collective-permute-start | bytes 49160 | tf_op jit(solution)/shard_map/ppermute | solution.py:19
  167.8 0.7 fusion.46
  173.0 0.1 pad_maximum_fusion.2
  173.1 0.1 fusion.29
  173.2 0.2 fusion.28
  173.4 0.4 fusion.2
  173.8 0.1 fusion.34
  173.9 0.1 fusion.35
  174.1 1.0 multiply_reduce_fusion.2
  175.1 2.0 select_maximum_fusion.2
  177.1 11.7 %all_to_all.34 = f32[32,1,128]{2,1,0:T(1,128)S(1)} all-to-all(f32[32,1,128]{2,1,0:T(1,128)S(1)} %broadcast_in_dim.22), channel_id=1, replica_groups=mesh['gx_0'=3,'gx_1'=4,'gx_2'=8,'gy_0'=4,'gy_1'=2] {'gx_1','gx_2'}, dimensions={0} | all-to-all | bytes 32768 | tf_op jit(solution)/shard_map/all_to_all | solution.py:47
  188.8 0.6 broadcast_in_dim.23
  189.4 5.2 %all-to-all-start.5 = ((f32[24,1,128]{2,1,0:T(1,128)}), f32[24,1,128]{2,1,0:T(1,128)S(1)}, u32[]{:S(2)}, u32[]{:S(2)}) async-start(f32[24,1,128]{2,1,0:T(1,128)} %broadcast_in_dim.23), calls=%async_computation.5 | async-start | bytes 24576 | tf_op jit(solution)/shard_map/all_to_all | solution.py:47
  195.9 8.0 %all-to-all-done.5 = f32[24,1,128]{2,1,0:T(1,128)S(1)} async-done(((f32[24,1,128]{2,1,0:T(1,128)}), f32[24,1,128]{2,1,0:T(1,128)S(1)}, u32[]{:S(2)}, u32[]{:S(2)}) %all-to-all-start.5) | async-done | bytes 12320 | tf_op jit(solution)/shard_map/all_to_all | solution.py:47
  204.0 0.6 fusion.47
  209.2 1.0 multiply_subtract_fusion
  210.2 0.6 pad_maximum_fusion.30
  (31 shorter events, 0.3 us)
Async XLA Ops:
  1.7 22.3 %copy-start = (f32[4,64,256]{2,1,0:T(8,128)S(1)}, f32[4,64,256]{2,1,0:T(8,128)}, u32[]{:S(2)}) copy-start(f32[4,64,256]{2,1,0:T(8,128)} %param.3) | copy-start | bytes 786436
  1.8 28.5 %collective-permute-start.4 = (f32[2,64,256]{2,1,0:T(8,128)S(1)}, f32[2,64,256]{2,1,0:T(8,128)S(1)}, u32[]{:S(2)}, u32[]{:S(2)}) collective-permute-start(f32[2,64,256]{2,1,0:T(8,128)S(1)} %get-tuple-element.54), channel_id=1, source_target_pairs={{0,8},{8,16},{16,24},{24,32},{32,40},{40,48},{48,56},{56,64},{64,7... | collective-permute-start | bytes 393224 | tf_op jit(solution)/shard_map/ppermute | solution.py:19
  5.9 24.3 %collective-permute-start.5 = (f32[2,64,256]{2,1,0:T(8,128)S(1)}, f32[2,64,256]{2,1,0:T(8,128)S(1)}, u32[]{:S(2)}, u32[]{:S(2)}) collective-permute-start(f32[2,64,256]{2,1,0:T(8,128)S(1)} %get-tuple-element.55), channel_id=1, source_target_pairs={{8,0},{16,8},{24,16},{32,24},{40,32},{48,40},{56,48},{64,56},{72,6... | collective-permute-start | bytes 393224 | tf_op jit(solution)/shard_map/ppermute | solution.py:20
  24.0 31.5 %collective-permute-start = (f32[4,1,256]{2,1,0:T(1,128)S(1)}, f32[4,1,256]{2,1,0:T(1,128)S(1)}, u32[]{:S(2)}, u32[]{:S(2)}) collective-permute-start(f32[4,1,256]{2,1,0:T(1,128)S(1)} %get-tuple-element.50), channel_id=1, source_target_pairs={{0,1},{1,2},{2,3},{3,4},{4,5},{5,6},{6,7},{7,0},{8,9},{9,10},{10,1... | collective-permute-start | bytes 12296 | tf_op jit(solution)/shard_map/ppermute | solution.py:33
  28.0 27.6 %collective-permute-start.3 = (f32[4,1,256]{2,1,0:T(1,128)S(1)}, f32[4,1,256]{2,1,0:T(1,128)S(1)}, u32[]{:S(2)}, u32[]{:S(2)}) collective-permute-start(f32[4,1,256]{2,1,0:T(1,128)S(1)} %get-tuple-element.51), channel_id=1, source_target_pairs={{1,0},{2,1},{3,2},{4,3},{5,4},{6,5},{7,6},{0,7},{9,8},{10,9},{11,1... | collective-permute-start | bytes 12296 | tf_op jit(solution)/shard_map/ppermute | solution.py:34
  30.3 12.7 %collective-permute-start.7 = (f32[8,2,256]{2,1,0:T(2,128)S(1)}, f32[8,2,256]{2,1,0:T(2,128)S(1)}, u32[]{:S(2)}, u32[]{:S(2)}) collective-permute-start(f32[8,2,256]{2,1,0:T(2,128)S(1)} %get-tuple-element.32), channel_id=1, source_target_pairs={{1,0},{2,1},{3,2},{4,3},{5,4},{6,5},{7,6},{0,7},{9,8},{10,9},{11,1... | collective-permute-start | bytes 49160 | tf_op jit(solution)/shard_map/ppermute | solution.py:20
  39.0 16.1 %collective-permute-start.6 = (f32[8,2,256]{2,1,0:T(2,128)S(1)}, f32[8,2,256]{2,1,0:T(2,128)S(1)}, u32[]{:S(2)}, u32[]{:S(2)}) collective-permute-start(f32[8,2,256]{2,1,0:T(2,128)S(1)} %get-tuple-element.33), channel_id=1, source_target_pairs={{0,1},{1,2},{2,3},{3,4},{4,5},{5,6},{6,7},{7,0},{8,9},{9,10},{10,1... | collective-permute-start | bytes 49160 | tf_op jit(solution)/shard_map/ppermute | solution.py:19
  41.0 14.6 %collective-permute-start.1 = (f32[1,64,256]{2,1,0:T(8,128)S(1)}, f32[1,64,256]{2,1,0:T(8,128)S(1)}, u32[]{:S(2)}, u32[]{:S(2)}) collective-permute-start(f32[1,64,256]{2,1,0:T(8,128)S(1)} %get-tuple-element.52), channel_id=1, source_target_pairs={{0,8},{8,16},{16,24},{24,32},{32,40},{40,48},{48,56},{56,64},{64,7... | collective-permute-start | bytes 196616 | tf_op jit(solution)/shard_map/ppermute | solution.py:33
  42.9 18.0 %collective-permute-start.2 = (f32[1,64,256]{2,1,0:T(8,128)S(1)}, f32[1,64,256]{2,1,0:T(8,128)S(1)}, u32[]{:S(2)}, u32[]{:S(2)}) collective-permute-start(f32[1,64,256]{2,1,0:T(8,128)S(1)} %get-tuple-element.53), channel_id=1, source_target_pairs={{8,0},{16,8},{24,16},{32,24},{40,32},{48,40},{56,48},{64,56},{72,6... | collective-permute-start | bytes 196616 | tf_op jit(solution)/shard_map/ppermute | solution.py:34
  61.5 1.0 copy-start.1
  63.3 44.1 %collective-permute-start.8 = (f32[2,64,256]{2,1,0:T(8,128)S(1)}, f32[2,64,256]{2,1,0:T(8,128)S(1)}, u32[]{:S(2)}, u32[]{:S(2)}) collective-permute-start(f32[2,64,256]{2,1,0:T(8,128)S(1)} %get-tuple-element.48), channel_id=1, source_target_pairs={{0,8},{8,16},{16,24},{24,32},{32,40},{40,48},{48,56},{56,64},{64,7... | collective-permute-start | bytes 393224 | tf_op jit(solution)/shard_map/ppermute | solution.py:19
  65.3 42.2 %collective-permute-start.9 = (f32[2,64,256]{2,1,0:T(8,128)S(1)}, f32[2,64,256]{2,1,0:T(8,128)S(1)}, u32[]{:S(2)}, u32[]{:S(2)}) collective-permute-start(f32[2,64,256]{2,1,0:T(8,128)S(1)} %get-tuple-element.49), channel_id=1, source_target_pairs={{8,0},{16,8},{24,16},{32,24},{40,32},{48,40},{56,48},{64,56},{72,6... | collective-permute-start | bytes 393224 | tf_op jit(solution)/shard_map/ppermute | solution.py:20
  107.5 7.5 %collective-permute-start.11 = (f32[8,2,256]{2,1,0:T(2,128)S(1)}, f32[8,2,256]{2,1,0:T(2,128)S(1)}, u32[]{:S(2)}, u32[]{:S(2)}) collective-permute-start(f32[8,2,256]{2,1,0:T(2,128)S(1)} %get-tuple-element.30), channel_id=1, source_target_pairs={{1,0},{2,1},{3,2},{4,3},{5,4},{6,5},{7,6},{0,7},{9,8},{10,9},{11,1... | collective-permute-start | bytes 49160 | tf_op jit(solution)/shard_map/ppermute | solution.py:20
  110.1 4.9 %collective-permute-start.10 = (f32[8,2,256]{2,1,0:T(2,128)S(1)}, f32[8,2,256]{2,1,0:T(2,128)S(1)}, u32[]{:S(2)}, u32[]{:S(2)}) collective-permute-start(f32[8,2,256]{2,1,0:T(2,128)S(1)} %get-tuple-element.31), channel_id=1, source_target_pairs={{0,1},{1,2},{2,3},{3,4},{4,5},{5,6},{6,7},{7,0},{8,9},{9,10},{10,1... | collective-permute-start | bytes 49160 | tf_op jit(solution)/shard_map/ppermute | solution.py:19
  117.1 45.1 %collective-permute-start.12 = (f32[2,64,256]{2,1,0:T(8,128)S(1)}, f32[2,64,256]{2,1,0:T(8,128)S(1)}, u32[]{:S(2)}, u32[]{:S(2)}) collective-permute-start(f32[2,64,256]{2,1,0:T(8,128)S(1)} %get-tuple-element.46), channel_id=1, source_target_pairs={{0,8},{8,16},{16,24},{24,32},{32,40},{40,48},{48,56},{56,64},{64,7... | collective-permute-start | bytes 393224 | tf_op jit(solution)/shard_map/ppermute | solution.py:19
  119.4 42.8 %collective-permute-start.13 = (f32[2,64,256]{2,1,0:T(8,128)S(1)}, f32[2,64,256]{2,1,0:T(8,128)S(1)}, u32[]{:S(2)}, u32[]{:S(2)}) collective-permute-start(f32[2,64,256]{2,1,0:T(8,128)S(1)} %get-tuple-element.47), channel_id=1, source_target_pairs={{8,0},{16,8},{24,16},{32,24},{40,32},{48,40},{56,48},{64,56},{72,6... | collective-permute-start | bytes 393224 | tf_op jit(solution)/shard_map/ppermute | solution.py:20
  162.2 10.8 %collective-permute-start.15 = (f32[8,2,256]{2,1,0:T(2,128)S(1)}, f32[8,2,256]{2,1,0:T(2,128)S(1)}, u32[]{:S(2)}, u32[]{:S(2)}) collective-permute-start(f32[8,2,256]{2,1,0:T(2,128)S(1)} %get-tuple-element.28), channel_id=1, source_target_pairs={{1,0},{2,1},{3,2},{4,3},{5,4},{6,5},{7,6},{0,7},{9,8},{10,9},{11,1... | collective-permute-start | bytes 49160 | tf_op jit(solution)/shard_map/ppermute | solution.py:20
  164.8 8.2 %collective-permute-start.14 = (f32[8,2,256]{2,1,0:T(2,128)S(1)}, f32[8,2,256]{2,1,0:T(2,128)S(1)}, u32[]{:S(2)}, u32[]{:S(2)}) collective-permute-start(f32[8,2,256]{2,1,0:T(2,128)S(1)} %get-tuple-element.29), channel_id=1, source_target_pairs={{0,1},{1,2},{2,3},{3,4},{4,5},{5,6},{6,7},{7,0},{8,9},{9,10},{10,1... | collective-permute-start | bytes 49160 | tf_op jit(solution)/shard_map/ppermute | solution.py:19
  189.4 14.6 %all-to-all-start.5 = ((f32[24,1,128]{2,1,0:T(1,128)}), f32[24,1,128]{2,1,0:T(1,128)S(1)}, u32[]{:S(2)}, u32[]{:S(2)}) async-start(f32[24,1,128]{2,1,0:T(1,128)} %broadcast_in_dim.23), calls=%async_computation.5 | async-start | bytes 24576 | tf_op jit(solution)/shard_map/all_to_all | solution.py:47

commit v2 on v1

v2 whole, which is shorter than its diff:
```python
import functools

import jax
import jax.numpy as jnp
from jax import lax
from jax.experimental import pallas as pl
from jax.experimental.pallas import tpu as pltpu
from jax.sharding import Mesh
from jax.sharding import PartitionSpec as P

GX = ("gx_0", "gx_1", "gx_2")
GY = ("gy_0", "gy_1")
ALL = GX + GY
PLANE = ("gx_1", "gx_2")
COLUMN = ("gx_0", "gy_0", "gy_1")
HI, XS, YS, RANKS = 3, 4, 8, 8
NGX = HI * XS * YS
SEG = XS * YS
VMEM = pl.BlockSpec(memory_space=pltpu.VMEM)
F32 = jnp.float32


def over_gx(moves):
    return [(a % NGX * RANKS + h, b % NGX * RANKS + h) for a, b in moves for h in range(RANKS)]


def corner(hi, x, y):
    return hi % HI * SEG + x % XS * YS + y % YS


def FIRST(k):
    return corner(k, 0, 0)


def LAST(k):
    return corner(k, XS - 1, YS - 1)


def SIDE_A(k):
    return corner(k, 0, YS - 1)


def SIDE_B(k):
    return corner(k, XS - 1, 0)


SEGS = range(HI)
UP = over_gx([(g, g + 1) for g in range(NGX) if g % SEG != SEG - 1])
DOWN = over_gx([(g, g - 1) for g in range(NGX) if g % SEG])
UP2 = over_gx([(g, g + 2) for g in range(NGX)])
DOWN2 = over_gx([(g, g - 2) for g in range(NGX)])
ROUTES = [
    (
        over_gx([(LAST(k), SIDE_A(k)) for k in SEGS] + [(FIRST(k), SIDE_B(k)) for k in SEGS]),
        over_gx([(SIDE_A(k), FIRST(k + 1)) for k in SEGS] + [(SIDE_B(k), LAST(k - 1)) for k in SEGS]),
    ),
    (
        over_gx([(LAST(k), SIDE_B(k)) for k in SEGS] + [(FIRST(k), SIDE_A(k)) for k in SEGS]),
        over_gx([(SIDE_B(k), FIRST(k + 1)) for k in SEGS] + [(SIDE_A(k), LAST(k - 1)) for k in SEGS]),
    ),
    (
        over_gx([(LAST(k), FIRST(k)) for k in SEGS] + [(FIRST(k), LAST(k)) for k in SEGS]),
        over_gx([(FIRST(k), FIRST(k + 1)) for k in SEGS] + [(LAST(k), LAST(k - 1)) for k in SEGS]),
    ),
]
CUTS = ((0, 3), (3, 6), (6, 8))
GY_UP = [(g * RANKS + h, g * RANKS + (h + 1) % RANKS) for g in range(NGX) for h in range(RANKS)]
GY_DOWN = [(b, a) for a, b in GY_UP]

ORDER = (("v", 0), ("v", 1), ("k", 0), ("k", 1), ("k", 2), ("v", 2), ("v", 3), ("k", 3))
AT = {what: i for i, what in enumerate(ORDER)}
V_PLANES = (
    [("pp", 0), ("pp", 1)]
    + [("prev", AT["v", i]) for i in range(4)]
    + [("own", AT["v", i]) for i in range(4)]
    + [("next", AT["v", i]) for i in range(4)]
    + [("nn", 0), ("nn", 1)]
)
K_PLANES = (
    [("pp", 2)]
    + [("prev", AT["k", i]) for i in range(4)]
    + [("own", AT["k", i]) for i in range(4)]
    + [("next", AT["k", i]) for i in range(4)]
    + [("nn", 2)]
)
PARTS = ("pp", "prev", "own", "next", "nn")


def two_sum(a, b):
    s = a + b
    t = s - a
    return s, (a - (s - t)) + (b - t)


def quick(a, b):
    s = a + b
    return s, b - (s - a)


def halves(a):
    c = a * F32(4097.0)
    h = c - (c - a)
    return h, a - h


def two_prod(a, b):
    p = a * b
    (ah, al), (bh, bl) = halves(a), halves(b)
    return p, ((ah * bh - p) + ah * bl + al * bh) + al * bl


def add(a, b):
    s, e = two_sum(a[0], b[0])
    t, f = two_sum(a[1], b[1])
    s, e = quick(s, e + t)
    return quick(s, e + f)


def neg(a):
    return -a[0], -a[1]


def sub(a, b):
    return add(a, neg(b))


def mul(a, b):
    p, e = two_prod(a[0], b[0])
    return quick(p, e + (a[0] * b[1] + a[1] * b[0]))


def twice(a):
    return a[0] + a[0], a[1] + a[1]


def div(a, b):
    q = a[0] / b[0]
    r = sub(a, mul(b, (q, jnp.zeros_like(q))))
    return quick(q, r[0] / b[0])


def form(c, table):
    n = len(c)
    total = None
    for a in range(n):
        for b in range(a, n):
            t = table(a, b)
            for f in (c[a], c[b]):
                t = t if f is None else mul(t, f)
            t = t if a == b else twice(t)
            total = t if total is None else add(total, t)
    return total


def coefficients(mu, gram):
    hankel = lambda a, b: mu[a + b]
    lifted = lambda a, b: mu[a + b + 1]
    gamma = mu[0]
    alpha0 = div(gamma, mu[1])
    rr = [gram(0, 0)]
    r1 = [None, neg(alpha0)]
    gamma1 = form(r1, hankel)
    delta1 = form(r1, lifted)
    rr.append(form(r1, gram))
    beta1 = div(gamma1, gamma)
    alpha1 = div(gamma1, sub(delta1, div(mul(beta1, gamma1), alpha0)))
    one = (jnp.ones_like(alpha0[0]), jnp.zeros_like(alpha0[0]))
    p1 = [add(one, beta1), neg(alpha0)]
    step1 = [mul(alpha1, p1[0]), mul(alpha1, p1[1])]
    r2 = [None, sub(neg(alpha0), step1[0]), neg(step1[1])]
    gamma2 = form(r2, hankel)
    delta2 = form(r2, lifted)
    rr.append(form(r2, gram))
    beta2 = div(gamma2, gamma1)
    alpha2 = div(gamma2, sub(delta2, div(mul(beta2, gamma2), alpha1)))
    p2 = [add(one, mul(beta2, p1[0])), add(r2[1], mul(beta2, p1[1])), r2[2]]
    x = [
        add(add(alpha0, step1[0]), mul(alpha2, p2[0])),
        add(step1[1], mul(alpha2, p2[1])),
        mul(alpha2, p2[2]),
    ]
    return [c[0] for c in x], [c[0] for c in rr]


def around(src, i):
    c = src[i]
    rows, lanes = c.shape
    total = src[i - 1] + src[i + 1]
    total = total + pltpu.roll(c, 1, 0) + pltpu.roll(c, rows - 1, 0)
    return c, total + pltpu.roll(c, 1, 1) + pltpu.roll(c, lanes - 1, 1)


def lanes_of(shape):
    return lax.broadcasted_iota(jnp.int32, shape, len(shape) - 1)


def powers_kernel(
    rhs, pp, prev, own, nxt, nn, low, high,
    y1_out, y2_out, y3_out, sums_out,
    v, k, t1, w1, t2, w2, t3, y1s, y2s, rows,
):
    parts = dict(zip(PARTS, (pp, prev, own, nxt, nn)))
    for j, (name, at) in enumerate(V_PLANES):
        v[j, 8:72] = parts[name][at]
        v[j, 0:8] = low[j]
        v[j, 72:80] = high[j]
    for j, (name, at) in enumerate(K_PLANES):
        k[j, 8:72] = 6.0 + parts[name][at]
        k[j, 0:8] = 6.0 + low[16 + j]
        k[j, 72:80] = 6.0 + high[16 + j]

    def apply(src, dst, shift, count):
        @pl.loop(0, count)
        def _(i):
            c, near = around(src, i + 1)
            dst[i] = k[i + shift] * c - near

    def apply_scaled(src, plain, scaled, shift, count):
        @pl.loop(0, count)
        def _(i):
            c, near = around(src, i + 1)
            kk = k[i + shift]
            y = kk * c - near
            plain[i] = y
            scaled[i] = (1.0 / (kk * kk + 6.0)) * y

    apply(v, t1, 0, 14)
    apply_scaled(t1, y1s, w1, 1, 12)
    apply(w1, t2, 2, 10)
    apply_scaled(t2, y2s, w2, 3, 8)
    apply(w2, t3, 4, 6)

    def folded(a, b):
        prod = a * b
        prod = prod[:, :128] + prod[:, 128:]
        out = [prod[8 * j : 8 * j + 8] for j in range(8)]
        while len(out) > 1:
            out = [out[2 * j] + out[2 * j + 1] for j in range(len(out) // 2)]
        return out[0]

    rows[...] = jnp.zeros_like(rows)

    @pl.loop(0, 4)
    def _(i):
        c, near = around(t3, i + 1)
        y3_out[i] = (k[i + 5] * c - near)[8:72]
        y0 = rhs[i]
        y1 = y1s[i + 4, 8:72]
        y2 = y2s[i + 2, 8:72]
        y1_out[i] = y1
        y2_out[i] = y2
        v0, v1, v2, g = v[i + 6, 8:72], w1[i + 4, 8:72], w2[i + 2, 8:72], c[8:72]
        pairs = (
            (y0, v0), (y1, v0), (y1, v1), (y2, v1), (y2, v2), (g, g),
            (y0, y0), (y0, y1), (y0, y2), (y1, y1), (y1, y2), (y2, y2),
        )
        for d, (a, b) in enumerate(pairs):
            rows[8 * d : 8 * d + 8] += folded(a, b)

    terms = [(rows[pl.ds(s, 16, stride=8), :], None) for s in range(8)]
    hi, lo = terms[0][0], jnp.zeros((16, 128), F32)
    for s in range(1, 8):
        hi, e = two_sum(hi, terms[s][0])
        lo = lo + e
    for shift in (64, 32, 16, 8, 4, 2, 1):
        hi, e = two_sum(hi, pltpu.roll(hi, shift, 1))
        lo = lo + pltpu.roll(lo, shift, 1) + e
    row = lax.broadcasted_iota(jnp.int32, (16, 128), 0)
    lane = lanes_of((16, 128))
    packed = jnp.where(lane == row, hi, 0.0) + jnp.where(lane == row + 16, lo, 0.0)
    sums_out[...] = jnp.broadcast_to(jnp.sum(packed, axis=0, keepdims=True), sums_out.shape)


def added(parts):
    tiles = [parts[8 * j : 8 * j + 8] for j in range(parts.shape[0] // 8)]
    hi, lo = tiles[0], jnp.zeros((8, 128), F32)
    for tile in tiles[1:]:
        hi, e = two_sum(hi, tile)
        lo = lo + e
    for shift in (4, 2, 1):
        hi, e = two_sum(hi, pltpu.roll(hi, shift, 0))
        lo = lo + pltpu.roll(lo, shift, 0) + e
    lane = lanes_of((8, 128))
    return hi + jnp.where((lane >= 16) & (lane < 32), pltpu.roll(lo, 16, 1), 0.0)


def add_kernel(parts, out):
    out[...] = jnp.broadcast_to(added(parts[...])[0:1], out.shape)


def finish_kernel(cells, parts, rhs, kappa, y1, y2, y3, x_out, r_out, rms_out):
    total = added(parts[...])[0:1]
    lane = lanes_of((1, 128))

    def pair(d):
        take = lambda i: jnp.sum(jnp.where(lane == i, total, 0.0), axis=1, keepdims=True)
        return take(d), take(d + 16)

    mu = [pair(d) for d in range(6)]
    table = [pair(6 + d) for d in range(6)]
    place = {(0, 0): 0, (0, 1): 1, (0, 2): 2, (1, 1): 3, (1, 2): 4, (2, 2): 5}
    c, rr = coefficients(mu, lambda a, b: table[place[a, b]])
    rms = jnp.zeros((1, 128), F32)
    for i in range(3):
        rms = jnp.where(lane == i, jnp.sqrt(rr[i] / F32(cells)), rms)
    rms_out[...] = rms
    wide = [jnp.broadcast_to(a, rhs.shape[1:]) for a in c]

    @pl.loop(0, 4)
    def _(i):
        a0, a1, a2 = rhs[i], y1[i], y2[i]
        kk = 6.0 + kappa[i]
        x_out[i] = (1.0 / (kk * kk + 6.0)) * (wide[0] * a0 + wide[1] * a1 + wide[2] * a2)
        r_out[i] = a0 - (wide[0] * a1 + wide[1] * a2 + wide[2] * y3[i])


def kernel(fn, outs, scratch=(), flops=0):
    return pl.pallas_call(
        fn,
        out_shape=[jax.ShapeDtypeStruct(s, F32) for s in outs],
        scratch_shapes=[pltpu.VMEM(s, F32) for s in scratch],
        cost_estimate=pl.CostEstimate(flops=flops, bytes_accessed=flops // 8 + 1024, transcendentals=0),
    )


def send(x, pairs):
    return lax.ppermute(x, ALL, pairs)


def neighbours(block):
    relayed = [send(block[a:b], spread) for (a, b), (spread, _) in zip(CUTS, ROUTES)]
    up = send(block, UP)
    down = send(block, DOWN)
    pp = send(block[5:8], UP2)
    nn = send(block[0:3], DOWN2)
    far = jnp.concatenate([send(x, onward) for x, (_, onward) in zip(relayed, ROUTES)], axis=0)
    place = lax.axis_index(PLANE)
    prev = jnp.where(place == 0, far, up)
    nxt = jnp.where(place == SEG - 1, far, down)
    return pp, prev, nxt, nn


def body(right_side, kappa_sq):
    cells = right_side.size * NGX * RANKS
    shifted = 6.0 + kappa_sq
    start = (1.0 / (shifted * shifted + 6.0)) * right_side
    source = {"v": start, "k": kappa_sq}
    own = jnp.stack([source[a][i] for a, i in ORDER])
    pp, prev, nxt, nn = neighbours(own)
    parts = dict(zip(PARTS, (pp, prev, own, nxt, nn)))
    edge = lambda cut: jnp.stack([parts[name][at, cut] for name, at in V_PLANES + K_PLANES])
    low = send(edge(slice(56, 64)), GY_UP)
    high = send(edge(slice(0, 8)), GY_DOWN)
    block, wide = right_side.shape, (80, 256)
    n_plane, n_column = lax.axis_size(PLANE), lax.axis_size(COLUMN)
    counts = (16, 14, 14, 12, 10, 8, 6, 12, 8)
    y1, y2, y3, sums = kernel(
        powers_kernel,
        [block] * 3 + [(n_plane, 128)],
        [(n, *wide) for n in counts] + [(128, 128)],
        flops=20_000_000,
    )(right_side, pp, prev, own, nxt, nn, low, high)
    sums = lax.all_to_all(sums.reshape(n_plane, 1, 128), PLANE, 0, 0).reshape(n_plane, 128)
    (sums,) = kernel(add_kernel, [(n_column, 128)], flops=20000)(sums)
    sums = lax.all_to_all(sums.reshape(n_column, 1, 128), COLUMN, 0, 0).reshape(n_column, 128)
    x, r, rms = kernel(
        functools.partial(finish_kernel, cells), [block, block, (1, 128)], flops=2_000_000
    )(sums, right_side, kappa_sq, y1, y2, y3)
    return x, r, rms[0, :3]


def solution(mesh):
    finer = Mesh(mesh.devices.reshape(3, 4, 8, 4, 2), ("gx_0", "gx_1", "gx_2", "gy_0", "gy_1"))
    in_specs = (P(GX, GY, None), P(GX, GY, None))
    out_specs = (P(GX, GY, None), P(GX, GY, None), P())
    return jax.shard_map(body, mesh=finer, in_specs=in_specs, out_specs=out_specs, check_vma=False)
```

time: 212 us -> 142 us (0.67)
  starting transfers between devices: 97.2 us -> 53.7 us
  blocking collectives: 69.1 us -> 44.9 us
  Pallas kernels: 0 us -> 13.3 us
  other arithmetic: 13 us -> 0.95 us
  between operations: 12.9 us -> 1.02 us
  waiting for transfers between devices: 13.5 us -> 23.8 us
    ppermute x16 -> x12, starting transfers between devices: 92.1 us -> 53.7 us  [send(): return lax.ppermute(x, ALL, pairs)]
    all_to_all x5 -> x2, blocking collectives: 69.1 us -> 44.9 us  [the longest x1 27.3 us: body(): lax.all_to_all(sums.reshape(n_column, 1, 128), COLUMN, 0, 0)]
    ppermute x16 -> x12, waiting for transfers between devices: 5.43 us -> 23.8 us  [send(): return lax.ppermute(x, ALL, pairs)]
    pallas_call x0 -> x3, Pallas kernels: none -> 13.3 us  [the longest x1 9.14 us: body(): kernel(powers_kernel, [block] * 3 + [(n_plane, 128)], [(n, *wide) for n i...]
    all_to_all x1 -> x0, waiting for transfers between devices: 8.03 us -> none  [stage(): lax.all_to_all(jnp.broadcast_to(x, (n, 1, 128)), axes, 0, 0)]
    another operation x4 -> x3, other arithmetic: 6.52 us -> 0.78 us  [body(): own = jnp.stack([source[a][i] for a, i in ORDER])]
    all_to_all x1 -> x0, starting transfers between devices: 5.19 us -> none  [stage(): lax.all_to_all(jnp.broadcast_to(x, (n, 1, 128)), axes, 0, 0)]
    reduce_sum x9 -> x0, other arithmetic: 2.94 us -> none  [the longest x3 2.83 us: body(): jnp.sum(residual * u_vec)]
  transfers between devices with their start and end apart: 17 -> 12, of which waited for: 2 -> 5; matrix products, arithmetic and copies ran while one was open for 3% -> 0% of each run, Pallas kernels for 0% -> 0%
where the time goes in v2:
time: 142 us
  starting transfers between devices  53.7 us (38%)
  blocking collectives  44.9 us (32%)
  waiting for transfers between devices  23.8 us (17%)
  Pallas kernels  13.3 us (9%)
  local copies, waits for them, and re-layouts  3.79 us (3%)
    ppermute x12, starting transfers between devices, send(): return lax.ppermute(x, ALL, pairs)  53.7 us
    all_to_all x1, blocking collectives, body(): lax.all_to_all(sums.reshape(n_column, 1, 128), COLUMN, 0, 0)  27.3 us
    ppermute x12, waiting for transfers between devices, send(): return lax.ppermute(x, ALL, pairs)  23.8 us
    all_to_all x1, blocking collectives, body(): lax.all_to_all(sums.reshape(n_plane, 1, 128), PLANE, 0, 0)  17.6 us
    pallas_call x1, Pallas kernels, body(): kernel(powers_kernel, [block] * 3 + [(n_plane, 128)], [(n, *wide) for n i...  9.14 us
  transfers between devices with their start and end apart: 12, of which 5 were waited for; matrix products, arithmetic and copies ran while one was open for 0% of the time, Pallas kernels for 0%

profile of v2, /device:TPU:1, one launch (start us, length us, event | category | flops | bytes accessed | tf_op | source)
XLA Modules:
  0.0 141.6 jit_solution(2402396464901540036)
XLA Ops:
  0.6 0.0 copy-start
  0.6 0.0 copy-start.3
  0.7 1.0 slice.192
  1.7 0.0 copy-done
  1.7 0.1 copy-done.3
  1.8 0.1 divide_multiply_fusion
  1.8 0.7 pad_maximum_fusion.2
  2.6 5.0 %collective-permute-start = (f32[3,64,256]{2,1,0:T(8,128)S(1)}, f32[3,64,256]{2,1,0:T(8,128)S(1)}, u32[]{:S(2)}, u32[]{:S(2)}) collective-permute-start(f32[3,64,256]{2,1,0:T(8,128)S(1)} %get-tuple-element.51), channel_id=1, source_target_pairs={{0,16},{1,17},{2,18},{3,19},{4,20},{5,21},{6,22},{7,23},{8,24},{9,... | collective-permute-start | bytes 589832 | tf_op jit(solution)/shard_map/ppermute | solution.py:327
  7.6 5.1 %collective-permute-start.1 = (f32[3,64,256]{2,1,0:T(8,128)}, f32[3,64,256]{2,1,0:T(8,128)}, u32[]{:S(2)}, u32[]{:S(2)}) collective-permute-start(f32[3,64,256]{2,1,0:T(8,128)} %get-tuple-element.50), channel_id=1, source_target_pairs={{248,56},{249,57},{250,58},{251,59},{252,60},{253,61},{254,62},{25... | collective-permute-start | bytes 589832 | tf_op jit(solution)/shard_map/ppermute | solution.py:327
  12.7 2.0 %collective-permute-start.3 = (f32[3,64,256]{2,1,0:T(8,128)S(1)}, f32[3,64,256]{2,1,0:T(8,128)}, u32[]{:S(2)}, u32[]{:S(2)}) collective-permute-start(f32[3,64,256]{2,1,0:T(8,128)S(1)} %get-tuple-element.49), channel_id=1, source_target_pairs={{248,192},{249,193},{250,194},{251,195},{252,196},{253,197},{254,1... | collective-permute-start | bytes 589832 | tf_op jit(solution)/shard_map/ppermute | solution.py:327
  14.7 0.0 copy-start.4
  14.7 1.3 collective-permute-start.8
  16.0 4.0 %collective-permute-start.7 = (f32[8,64,256]{2,1,0:T(8,128)S(1)}, f32[8,64,256]{2,1,0:T(8,128)S(1)}, u32[]{:S(2)}, u32[]{:S(2)}) collective-permute-start(f32[8,64,256]{2,1,0:T(8,128)S(1)} %pad_maximum_fusion.own), channel_id=1, source_target_pairs={{0,8},{1,9},{2,10},{3,11},{4,12},{5,13},{6,14},{7,15},{8,16},{9,17... | collective-permute-start | bytes 1572872 | tf_op jit(solution)/shard_map/ppermute | solution.py:327
  20.1 9.2 %collective-permute-done.pp = f32[3,64,256]{2,1,0:T(8,128)S(1)} collective-permute-done((f32[3,64,256]{2,1,0:T(8,128)S(1)}, f32[3,64,256]{2,1,0:T(8,128)S(1)}, u32[]{:S(2)}, u32[]{:S(2)}) %collective-permute-start) | collective-permute-done | bytes 196640 | tf_op jit(solution)/shard_map/ppermute | solution.py:327
  29.2 0.0 copy-start.5
  29.2 1.9 %collective-permute-start.5 = (f32[2,64,256]{2,1,0:T(8,128)S(1)}, f32[2,64,256]{2,1,0:T(8,128)S(1)}, u32[]{:S(2)}, u32[]{:S(2)}) collective-permute-start(f32[2,64,256]{2,1,0:T(8,128)S(1)} %fusion), channel_id=1, source_target_pairs={{248,0},{249,1},{250,2},{251,3},{252,4},{253,5},{254,6},{255,7},{5... | collective-permute-start | bytes 393224 | tf_op jit(solution)/shard_map/ppermute | solution.py:327
  31.2 0.0 collective-permute-done.1
  31.2 1.3 collective-permute-start.2
  32.5 0.0 collective-permute-done.3
  32.5 1.3 collective-permute-start.4
  33.8 4.5 %collective-permute-done.5 = f32[2,64,256]{2,1,0:T(8,128)S(1)} collective-permute-done((f32[2,64,256]{2,1,0:T(8,128)S(1)}, f32[2,64,256]{2,1,0:T(8,128)S(1)}, u32[]{:S(2)}, u32[]{:S(2)}) %collective-permute-start.5) | collective-permute-done | bytes 131104 | tf_op jit(solution)/shard_map/ppermute | solution.py:327
  38.3 1.9 %collective-permute-start.9 = (f32[3,64,256]{2,1,0:T(8,128)}, f32[3,64,256]{2,1,0:T(8,128)S(1)}, u32[]{:S(2)}, u32[]{:S(2)}) collective-permute-start(f32[3,64,256]{2,1,0:T(8,128)} %get-tuple-element.50), channel_id=1, source_target_pairs={{0,752},{1,753},{2,754},{3,755},{4,756},{5,757},{6,758},{7,759},{8... | collective-permute-start | bytes 589832 | tf_op jit(solution)/shard_map/ppermute | solution.py:327
  40.2 3.6 %collective-permute-done.2 = f32[3,64,256]{2,1,0:T(8,128)S(1)} collective-permute-done((f32[3,64,256]{2,1,0:T(8,128)}, f32[3,64,256]{2,1,0:T(8,128)S(1)}, u32[]{:S(2)}, u32[]{:S(2)}) %collective-permute-start.2) | collective-permute-done | bytes 196640 | tf_op jit(solution)/shard_map/ppermute | solution.py:327
  43.8 5.2 %collective-permute-start.6 = (f32[2,64,256]{2,1,0:T(8,128)S(1)}, f32[2,64,256]{2,1,0:T(8,128)S(1)}, u32[]{:S(2)}, u32[]{:S(2)}) collective-permute-start(f32[2,64,256]{2,1,0:T(8,128)S(1)} %collective-permute-done.5), channel_id=1, source_target_pairs={{0,256},{1,257},{2,258},{3,259},{4,260},{5,261},{6,262},{7,263},{2... | collective-permute-start | bytes 393224 | tf_op jit(solution)/shard_map/ppermute | solution.py:327
  49.1 0.0 collective-permute-done.4
  49.1 0.0 copy-done.4
  49.1 5.4 %collective-permute-done.6 = f32[2,64,256]{2,1,0:T(8,128)S(1)} collective-permute-done((f32[2,64,256]{2,1,0:T(8,128)S(1)}, f32[2,64,256]{2,1,0:T(8,128)S(1)}, u32[]{:S(2)}, u32[]{:S(2)}) %collective-permute-start.6) | collective-permute-done | bytes 131104 | tf_op jit(solution)/shard_map/ppermute | solution.py:327
  54.5 0.0 collective-permute-done.8
  54.5 0.0 collective-permute-done.7
  54.5 0.1 broadcast_select_fusion
  54.6 0.0 copy-start.1
  54.7 0.0 copy-start.2
  54.7 0.0 collective-permute-done.9.nn
  54.7 0.0 copy-start.6
  54.8 0.0 copy-done.5
  54.9 0.7 copy-done.6
  55.5 14.0 %collective-permute-start.10 = (f32[30,8,256]{2,1,0:T(8,128)S(1)}, f32[30,8,256]{2,1,0:T(8,128)S(1)}, u32[]{:S(2)}, u32[]{:S(2)}) collective-permute-start(f32[30,8,256]{2,1,0:T(8,128)S(1)} %get-tuple-element.42), channel_id=1, source_target_pairs={{0,1},{1,2},{2,3},{3,4},{4,5},{5,6},{6,7},{7,0},{8,9},{9,10},{10,1... | collective-permute-start | bytes 737288 | tf_op jit(solution)/shard_map/ppermute | solution.py:327
  69.5 10.8 %collective-permute-start.11 = (f32[30,8,256]{2,1,0:T(8,128)S(1)}, f32[30,8,256]{2,1,0:T(8,128)S(1)}, u32[]{:S(2)}, u32[]{:S(2)}) collective-permute-start(f32[30,8,256]{2,1,0:T(8,128)S(1)} %get-tuple-element.41), channel_id=1, source_target_pairs={{1,0},{2,1},{3,2},{4,3},{5,4},{6,5},{7,6},{0,7},{9,8},{10,9},{11,1... | collective-permute-start | bytes 737288 | tf_op jit(solution)/shard_map/ppermute | solution.py:327
  80.3 0.0 collective-permute-done.10.low
  80.3 0.0 copy-start.7
  80.3 1.1 collective-permute-done.11.high
  81.4 0.0 copy-done.1
  81.4 0.0 copy-done.2
  81.4 0.0 copy-done.7
  81.4 0.0 copy-start.8
  81.4 0.7 copy-done.8
  82.1 9.1 %shard_map.49 = (f32[4,64,256]{2,1,0:T(8,128)}, f32[4,64,256]{2,1,0:T(8,128)}, f32[4,64,256]{2,1,0:T(8,128)}, f32[32,128]{1,0:T(8,128)}) custom-call(f32[4,64,256]{2,1,0:T(8,128)} %rhs.3, f32[3,64,256]{2,1,0:T(8,128)} %copy-done.5, f32[8,64,256]{2,1,0:T(8,128)} %copy-done.2, f32[8,64,256]{2,1,0:T(8,128)} %copy-done.4, f32[8,64,256]{2,1,0:T(8,128)} %copy-done.1, ...), custom_call_target="tpu_custom_call" | custom-call | flops 20000000 | bytes 2501024 | tf_op jit(solution)/shard_map/pallas_call | solution.py:357
  91.3 17.6 %all_to_all.10 = f32[32,1,128]{2,1,0:T(1,128)} all-to-all(f32[32,1,128]{2,1,0:T(1,128)} %bitcast.13), channel_id=1, replica_groups=mesh['gx_0'=3,'gx_1'=4,'gx_2'=8,'gy_0'=4,'gy_1'=2] {'gx_1','gx_2'}, dimensions={0} | all-to-all | bytes 32768 | tf_op jit(solution)/shard_map/all_to_all | solution.py:363
  108.9 1.4 shard_map.50
  110.3 27.3 %all_to_all.11 = f32[24,1,128]{2,1,0:T(1,128)} all-to-all(f32[24,1,128]{2,1,0:T(1,128)} %bitcast.12), channel_id=1, replica_groups=mesh['gx_0'=3,'gx_1'=4,'gx_2'=8,'gy_0'=4,'gy_1'=2] {'gx_0','gy_0','gy_1'}, dimensions={0} | all-to-all | bytes 24576 | tf_op jit(solution)/shard_map/all_to_all | solution.py:365
  137.6 2.8 %shard_map.51 = (f32[4,64,256]{2,1,0:T(8,128)}, f32[4,64,256]{2,1,0:T(8,128)}, f32[1,128]{1,0:T(1,128)}) custom-call(f32[24,128]{1,0:T(8,128)} %bitcast.11, f32[4,64,256]{2,1,0:T(8,128)} %rhs.3, f32[4,64,256]{2,1,0:T(8,128)} %kappa.1, f32[4,64,256]{2,1,0:T(8,128)} %get-tuple-element.11.y1, f32[4,64,256]{2,1,0:T(8,128)} %get-tuple-element.12.y2, ...), custom_call_target="tpu_custom_call" | custom-call | flops 2000000 | bytes 251024 | tf_op jit(solution)/shard_map/pallas_call | solution.py:366
  140.4 0.0 copy-start.9
  140.4 0.7 copy-done.9
  141.1 0.5 slice_bitcast_fusion
  (21 shorter events, 0.2 us)
Async XLA Ops:
  0.6 1.0 copy-start
  0.6 1.1 copy-start.3
  2.6 26.7 %collective-permute-start = (f32[3,64,256]{2,1,0:T(8,128)S(1)}, f32[3,64,256]{2,1,0:T(8,128)S(1)}, u32[]{:S(2)}, u32[]{:S(2)}) collective-permute-start(f32[3,64,256]{2,1,0:T(8,128)S(1)} %get-tuple-element.51), channel_id=1, source_target_pairs={{0,16},{1,17},{2,18},{3,19},{4,20},{5,21},{6,22},{7,23},{8,24},{9,... | collective-permute-start | bytes 589832 | tf_op jit(solution)/shard_map/ppermute | solution.py:327
  7.6 23.6 %collective-permute-start.1 = (f32[3,64,256]{2,1,0:T(8,128)}, f32[3,64,256]{2,1,0:T(8,128)}, u32[]{:S(2)}, u32[]{:S(2)}) collective-permute-start(f32[3,64,256]{2,1,0:T(8,128)} %get-tuple-element.50), channel_id=1, source_target_pairs={{248,56},{249,57},{250,58},{251,59},{252,60},{253,61},{254,62},{25... | collective-permute-start | bytes 589832 | tf_op jit(solution)/shard_map/ppermute | solution.py:327
  12.7 19.8 %collective-permute-start.3 = (f32[3,64,256]{2,1,0:T(8,128)S(1)}, f32[3,64,256]{2,1,0:T(8,128)}, u32[]{:S(2)}, u32[]{:S(2)}) collective-permute-start(f32[3,64,256]{2,1,0:T(8,128)S(1)} %get-tuple-element.49), channel_id=1, source_target_pairs={{248,192},{249,193},{250,194},{251,195},{252,196},{253,197},{254,1... | collective-permute-start | bytes 589832 | tf_op jit(solution)/shard_map/ppermute | solution.py:327
  14.7 34.4 %copy-start.4 = (f32[8,64,256]{2,1,0:T(8,128)}, f32[8,64,256]{2,1,0:T(8,128)S(1)}, u32[]{:S(2)}) copy-start(f32[8,64,256]{2,1,0:T(8,128)S(1)} %pad_maximum_fusion.own) | copy-start | bytes 1572868
  14.7 39.8 %collective-permute-start.8 = (f32[8,64,256]{2,1,0:T(8,128)S(1)}, f32[8,64,256]{2,1,0:T(8,128)S(1)}, u32[]{:S(2)}, u32[]{:S(2)}) collective-permute-start(f32[8,64,256]{2,1,0:T(8,128)S(1)} %pad_maximum_fusion.own), channel_id=1, source_target_pairs={{8,0},{9,1},{10,2},{11,3},{12,4},{13,5},{14,6},{15,7},{16,8},{17,9... | collective-permute-start | bytes 1572872 | tf_op jit(solution)/shard_map/ppermute | solution.py:327
  16.0 38.5 %collective-permute-start.7 = (f32[8,64,256]{2,1,0:T(8,128)S(1)}, f32[8,64,256]{2,1,0:T(8,128)S(1)}, u32[]{:S(2)}, u32[]{:S(2)}) collective-permute-start(f32[8,64,256]{2,1,0:T(8,128)S(1)} %pad_maximum_fusion.own), channel_id=1, source_target_pairs={{0,8},{1,9},{2,10},{3,11},{4,12},{5,13},{6,14},{7,15},{8,16},{9,17... | collective-permute-start | bytes 1572872 | tf_op jit(solution)/shard_map/ppermute | solution.py:327
  29.2 25.5 %copy-start.5 = (f32[3,64,256]{2,1,0:T(8,128)}, f32[3,64,256]{2,1,0:T(8,128)S(1)}, u32[]{:S(2)}) copy-start(f32[3,64,256]{2,1,0:T(8,128)S(1)} %collective-permute-done.pp) | copy-start | bytes 589828
  29.2 9.0 %collective-permute-start.5 = (f32[2,64,256]{2,1,0:T(8,128)S(1)}, f32[2,64,256]{2,1,0:T(8,128)S(1)}, u32[]{:S(2)}, u32[]{:S(2)}) collective-permute-start(f32[2,64,256]{2,1,0:T(8,128)S(1)} %fusion), channel_id=1, source_target_pairs={{248,0},{249,1},{250,2},{251,3},{252,4},{253,5},{254,6},{255,7},{5... | collective-permute-start | bytes 393224 | tf_op jit(solution)/shard_map/ppermute | solution.py:327
  31.2 12.6 %collective-permute-start.2 = (f32[3,64,256]{2,1,0:T(8,128)}, f32[3,64,256]{2,1,0:T(8,128)S(1)}, u32[]{:S(2)}, u32[]{:S(2)}) collective-permute-start(f32[3,64,256]{2,1,0:T(8,128)} %collective-permute-done.1), channel_id=1, source_target_pairs={{56,256},{57,257},{58,258},{59,259},{60,260},{61,261},{62,262},{63... | collective-permute-start | bytes 589832 | tf_op jit(solution)/shard_map/ppermute | solution.py:327
  32.5 16.6 %collective-permute-start.4 = (f32[3,64,256]{2,1,0:T(8,128)}, f32[3,64,256]{2,1,0:T(8,128)S(1)}, u32[]{:S(2)}, u32[]{:S(2)}) collective-permute-start(f32[3,64,256]{2,1,0:T(8,128)} %collective-permute-done.3), channel_id=1, source_target_pairs={{192,256},{193,257},{194,258},{195,259},{196,260},{197,261},{198,2... | collective-permute-start | bytes 589832 | tf_op jit(solution)/shard_map/ppermute | solution.py:327
  38.3 16.5 %collective-permute-start.9 = (f32[3,64,256]{2,1,0:T(8,128)}, f32[3,64,256]{2,1,0:T(8,128)S(1)}, u32[]{:S(2)}, u32[]{:S(2)}) collective-permute-start(f32[3,64,256]{2,1,0:T(8,128)} %get-tuple-element.50), channel_id=1, source_target_pairs={{0,752},{1,753},{2,754},{3,755},{4,756},{5,757},{6,758},{7,759},{8... | collective-permute-start | bytes 589832 | tf_op jit(solution)/shard_map/ppermute | solution.py:327
  43.8 10.7 %collective-permute-start.6 = (f32[2,64,256]{2,1,0:T(8,128)S(1)}, f32[2,64,256]{2,1,0:T(8,128)S(1)}, u32[]{:S(2)}, u32[]{:S(2)}) collective-permute-start(f32[2,64,256]{2,1,0:T(8,128)S(1)} %collective-permute-done.5), channel_id=1, source_target_pairs={{0,256},{1,257},{2,258},{3,259},{4,260},{5,261},{6,262},{7,263},{2... | collective-permute-start | bytes 393224 | tf_op jit(solution)/shard_map/ppermute | solution.py:327
  54.6 26.8 %copy-start.1 = (f32[8,64,256]{2,1,0:T(8,128)}, f32[8,64,256]{2,1,0:T(8,128)S(1)}, u32[]{:S(2)}) copy-start(f32[8,64,256]{2,1,0:T(8,128)S(1)} %get-tuple-element.33.nxt) | copy-start | bytes 1572868
  54.7 26.8 %copy-start.2 = (f32[8,64,256]{2,1,0:T(8,128)}, f32[8,64,256]{2,1,0:T(8,128)S(1)}, u32[]{:S(2)}) copy-start(f32[8,64,256]{2,1,0:T(8,128)S(1)} %get-tuple-element.34.prev) | copy-start | bytes 1572868
  54.7 0.8 copy-start.6
  55.5 24.8 %collective-permute-start.10 = (f32[30,8,256]{2,1,0:T(8,128)S(1)}, f32[30,8,256]{2,1,0:T(8,128)S(1)}, u32[]{:S(2)}, u32[]{:S(2)}) collective-permute-start(f32[30,8,256]{2,1,0:T(8,128)S(1)} %get-tuple-element.42), channel_id=1, source_target_pairs={{0,1},{1,2},{2,3},{3,4},{4,5},{5,6},{6,7},{7,0},{8,9},{9,10},{10,1... | collective-permute-start | bytes 737288 | tf_op jit(solution)/shard_map/ppermute | solution.py:327
  69.5 11.9 %collective-permute-start.11 = (f32[30,8,256]{2,1,0:T(8,128)S(1)}, f32[30,8,256]{2,1,0:T(8,128)S(1)}, u32[]{:S(2)}, u32[]{:S(2)}) collective-permute-start(f32[30,8,256]{2,1,0:T(8,128)S(1)} %get-tuple-element.41), channel_id=1, source_target_pairs={{1,0},{2,1},{3,2},{4,3},{5,4},{6,5},{7,6},{0,7},{9,8},{10,9},{11,1... | collective-permute-start | bytes 737288 | tf_op jit(solution)/shard_map/ppermute | solution.py:327
  80.3 1.1 copy-start.7
  81.4 0.7 copy-start.8
  140.4 0.7 copy-start.9

commit v3 on v2

--- a/solution.py
+++ b/solution.py
@@ -7,6 +7,7 @@
 from jax.experimental.pallas import tpu as pltpu
 from jax.sharding import Mesh
 from jax.sharding import PartitionSpec as P
+
 
 GX = ("gx_0", "gx_1", "gx_2")
 GY = ("gy_0", "gy_1")
@@ -44,11 +45,23 @@
     return corner(k, XS - 1, 0)
 
 
+def NEAR_LAST(k):
+    return corner(k, XS - 2, YS - 1)
+
+
+def NEAR_FIRST(k):
+    return corner(k, 1, 0)
+
+
 SEGS = range(HI)
-UP = over_gx([(g, g + 1) for g in range(NGX) if g % SEG != SEG - 1])
-DOWN = over_gx([(g, g - 1) for g in range(NGX) if g % SEG])
-UP2 = over_gx([(g, g + 2) for g in range(NGX)])
-DOWN2 = over_gx([(g, g - 2) for g in range(NGX)])
+EVEN = over_gx([(g, g ^ 1) for g in range(NGX)])
+ODD = over_gx([(g, ((g + 1) ^ 1) - 1) for g in range(NGX) if g % SEG not in (0, SEG - 1)])
+STEP = over_gx(
+    [(LAST(k), FIRST(k + 1)) for k in SEGS] + [(FIRST(k), LAST(k - 1)) for k in SEGS]
+)
+ACROSS = over_gx(
+    [(LAST(k) - 1, FIRST(k + 1)) for k in SEGS] + [(FIRST(k) + 1, LAST(k - 1)) for k in SEGS]
+)
 ROUTES = [
     (
         over_gx([(LAST(k), SIDE_A(k)) for k in SEGS] + [(FIRST(k), SIDE_B(k)) for k in SEGS]),
@@ -59,31 +72,22 @@
         over_gx([(SIDE_B(k), FIRST(k + 1)) for k in SEGS] + [(SIDE_A(k), LAST(k - 1)) for k in SEGS]),
     ),
     (
-        over_gx([(LAST(k), FIRST(k)) for k in SEGS] + [(FIRST(k), LAST(k)) for k in SEGS]),
-        over_gx([(FIRST(k), FIRST(k + 1)) for k in SEGS] + [(LAST(k), LAST(k - 1)) for k in SEGS]),
+        over_gx([(LAST(k), NEAR_LAST(k)) for k in SEGS] + [(FIRST(k), NEAR_FIRST(k)) for k in SEGS]),
+        over_gx([(NEAR_LAST(k), FIRST(k + 1)) for k in SEGS] + [(NEAR_FIRST(k), LAST(k - 1)) for k in SEGS]),
     ),
 ]
-CUTS = ((0, 3), (3, 6), (6, 8))
 GY_UP = [(g * RANKS + h, g * RANKS + (h + 1) % RANKS) for g in range(NGX) for h in range(RANKS)]
 GY_DOWN = [(b, a) for a, b in GY_UP]
 
 ORDER = (("v", 0), ("v", 1), ("k", 0), ("k", 1), ("k", 2), ("v", 2), ("v", 3), ("k", 3))
 AT = {what: i for i, what in enumerate(ORDER)}
-V_PLANES = (
+PLANES = (
     [("pp", 0), ("pp", 1)]
-    + [("prev", AT["v", i]) for i in range(4)]
-    + [("own", AT["v", i]) for i in range(4)]
-    + [("next", AT["v", i]) for i in range(4)]
-    + [("nn", 0), ("nn", 1)]
-)
-K_PLANES = (
-    [("pp", 2)]
-    + [("prev", AT["k", i]) for i in range(4)]
-    + [("own", AT["k", i]) for i in range(4)]
-    + [("next", AT["k", i]) for i in range(4)]
+    + [(name, AT["v", i]) for name in ("prev", "own", "next") for i in range(4)]
+    + [("nn", 0), ("nn", 1), ("pp", 2)]
+    + [(name, AT["k", i]) for name in ("prev", "own", "next") for i in range(4)]
     + [("nn", 2)]
 )
-PARTS = ("pp", "prev", "own", "next", "nn")
 
 
 def two_sum(a, b):
@@ -194,18 +198,111 @@
     return lax.broadcasted_iota(jnp.int32, shape, len(shape) - 1)
 
 
+def is_odd():
+    return lax.rem(lax.axis_index("gx_2"), 2) == 1
+
+
+def at_step():
+    place = lax.axis_index("gx_1") * YS + lax.axis_index("gx_2")
+    return (place == 0) | (place == SEG - 1)
+
+
+def start_kernel(flags, rhs, kappa, own, p0, p1, p2, p3, across):
+    for i in range(4):
+        k = kappa[i]
+        shifted = 6.0 + k
+        own[AT["v", i]] = (1.0 / (shifted * shifted + 6.0)) * rhs[i]
+        own[AT["k", i]] = k
+    for i, piece in enumerate((p0, p1, p2, p3)):
+        piece[...] = own[2 * i : 2 * i + 2]
+
+    @pl.when(flags[0] == 1)
+    def _():
+        across[...] = own[0:3]
+
+    @pl.when(flags[0] == 0)
+    def _():
+        across[...] = own[5:8]
+
+
+def forward_odd_kernel(flags, even, out):
+    @pl.when(flags[0] == 1)
+    def _():
+        out[...] = even[5:8]
+
+    @pl.when(flags[0] == 0)
+    def _():
+        out[...] = even[0:3]
+
+
+def forward_even_kernel(flags, odd, d0, d1, d2, d3, out, block):
+    @pl.when(flags[1] == 0)
+    def _():
+        block[...] = odd[...]
+
+    @pl.when(flags[1] == 1)
+    def _():
+        for i, piece in enumerate((d0, d1, d2, d3)):
+            block[2 * i : 2 * i + 2] = piece[...]
+
+    @pl.when(flags[0] == 1)
+    def _():
+        out[...] = block[0:3]
+
+    @pl.when(flags[0] == 0)
+    def _():
+        out[...] = block[5:8]
+
+
+def gather_kernel(flags, own, even, odd, even2, odd2, across, center, first, last):
+    def lay(names):
+        for j, (name, at) in enumerate(PLANES):
+            if name in names:
+                plane = names[name][at]
+                center[j] = plane
+                first[j] = plane[0:8]
+                last[j] = plane[56:64]
+
+    lay({"own": own})
+    odd_place = flags[0] == 1
+    inner = flags[1] == 0
+
+    @pl.when(odd_place)
+    def _():
+        lay({"prev": even, "next": odd, "pp": even2})
+
+    @pl.when(odd_place & inner)
+    def _():
+        lay({"nn": odd2})
+
+    @pl.when(odd_place & ~inner)
+    def _():
+        lay({"nn": across})
+
+    @pl.when(~odd_place)
+    def _():
+        lay({"prev": odd, "next": even, "nn": even2})
+
+    @pl.when(~odd_place & inner)
+    def _():
+        lay({"pp": odd2})
+
+    @pl.when(~odd_place & ~inner)
+    def _():
+        lay({"pp": across})
+
+
 def powers_kernel(
-    rhs, pp, prev, own, nxt, nn, low, high,
+    rhs, center, low, high,
     y1_out, y2_out, y3_out, sums_out,
     v, k, t1, w1, t2, w2, t3, y1s, y2s, rows,
 ):
-    parts = dict(zip(PARTS, (pp, prev, own, nxt, nn)))
-    for j, (name, at) in enumerate(V_PLANES):
-        v[j, 8:72] = parts[name][at]
+    for j in range(16):
+        v[j, 8:72] = center[j]
         v[j, 0:8] = low[j]
         v[j, 72:80] = high[j]
-    for j, (name, at) in enumerate(K_PLANES):
-        k[j, 8:72] = 6.0 + parts[name][at]
+    for j in range(14):
+        k[j, 8:72] = 6.0 + center[16 + j]
         k[j, 0:8] = 6.0 + low[16 + j]
         k[j, 72:80] = 6.0 + high[16 + j]
 
@@ -300,10 +397,8 @@
     table = [pair(6 + d) for d in range(6)]
     place = {(0, 0): 0, (0, 1): 1, (0, 2): 2, (1, 1): 3, (1, 2): 4, (2, 2): 5}
     c, rr = coefficients(mu, lambda a, b: table[place[a, b]])
-    rms = jnp.zeros((1, 128), F32)
     for i in range(3):
-        rms = jnp.where(lane == i, jnp.sqrt(rr[i] / F32(cells)), rms)
-    rms_out[...] = rms
+        rms_out[i] = jnp.sqrt(rr[i] / F32(cells))[0, 0]
     wide = [jnp.broadcast_to(a, rhs.shape[1:]) for a in c]
 
     @pl.loop(0, 4)
@@ -314,43 +409,63 @@
         r_out[i] = a0 - (wide[0] * a1 + wide[1] * a2 + wide[2] * y3[i])
 
 
-def kernel(fn, outs, scratch=(), flops=0):
-    return pl.pallas_call(
-        fn,
-        out_shape=[jax.ShapeDtypeStruct(s, F32) for s in outs],
-        scratch_shapes=[pltpu.VMEM(s, F32) for s in scratch],
-        cost_estimate=pl.CostEstimate(flops=flops, bytes_accessed=flops // 8 + 1024, transcendentals=0),
-    )
+def kernel(fn, outs, scratch=(), flops=0, flagged=False, scalars=False, limit=24):
+    def call(*args):
+        specs = [VMEM] * len(args)
+        out_specs = [VMEM] * len(outs)
+        if flagged:
+            specs[0] = pl.BlockSpec(memory_space=pltpu.SMEM)
+        if scalars:
+            out_specs[-1] = pl.BlockSpec(memory_space=pltpu.SMEM)
+        return pl.pallas_call(
+            fn,
+            out_shape=[jax.ShapeDtypeStruct(s, F32) for s in outs],
+            in_specs=specs,
+            out_specs=out_specs,
+            scratch_shapes=[pltpu.VMEM(s, F32) for s in scratch],
+            cost_estimate=pl.CostEstimate(
+                flops=flops, bytes_accessed=flops // 8 + 1024, transcendentals=0
+            ),
+            compiler_params=pltpu.CompilerParams(vmem_limit_bytes=limit << 20),
+        )(*args)
+
+    return call
 
 
 def send(x, pairs):
     return lax.ppermute(x, ALL, pairs)
 
 
-def neighbours(block):
-    relayed = [send(block[a:b], spread) for (a, b), (spread, _) in zip(CUTS, ROUTES)]
-    up = send(block, UP)
-    down = send(block, DOWN)
-    pp = send(block[5:8], UP2)
-    nn = send(block[0:3], DOWN2)
-    far = jnp.concatenate([send(x, onward) for x, (_, onward) in zip(relayed, ROUTES)], axis=0)
-    place = lax.axis_index(PLANE)
-    prev = jnp.where(place == 0, far, up)
-    nxt = jnp.where(place == SEG - 1, far, down)
-    return pp, prev, nxt, nn
-
-
-def body(right_side, kappa_sq):
+def extended(flags, right_side, kappa_sq):
+    _, cols, lanes = right_side.shape
+    shape = lambda n: (n, cols, lanes)
+    own, p0, p1, p2, p3, near = kernel(
+        start_kernel, [shape(8)] + [shape(2)] * 4 + [shape(3)], flops=10**6, flagged=True
+    )(flags, right_side, kappa_sq)
+    relayed = [send(piece, spread) for piece, (spread, _) in zip((p0, p1, p2), ROUTES)]
+    across = send(near, ACROSS)
+    even = send(own, EVEN)
+    odd = send(own, ODD)
+    pieces = [send(x, onward) for x, (_, onward) in zip(relayed, ROUTES)]
+    pieces.append(send(p3, STEP))
+    (near,) = kernel(forward_odd_kernel, [shape(3)], flops=10**5, flagged=True)(flags, even)
+    odd2 = send(near, ODD)
+    near, odd = kernel(
+        forward_even_kernel, [shape(3), shape(8)], flops=10**5, flagged=True
+    )(flags, odd, *pieces)
+    even2 = send(near, EVEN)
+    edge = (len(PLANES), 8, lanes)
+    return kernel(
+        gather_kernel, [shape(len(PLANES)), edge, edge], flops=10**6, flagged=True
+    )(flags, own, even, odd, even2, odd2, across)
+
+
+def steps(right_side, kappa_sq):
     cells = right_side.size * NGX * RANKS
-    shifted = 6.0 + kappa_sq
-    start = (1.0 / (shifted * shifted + 6.0)) * right_side
-    source = {"v": start, "k": kappa_sq}
-    own = jnp.stack([source[a][i] for a, i in ORDER])
-    pp, prev, nxt, nn = neighbours(own)
-    parts = dict(zip(PARTS, (pp, prev, own, nxt, nn)))
-    edge = lambda cut: jnp.stack([parts[name][at, cut] for name, at in V_PLANES + K_PLANES])
-    low = send(edge(slice(56, 64)), GY_UP)
-    high = send(edge(slice(0, 8)), GY_DOWN)
+    flags = jnp.stack([is_odd(), at_step()]).astype(jnp.int32)
+    center, first, last = extended(flags, right_side, kappa_sq)
+    low = send(last, GY_UP)
+    high = send(first, GY_DOWN)
     block, wide = right_side.shape, (80, 256)
     n_plane, n_column = lax.axis_size(PLANE), lax.axis_size(COLUMN)
     counts = (16, 14, 14, 12, 10, 8, 6, 12, 8)
@@ -359,18 +474,17 @@
         [block] * 3 + [(n_plane, 128)],
         [(n, *wide) for n in counts] + [(128, 128)],
         flops=20_000_000,
-    )(right_side, pp, prev, own, nxt, nn, low, high)
+    )(right_side, center, low, high)
     sums = lax.all_to_all(sums.reshape(n_plane, 1, 128), PLANE, 0, 0).reshape(n_plane, 128)
     (sums,) = kernel(add_kernel, [(n_column, 128)], flops=20000)(sums)
     sums = lax.all_to_all(sums.reshape(n_column, 1, 128), COLUMN, 0, 0).reshape(n_column, 128)
-    x, r, rms = kernel(
-        functools.partial(finish_kernel, cells), [block, block, (1, 128)], flops=2_000_000
+    return kernel(
+        functools.partial(finish_kernel, cells), [block, block, (3,)], flops=2_000_000, scalars=True
     )(sums, right_side, kappa_sq, y1, y2, y3)
-    return x, r, rms[0, :3]
 
 
 def solution(mesh):
     finer = Mesh(mesh.devices.reshape(3, 4, 8, 4, 2), ("gx_0", "gx_1", "gx_2", "gy_0", "gy_1"))
     in_specs = (P(GX, GY, None), P(GX, GY, None))
     out_specs = (P(GX, GY, None), P(GX, GY, None), P())
-    return jax.shard_map(body, mesh=finer, in_specs=in_specs, out_specs=out_specs, check_vma=False)
+    return jax.shard_map(steps, mesh=finer, in_specs=in_specs, out_specs=out_specs, check_vma=False)

time: 142 us -> 132 us (0.930)
  waiting for transfers between devices: 23.8 us -> 40.6 us
  blocking collectives: 44.9 us -> 30.4 us
  starting transfers between devices: 53.7 us -> 46.9 us
  Pallas kernels: 13.3 us -> 11 us
  local copies, waits for them, and re-layouts: 3.79 us -> 1.91 us
    ppermute x12 -> x14, waiting for transfers between devices: 23.8 us -> 40.6 us  [send(): return lax.ppermute(x, ALL, pairs)]
    all_to_all x2, blocking collectives: 44.9 us -> 30.4 us  [the longest x1 18.8 us: steps(): lax.all_to_all(sums.reshape(n_column, 1, 128), COLUMN, 0, 0)]
    ppermute x12 -> x14, starting transfers between devices: 53.7 us -> 46.9 us  [send(): return lax.ppermute(x, ALL, pairs)]
    pallas_call x3 -> x7, Pallas kernels: 13.3 us -> 11 us  [call(): pl.pallas_call(fn, out_shape=[jax.ShapeDtypeStruct(s, F32) for s in outs]...]
  transfers between devices with their start and end apart: 12 -> 14, of which waited for: 5 -> 5; matrix products, arithmetic and copies ran while one was open for 0% -> 0% of each run, Pallas kernels for 0% -> 1%
where the time goes in v3:
time: 132 us
  starting transfers between devices  46.9 us (36%)
  waiting for transfers between devices  40.6 us (31%)
  blocking collectives  30.4 us (23%)
  Pallas kernels  11 us (8%)
  local copies, waits for them, and re-layouts  1.91 us (1%)
    ppermute x14, starting transfers between devices, send(): return lax.ppermute(x, ALL, pairs)  46.9 us
    ppermute x14, waiting for transfers between devices, send(): return lax.ppermute(x, ALL, pairs)  40.6 us
    all_to_all x1, blocking collectives, steps(): lax.all_to_all(sums.reshape(n_column, 1, 128), COLUMN, 0, 0)  18.8 us
    all_to_all x1, blocking collectives, steps(): lax.all_to_all(sums.reshape(n_plane, 1, 128), PLANE, 0, 0)  11.6 us
    pallas_call x7, Pallas kernels, call(): pl.pallas_call(fn, out_shape=[jax.ShapeDtypeStruct(s, F32) for s in outs]...  11 us
  transfers between devices with their start and end apart: 14, of which 5 were waited for; matrix products, arithmetic and copies ran while one was open for 0% of the time, Pallas kernels for 1%

profile of v3, /device:TPU:1, one launch (start us, length us, event | category | flops | bytes accessed | tf_op | source)
XLA Modules:
  0.0 131.7 jit_solution(14934912638940302068)
XLA Ops:
  0.6 0.1 add_convert_fusion.flags
  0.7 0.0 copy-start
  0.7 0.9 copy-done
  1.7 0.0 copy-start.2
  1.7 0.9 copy-done.2
  2.6 0.6 shard_map.49
  3.3 0.7 collective-permute-start.1
  4.0 6.5 %collective-permute-start = (f32[8,64,256]{2,1,0:T(8,128)S(1)}, f32[8,64,256]{2,1,0:T(8,128)S(1)}, u32[]{:S(2)}, u32[]{:S(2)}) collective-permute-start(f32[8,64,256]{2,1,0:T(8,128)S(1)} %get-tuple-element.18.own), channel_id=1, source_target_pairs={{0,8},{1,9},{2,10},{3,11},{4,12},{5,13},{6,14},{7,15},{8,0},{9,1},... | collective-permute-start | bytes 1572872 | tf_op jit(solution)/shard_map/ppermute | solution.py:436
  10.5 5.3 %collective-permute-start.2 = (f32[2,64,256]{2,1,0:T(8,128)S(1)}, f32[2,64,256]{2,1,0:T(8,128)S(1)}, u32[]{:S(2)}, u32[]{:S(2)}) collective-permute-start(f32[2,64,256]{2,1,0:T(8,128)S(1)} %get-tuple-element.19), channel_id=1, source_target_pairs={{248,56},{249,57},{250,58},{251,59},{252,60},{253,61},{254,62},{25... | collective-permute-start | bytes 393224 | tf_op jit(solution)/shard_map/ppermute | solution.py:436
  15.8 1.3 collective-permute-start.4
  17.1 1.3 collective-permute-start.6
  18.4 0.0 collective-permute-done.2
  18.4 16.4 %collective-permute-start.8 = (f32[2,64,256]{2,1,0:T(8,128)S(1)}, f32[2,64,256]{2,1,0:T(8,128)S(1)}, u32[]{:S(2)}, u32[]{:S(2)}) collective-permute-start(f32[2,64,256]{2,1,0:T(8,128)S(1)} %get-tuple-element.22), channel_id=1, source_target_pairs={{248,256},{249,257},{250,258},{251,259},{252,260},{253,261},{254,2... | collective-permute-start | bytes 393224 | tf_op jit(solution)/shard_map/ppermute | solution.py:436
  34.8 0.0 collective-permute-done.4
  34.8 1.3 collective-permute-start.3
  36.1 0.0 collective-permute-done.6
  36.1 1.3 collective-permute-start.5
  37.4 0.1 collective-permute-done.8.d3
  37.5 1.3 collective-permute-start.7
  38.8 17.5 %collective-permute-done.3.d0 = f32[2,64,256]{2,1,0:T(8,128)S(1)} collective-permute-done((f32[2,64,256]{2,1,0:T(8,128)S(1)}, f32[2,64,256]{2,1,0:T(8,128)S(1)}, u32[]{:S(2)}, u32[]{:S(2)}) %collective-permute-start.3) | collective-permute-done | bytes 131104 | tf_op jit(solution)/shard_map/ppermute | solution.py:436
  56.2 0.0 copy-start.1
  56.2 1.4 %collective-permute-start.11 = (f32[3,64,256]{2,1,0:T(8,128)S(1)}, f32[3,64,256]{2,1,0:T(8,128)S(1)}, u32[]{:S(2)}, u32[]{:S(2)}) collective-permute-start(f32[3,64,256]{2,1,0:T(8,128)S(1)} %get-tuple-element.25), channel_id=1, source_target_pairs={{240,256},{241,257},{242,258},{243,259},{244,260},{245,261},{246,2... | collective-permute-start | bytes 589832 | tf_op jit(solution)/shard_map/ppermute | solution.py:436
  57.7 0.0 collective-permute-done.5.d1
  57.7 0.0 collective-permute-done.7.d2
  57.7 0.0 collective-permute-done.1.odd
  57.7 0.6 shard_map.50
  58.3 1.9 %collective-permute-start.9 = (f32[3,64,256]{2,1,0:T(8,128)S(1)}, f32[3,64,256]{2,1,0:T(8,128)S(1)}, u32[]{:S(2)}, u32[]{:S(2)}) collective-permute-start(f32[3,64,256]{2,1,0:T(8,128)S(1)} %get-tuple-element.24), channel_id=1, source_target_pairs={{0,8},{1,9},{2,10},{3,11},{4,12},{5,13},{6,14},{7,15},{8,0},{9,1},... | collective-permute-start | bytes 589832 | tf_op jit(solution)/shard_map/ppermute | solution.py:436
  60.2 0.0 collective-permute-done.even
  60.3 0.6 shard_map.51
  60.8 0.7 collective-permute-start.10
  61.5 16.9 %collective-permute-done.11.across = f32[3,64,256]{2,1,0:T(8,128)S(1)} collective-permute-done((f32[3,64,256]{2,1,0:T(8,128)S(1)}, f32[3,64,256]{2,1,0:T(8,128)S(1)}, u32[]{:S(2)}, u32[]{:S(2)}) %collective-permute-start.11) | collective-permute-done | bytes 196640 | tf_op jit(solution)/shard_map/ppermute | solution.py:436
  78.4 0.0 collective-permute-done.9.even2
  78.4 0.0 collective-permute-done.10.odd2
  78.4 0.0 copy-start.3
  78.4 0.7 shard_map.52
  79.1 5.6 %collective-permute-start.12 = (f32[30,8,256]{2,1,0:T(8,128)S(1)}, f32[30,8,256]{2,1,0:T(8,128)S(1)}, u32[]{:S(2)}, u32[]{:S(2)}) collective-permute-start(f32[30,8,256]{2,1,0:T(8,128)S(1)} %get-tuple-element.27), channel_id=1, source_target_pairs={{0,1},{1,2},{2,3},{3,4},{4,5},{5,6},{6,7},{7,0},{8,9},{9,10},{10,1... | collective-permute-start | bytes 737288 | tf_op jit(solution)/shard_map/ppermute | solution.py:436
  84.7 1.9 %collective-permute-start.13 = (f32[30,8,256]{2,1,0:T(8,128)S(1)}, f32[30,8,256]{2,1,0:T(8,128)S(1)}, u32[]{:S(2)}, u32[]{:S(2)}) collective-permute-start(f32[30,8,256]{2,1,0:T(8,128)S(1)} %get-tuple-element.28), channel_id=1, source_target_pairs={{1,0},{2,1},{3,2},{4,3},{5,4},{6,5},{7,6},{0,7},{9,8},{10,9},{11,1... | collective-permute-start | bytes 737288 | tf_op jit(solution)/shard_map/ppermute | solution.py:436
  86.7 1.2 collective-permute-done.12.low
  87.9 5.0 %collective-permute-done.13.high = f32[30,8,256]{2,1,0:T(8,128)S(1)} collective-permute-done((f32[30,8,256]{2,1,0:T(8,128)S(1)}, f32[30,8,256]{2,1,0:T(8,128)S(1)}, u32[]{:S(2)}, u32[]{:S(2)}) %collective-permute-start.13) | collective-permute-done | bytes 245792 | tf_op jit(solution)/shard_map/ppermute | solution.py:436
  92.8 0.0 copy-done.1
  92.8 6.8 %shard_map.53 = (f32[4,64,256]{2,1,0:T(8,128)S(1)}, f32[4,64,256]{2,1,0:T(8,128)S(1)}, f32[4,64,256]{2,1,0:T(8,128)S(1)}, f32[32,128]{1,0:T(8,128)S(1)}) custom-call(f32[4,64,256]{2,1,0:T(8,128)S(1)} %copy-done.1, f32[30,64,256]{2,1,0:T(8,128)S(1)} %get-tuple-element.26.center, f32[30,8,256]{2,1,0:T(8,128)S(1)} %collective-permute-done.12.low, ...), custom_call_target="tpu_custom_call" | custom-call | flops 20000000 | bytes 2501024 | tf_op jit(solution)/shard_map/pallas_call | solution.py:420
  99.7 11.6 %all_to_all.10 = f32[32,1,128]{2,1,0:T(1,128)S(1)} all-to-all(f32[32,1,128]{2,1,0:T(1,128)S(1)} %bitcast.13), channel_id=1, replica_groups=mesh['gx_0'=3,'gx_1'=4,'gx_2'=8,'gy_0'=4,'gy_1'=2] {'gx_1','gx_2'}, dimensions={0} | all-to-all | bytes 32768 | tf_op jit(solution)/shard_map/all_to_all | solution.py:478
  111.3 0.1 shard_map.54
  111.4 18.8 %all_to_all.11 = f32[24,1,128]{2,1,0:T(1,128)S(1)} all-to-all(f32[24,1,128]{2,1,0:T(1,128)S(1)} %bitcast.12), channel_id=1, replica_groups=mesh['gx_0'=3,'gx_1'=4,'gx_2'=8,'gy_0'=4,'gy_1'=2] {'gx_0','gy_0','gy_1'}, dimensions={0} | all-to-all | bytes 24576 | tf_op jit(solution)/shard_map/all_to_all | solution.py:480
  130.2 0.0 copy-done.3
  130.2 1.5 %shard_map.55 = (f32[4,64,256]{2,1,0:T(8,128)}, f32[4,64,256]{2,1,0:T(8,128)}, f32[3]{0:T(128)}) custom-call(f32[24,128]{1,0:T(8,128)S(1)} %bitcast.11, f32[4,64,256]{2,1,0:T(8,128)S(1)} %copy-done.1, f32[4,64,256]{2,1,0:T(8,128)S(1)} %copy-done.3, f32[4,64,256]{2,1,0:T(8,128)S(1)} %get-tuple-element.30.y1, f32[4,64,256]{2,1,0:T(8,128)S(1)} %get-tuple-element.31.y2, ...), custom_call_target="tpu_custom_call" | custom-call | flops 2000000 | bytes 251024 | tf_op jit(solution)/shard_map/pallas_call | solution.py:420
Async XLA Ops:
  0.7 1.0 copy-start
  1.7 0.9 copy-start.2
  3.3 54.4 %collective-permute-start.1 = (f32[8,64,256]{2,1,0:T(8,128)S(1)}, f32[8,64,256]{2,1,0:T(8,128)S(1)}, u32[]{:S(2)}, u32[]{:S(2)}) collective-permute-start(f32[8,64,256]{2,1,0:T(8,128)S(1)} %get-tuple-element.18.own), channel_id=1, source_target_pairs={{8,16},{9,17},{10,18},{11,19},{12,20},{13,21},{14,22},{15,23},{16,... | collective-permute-start | bytes 1572872 | tf_op jit(solution)/shard_map/ppermute | solution.py:436
  4.0 56.3 %collective-permute-start = (f32[8,64,256]{2,1,0:T(8,128)S(1)}, f32[8,64,256]{2,1,0:T(8,128)S(1)}, u32[]{:S(2)}, u32[]{:S(2)}) collective-permute-start(f32[8,64,256]{2,1,0:T(8,128)S(1)} %get-tuple-element.18.own), channel_id=1, source_target_pairs={{0,8},{1,9},{2,10},{3,11},{4,12},{5,13},{6,14},{7,15},{8,0},{9,1},... | collective-permute-start | bytes 1572872 | tf_op jit(solution)/shard_map/ppermute | solution.py:436
  10.5 7.9 %collective-permute-start.2 = (f32[2,64,256]{2,1,0:T(8,128)S(1)}, f32[2,64,256]{2,1,0:T(8,128)S(1)}, u32[]{:S(2)}, u32[]{:S(2)}) collective-permute-start(f32[2,64,256]{2,1,0:T(8,128)S(1)} %get-tuple-element.19), channel_id=1, source_target_pairs={{248,56},{249,57},{250,58},{251,59},{252,60},{253,61},{254,62},{25... | collective-permute-start | bytes 393224 | tf_op jit(solution)/shard_map/ppermute | solution.py:436
  15.8 19.0 %collective-permute-start.4 = (f32[2,64,256]{2,1,0:T(8,128)S(1)}, f32[2,64,256]{2,1,0:T(8,128)S(1)}, u32[]{:S(2)}, u32[]{:S(2)}) collective-permute-start(f32[2,64,256]{2,1,0:T(8,128)S(1)} %get-tuple-element.20), channel_id=1, source_target_pairs={{248,192},{249,193},{250,194},{251,195},{252,196},{253,197},{254,1... | collective-permute-start | bytes 393224 | tf_op jit(solution)/shard_map/ppermute | solution.py:436
  17.1 19.0 %collective-permute-start.6 = (f32[2,64,256]{2,1,0:T(8,128)S(1)}, f32[2,64,256]{2,1,0:T(8,128)S(1)}, u32[]{:S(2)}, u32[]{:S(2)}) collective-permute-start(f32[2,64,256]{2,1,0:T(8,128)S(1)} %get-tuple-element.21), channel_id=1, source_target_pairs={{248,184},{249,185},{250,186},{251,187},{252,188},{253,189},{254,1... | collective-permute-start | bytes 393224 | tf_op jit(solution)/shard_map/ppermute | solution.py:436
  18.4 19.1 %collective-permute-start.8 = (f32[2,64,256]{2,1,0:T(8,128)S(1)}, f32[2,64,256]{2,1,0:T(8,128)S(1)}, u32[]{:S(2)}, u32[]{:S(2)}) collective-permute-start(f32[2,64,256]{2,1,0:T(8,128)S(1)} %get-tuple-element.22), channel_id=1, source_target_pairs={{248,256},{249,257},{250,258},{251,259},{252,260},{253,261},{254,2... | collective-permute-start | bytes 393224 | tf_op jit(solution)/shard_map/ppermute | solution.py:436
  34.8 21.4 %collective-permute-start.3 = (f32[2,64,256]{2,1,0:T(8,128)S(1)}, f32[2,64,256]{2,1,0:T(8,128)S(1)}, u32[]{:S(2)}, u32[]{:S(2)}) collective-permute-start(f32[2,64,256]{2,1,0:T(8,128)S(1)} %collective-permute-done.2), channel_id=1, source_target_pairs={{56,256},{57,257},{58,258},{59,259},{60,260},{61,261},{62,262},{63... | collective-permute-start | bytes 393224 | tf_op jit(solution)/shard_map/ppermute | solution.py:436
  36.1 21.6 %collective-permute-start.5 = (f32[2,64,256]{2,1,0:T(8,128)S(1)}, f32[2,64,256]{2,1,0:T(8,128)S(1)}, u32[]{:S(2)}, u32[]{:S(2)}) collective-permute-start(f32[2,64,256]{2,1,0:T(8,128)S(1)} %collective-permute-done.4), channel_id=1, source_target_pairs={{192,256},{193,257},{194,258},{195,259},{196,260},{197,261},{198,2... | collective-permute-start | bytes 393224 | tf_op jit(solution)/shard_map/ppermute | solution.py:436
  37.5 20.2 %collective-permute-start.7 = (f32[2,64,256]{2,1,0:T(8,128)S(1)}, f32[2,64,256]{2,1,0:T(8,128)S(1)}, u32[]{:S(2)}, u32[]{:S(2)}) collective-permute-start(f32[2,64,256]{2,1,0:T(8,128)S(1)} %collective-permute-done.6), channel_id=1, source_target_pairs={{184,256},{185,257},{186,258},{187,259},{188,260},{189,261},{190,2... | collective-permute-start | bytes 393224 | tf_op jit(solution)/shard_map/ppermute | solution.py:436
  56.2 36.6 %copy-start.1 = (f32[4,64,256]{2,1,0:T(8,128)S(1)}, f32[4,64,256]{2,1,0:T(8,128)}, u32[]{:S(2)}) copy-start(f32[4,64,256]{2,1,0:T(8,128)} %rhs.5) | copy-start | bytes 786436
  56.2 22.1 %collective-permute-start.11 = (f32[3,64,256]{2,1,0:T(8,128)S(1)}, f32[3,64,256]{2,1,0:T(8,128)S(1)}, u32[]{:S(2)}, u32[]{:S(2)}) collective-permute-start(f32[3,64,256]{2,1,0:T(8,128)S(1)} %get-tuple-element.25), channel_id=1, source_target_pairs={{240,256},{241,257},{242,258},{243,259},{244,260},{245,261},{246,2... | collective-permute-start | bytes 589832 | tf_op jit(solution)/shard_map/ppermute | solution.py:436
  58.3 20.1 %collective-permute-start.9 = (f32[3,64,256]{2,1,0:T(8,128)S(1)}, f32[3,64,256]{2,1,0:T(8,128)S(1)}, u32[]{:S(2)}, u32[]{:S(2)}) collective-permute-start(f32[3,64,256]{2,1,0:T(8,128)S(1)} %get-tuple-element.24), channel_id=1, source_target_pairs={{0,8},{1,9},{2,10},{3,11},{4,12},{5,13},{6,14},{7,15},{8,0},{9,1},... | collective-permute-start | bytes 589832 | tf_op jit(solution)/shard_map/ppermute | solution.py:436
  60.8 17.6 %collective-permute-start.10 = (f32[3,64,256]{2,1,0:T(8,128)S(1)}, f32[3,64,256]{2,1,0:T(8,128)S(1)}, u32[]{:S(2)}, u32[]{:S(2)}) collective-permute-start(f32[3,64,256]{2,1,0:T(8,128)S(1)} %shard_map.51), channel_id=1, source_target_pairs={{8,16},{9,17},{10,18},{11,19},{12,20},{13,21},{14,22},{15,23},{16,... | collective-permute-start | bytes 589832 | tf_op jit(solution)/shard_map/ppermute | solution.py:436
  78.4 51.8 %copy-start.3 = (f32[4,64,256]{2,1,0:T(8,128)S(1)}, f32[4,64,256]{2,1,0:T(8,128)}, u32[]{:S(2)}) copy-start(f32[4,64,256]{2,1,0:T(8,128)} %kappa.3) | copy-start | bytes 786436
  79.1 8.8 %collective-permute-start.12 = (f32[30,8,256]{2,1,0:T(8,128)S(1)}, f32[30,8,256]{2,1,0:T(8,128)S(1)}, u32[]{:S(2)}, u32[]{:S(2)}) collective-permute-start(f32[30,8,256]{2,1,0:T(8,128)S(1)} %get-tuple-element.27), channel_id=1, source_target_pairs={{0,1},{1,2},{2,3},{3,4},{4,5},{5,6},{6,7},{7,0},{8,9},{9,10},{10,1... | collective-permute-start | bytes 737288 | tf_op jit(solution)/shard_map/ppermute | solution.py:436
  84.7 8.1 %collective-permute-start.13 = (f32[30,8,256]{2,1,0:T(8,128)S(1)}, f32[30,8,256]{2,1,0:T(8,128)S(1)}, u32[]{:S(2)}, u32[]{:S(2)}) collective-permute-start(f32[30,8,256]{2,1,0:T(8,128)S(1)} %get-tuple-element.28), channel_id=1, source_target_pairs={{1,0},{2,1},{3,2},{4,3},{5,4},{6,5},{7,6},{0,7},{9,8},{10,9},{11,1... | collective-permute-start | bytes 737288 | tf_op jit(solution)/shard_map/ppermute | solution.py:436

commit v4 on v3

--- a/solution.py
+++ b/solution.py
@@ -59,6 +59,8 @@
 STEP = over_gx(
     [(LAST(k), FIRST(k + 1)) for k in SEGS] + [(FIRST(k), LAST(k - 1)) for k in SEGS]
 )
+LOW2 = over_gx([(g, g ^ 2) for g in range(NGX)])
+HIGH2 = over_gx([(g, ((g + 2) ^ 2) - 2) for g in range(NGX) if 1 < g % SEG < SEG - 2])
 ACROSS = over_gx(
     [(LAST(k) - 1, FIRST(k + 1)) for k in SEGS] + [(FIRST(k) + 1, LAST(k - 1)) for k in SEGS]
 )
@@ -75,9 +77,18 @@
         over_gx([(LAST(k), NEAR_LAST(k)) for k in SEGS] + [(FIRST(k), NEAR_FIRST(k)) for k in SEGS]),
         over_gx([(NEAR_LAST(k), FIRST(k + 1)) for k in SEGS] + [(NEAR_FIRST(k), LAST(k - 1)) for k in SEGS]),
     ),
+    (
+        over_gx([(LAST(k), corner(k, XS - 1, 1)) for k in SEGS] + [(FIRST(k), corner(k, 0, YS - 2)) for k in SEGS]),
+        over_gx(
+            [(corner(k, XS - 1, 1), FIRST(k + 1) + 1) for k in SEGS]
+            + [(corner(k, 0, YS - 2), LAST(k - 1) - 1) for k in SEGS]
+        ),
+    ),
 ]
-GY_UP = [(g * RANKS + h, g * RANKS + (h + 1) % RANKS) for g in range(NGX) for h in range(RANKS)]
-GY_DOWN = [(b, a) for a, b in GY_UP]
+GY_EVEN = [(g * RANKS + h, g * RANKS + (h ^ 1)) for g in range(NGX) for h in range(RANKS)]
+GY_ODD = [
+    (g * RANKS + h, g * RANKS + (((h + 1) ^ 1) - 1) % RANKS) for g in range(NGX) for h in range(RANKS)
+]
 
 ORDER = (("v", 0), ("v", 1), ("k", 0), ("k", 1), ("k", 2), ("v", 2), ("v", 3), ("k", 3))
 AT = {what: i for i, what in enumerate(ORDER)}
@@ -88,6 +99,8 @@
     + [(name, AT["k", i]) for name in ("prev", "own", "next") for i in range(4)]
     + [("nn", 2)]
 )
+
+WIDE = tuple(j for j in range(len(PLANES)) if j not in (0, 15, 16, 29))
 
 
 def two_sum(a, b):
@@ -198,16 +211,24 @@
     return lax.broadcasted_iota(jnp.int32, shape, len(shape) - 1)
 
 
-def is_odd():
-    return lax.rem(lax.axis_index("gx_2"), 2) == 1
-
-
-def at_step():
-    place = lax.axis_index("gx_1") * YS + lax.axis_index("gx_2")
-    return (place == 0) | (place == SEG - 1)
-
-
-def start_kernel(flags, rhs, kappa, own, p0, p1, p2, p3, across):
+def place_flags():
+    place = lax.axis_index(PLANE)
+    beside = (place == 0) | (place == SEG - 1)
+    near = (place < 2) | (place >= SEG - 2)
+    return jnp.stack(
+        [place % 2 == 1, place % 4 >= 2, lax.axis_index("gy_1") == 1, beside, near]
+    ).astype(jnp.int32)
+
+
+def start_kernel(flags, rhs_hbm, kappa_hbm, own, p0, p1, p2, p3, low2, high2, rhs, kappa, sems):
+    fetch = [
+        pltpu.make_async_copy(rhs_hbm, rhs, sems.at[0]),
+        pltpu.make_async_copy(kappa_hbm, kappa, sems.at[1]),
+    ]
+    for copy in fetch:
+        copy.start()
+    for copy in fetch:
+        copy.wait()
     for i in range(4):
         k = kappa[i]
         shifted = 6.0 + k
@@ -216,95 +237,87 @@
     for i, piece in enumerate((p0, p1, p2, p3)):
         piece[...] = own[2 * i : 2 * i + 2]
 
-    @pl.when(flags[0] == 1)
-    def _():
-        across[...] = own[0:3]
-
-    @pl.when(flags[0] == 0)
-    def _():
-        across[...] = own[5:8]
-
-
-def forward_odd_kernel(flags, even, out):
-    @pl.when(flags[0] == 1)
-    def _():
-        out[...] = even[5:8]
-
-    @pl.when(flags[0] == 0)
-    def _():
-        out[...] = even[0:3]
-
-
-def forward_even_kernel(flags, odd, d0, d1, d2, d3, out, block):
     @pl.when(flags[1] == 0)
     def _():
-        block[...] = odd[...]
+        low2[...] = own[5:8]
+        high2[...] = own[0:3]
 
     @pl.when(flags[1] == 1)
     def _():
-        for i, piece in enumerate((d0, d1, d2, d3)):
-            block[2 * i : 2 * i + 2] = piece[...]
-
-    @pl.when(flags[0] == 1)
-    def _():
-        out[...] = block[0:3]
-
-    @pl.when(flags[0] == 0)
-    def _():
-        out[...] = block[5:8]
-
-
-def gather_kernel(flags, own, even, odd, even2, odd2, across, center, first, last):
-    def lay(names):
+        low2[...] = own[0:3]
+        high2[...] = own[5:8]
+
+
+def gather_kernel(
+    flags, own, even, odd, low2, high2, across, ahead, d0, d1, d2, d3, center, to_even, to_odd
+):
+    even_side = pl.multiple_of((1 - flags[2]) * 56, 8)
+    odd_side = pl.multiple_of(flags[2] * 56, 8)
+
+    def lay(part, ref):
         for j, (name, at) in enumerate(PLANES):
-            if name in names:
-                plane = names[name][at]
-                center[j] = plane
-                first[j] = plane[0:8]
-                last[j] = plane[56:64]
-
-    lay({"own": own})
-    odd_place = flags[0] == 1
-    inner = flags[1] == 0
-
-    @pl.when(odd_place)
-    def _():
-        lay({"prev": even, "next": odd, "pp": even2})
-
-    @pl.when(odd_place & inner)
-    def _():
-        lay({"nn": odd2})
-
-    @pl.when(odd_place & ~inner)
-    def _():
-        lay({"nn": across})
-
-    @pl.when(~odd_place)
-    def _():
-        lay({"prev": odd, "next": even, "nn": even2})
-
-    @pl.when(~odd_place & inner)
-    def _():
-        lay({"pp": odd2})
-
-    @pl.when(~odd_place & ~inner)
-    def _():
-        lay({"pp": across})
+            if name == part:
+                src, i = ((d0, d1, d2, d3)[at // 2], at % 2) if ref is None else (ref, at)
+                center[j] = src[i]
+                if j in WIDE:
+                    to_even[WIDE.index(j)] = src[i, pl.ds(even_side, 8)]
+                    to_odd[WIDE.index(j)] = src[i, pl.ds(odd_side, 8)]
+
+    def when(*conditions):
+        here = functools.reduce(lambda a, b: a & b, [flags[i] == value for i, value in conditions])
+        return pl.when(here)
+
+    lay("own", own)
+    for value, (by_even, by_odd) in enumerate((("next", "prev"), ("prev", "next"))):
+
+        @when((0, value))
+        def _():
+            lay(by_even, even)
+
+        @when((0, value), (3, 0))
+        def _():
+            lay(by_odd, odd)
+
+        @when((0, value), (3, 1))
+        def _():
+            lay(by_odd, None)
+
+    for value, (by_low, by_high) in enumerate((("nn", "pp"), ("pp", "nn"))):
+
+        @when((1, value))
+        def _():
+            lay(by_low, low2)
+
+        @when((1, value), (4, 0))
+        def _():
+            lay(by_high, high2)
+
+        @when((1, value), (3, 1))
+        def _():
+            lay(by_high, across)
+
+        @when((1, value), (3, 0), (4, 1))
+        def _():
+            lay(by_high, ahead)
 
 
 def powers_kernel(
-    rhs, center, low, high,
+    flags, rhs, center, even, odd,
     y1_out, y2_out, y3_out, sums_out,
     v, k, t1, w1, t2, w2, t3, y1s, y2s, rows,
 ):
-    for j in range(16):
-        v[j, 8:72] = center[j]
-        v[j, 0:8] = low[j]
-        v[j, 72:80] = high[j]
-    for j in range(14):
-        k[j, 8:72] = 6.0 + center[16 + j]
-        k[j, 0:8] = 6.0 + low[16 + j]
-        k[j, 72:80] = 6.0 + high[16 + j]
+    even_side = pl.multiple_of((1 - flags[2]) * 72, 8)
+    odd_side = pl.multiple_of(flags[2] * 72, 8)
+    for j in range(30):
+        ref, at, base = (v, j, 0.0) if j < 16 else (k, j - 16, 6.0)
+        put = lambda plane: plane if ref is v else base + plane
+        ref[at, 8:72] = put(center[j])
+        if j in WIDE:
+            ref[at, pl.ds(even_side, 8)] = put(even[WIDE.index(j)])
+            ref[at, pl.ds(odd_side, 8)] = put(odd[WIDE.index(j)])
+        else:
+            ref[at, 0:8] = jnp.zeros((8, ref.shape[2]), F32)
+            ref[at, 72:80] = jnp.zeros((8, ref.shape[2]), F32)
 
     def apply(src, dst, shift, count):
         @pl.loop(0, count)
@@ -409,12 +422,14 @@
         r_out[i] = a0 - (wide[0] * a1 + wide[1] * a2 + wide[2] * y3[i])
 
 
-def kernel(fn, outs, scratch=(), flops=0, flagged=False, scalars=False, limit=24):
+def kernel(fn, outs, scratch=(), flops=0, flagged=False, scalars=False, fetched=0, limit=24):
     def call(*args):
         specs = [VMEM] * len(args)
         out_specs = [VMEM] * len(outs)
         if flagged:
             specs[0] = pl.BlockSpec(memory_space=pltpu.SMEM)
+        if fetched:
+            specs[-fetched:] = [pl.BlockSpec(memory_space=pltpu.HBM)] * fetched
         if scalars:
             out_specs[-1] = pl.BlockSpec(memory_space=pltpu.SMEM)
         return pl.pallas_call(
@@ -422,7 +437,8 @@
             out_shape=[jax.ShapeDtypeStruct(s, F32) for s in outs],
             in_specs=specs,
             out_specs=out_specs,
-            scratch_shapes=[pltpu.VMEM(s, F32) for s in scratch],
+            scratch_shapes=[pltpu.VMEM(s, F32) for s in scratch]
+            + [pltpu.SemaphoreType.DMA((fetched,))] * bool(fetched),
             cost_estimate=pl.CostEstimate(
                 flops=flops, bytes_accessed=flops // 8 + 1024, transcendentals=0
             ),
@@ -439,33 +455,33 @@
 def extended(flags, right_side, kappa_sq):
     _, cols, lanes = right_side.shape
     shape = lambda n: (n, cols, lanes)
-    own, p0, p1, p2, p3, near = kernel(
-        start_kernel, [shape(8)] + [shape(2)] * 4 + [shape(3)], flops=10**6, flagged=True
+    own, p0, p1, p2, p3, low2, high2 = kernel(
+        start_kernel,
+        [shape(8)] + [shape(2)] * 4 + [shape(3)] * 2,
+        [right_side.shape] * 2,
+        flops=10**6,
+        flagged=True,
+        fetched=2,
     )(flags, right_side, kappa_sq)
-    relayed = [send(piece, spread) for piece, (spread, _) in zip((p0, p1, p2), ROUTES)]
-    across = send(near, ACROSS)
-    even = send(own, EVEN)
-    odd = send(own, ODD)
-    pieces = [send(x, onward) for x, (_, onward) in zip(relayed, ROUTES)]
+    relayed = [send(piece, spread) for piece, (spread, _) in zip((p0, p1, p2, high2), ROUTES)]
+    swapped = [
+        send(x, pairs)
+        for x, pairs in ((own, EVEN), (own, ODD), (low2, LOW2), (high2, HIGH2), (high2, ACROSS))
+    ]
+    *pieces, ahead = [send(x, onward) for x, (_, onward) in zip(relayed, ROUTES)]
     pieces.append(send(p3, STEP))
-    (near,) = kernel(forward_odd_kernel, [shape(3)], flops=10**5, flagged=True)(flags, even)
-    odd2 = send(near, ODD)
-    near, odd = kernel(
-        forward_even_kernel, [shape(3), shape(8)], flops=10**5, flagged=True
-    )(flags, odd, *pieces)
-    even2 = send(near, EVEN)
-    edge = (len(PLANES), 8, lanes)
+    edge = (len(WIDE), 8, lanes)
     return kernel(
         gather_kernel, [shape(len(PLANES)), edge, edge], flops=10**6, flagged=True
-    )(flags, own, even, odd, even2, odd2, across)
+    )(flags, own, *swapped, ahead, *pieces)
 
 
 def steps(right_side, kappa_sq):
     cells = right_side.size * NGX * RANKS
-    flags = jnp.stack([is_odd(), at_step()]).astype(jnp.int32)
-    center, first, last = extended(flags, right_side, kappa_sq)
-    low = send(last, GY_UP)
-    high = send(first, GY_DOWN)
+    flags = place_flags()
+    center, to_even, to_odd = extended(flags, right_side, kappa_sq)
+    even = send(to_even, GY_EVEN)
+    odd = send(to_odd, GY_ODD)
     block, wide = right_side.shape, (80, 256)
     n_plane, n_column = lax.axis_size(PLANE), lax.axis_size(COLUMN)
     counts = (16, 14, 14, 12, 10, 8, 6, 12, 8)
@@ -474,7 +490,8 @@
         [block] * 3 + [(n_plane, 128)],
         [(n, *wide) for n in counts] + [(128, 128)],
         flops=20_000_000,
-    )(right_side, center, low, high)
+        flagged=True,
+    )(flags, right_side, center, even, odd)
     sums = lax.all_to_all(sums.reshape(n_plane, 1, 128), PLANE, 0, 0).reshape(n_plane, 128)
     (sums,) = kernel(add_kernel, [(n_column, 128)], flops=20000)(sums)
     sums = lax.all_to_all(sums.reshape(n_column, 1, 128), COLUMN, 0, 0).reshape(n_column, 128)

time: 132 us -> 141 us (1.068)
  starting transfers between devices: 46.9 us -> 64.5 us
  waiting for transfers between devices: 40.6 us -> 32.8 us
    ppermute x14 -> x16, starting transfers between devices: 46.9 us -> 64.5 us  [send(): return lax.ppermute(x, ALL, pairs)]
    ppermute x14 -> x16, waiting for transfers between devices: 40.6 us -> 32.8 us  [send(): return lax.ppermute(x, ALL, pairs)]
    pallas_call x7 -> x5, Pallas kernels: 11 us -> 10.5 us  [call(): pl.pallas_call(fn, out_shape=[jax.ShapeDtypeStruct(s, F32) for s in outs]...]
  transfers between devices with their start and end apart: 14 -> 16, of which waited for: 5 -> 5; matrix products, arithmetic and copies ran while one was open for 0% -> 0% of each run, Pallas kernels for 1% -> 0%
where the time goes in v4:
time: 141 us
  starting transfers between devices  64.5 us (46%)
  waiting for transfers between devices  32.8 us (23%)
  blocking collectives  30.1 us (21%)
  Pallas kernels  10.5 us (7%)
  local copies, waits for them, and re-layouts  2.02 us (1%)
    ppermute x16, starting transfers between devices, send(): return lax.ppermute(x, ALL, pairs)  64.5 us
    ppermute x16, waiting for transfers between devices, send(): return lax.ppermute(x, ALL, pairs)  32.8 us
    all_to_all x1, blocking collectives, steps(): lax.all_to_all(sums.reshape(n_column, 1, 128), COLUMN, 0, 0)  18.4 us
    all_to_all x1, blocking collectives, steps(): lax.all_to_all(sums.reshape(n_plane, 1, 128), PLANE, 0, 0)  11.6 us
    pallas_call x5, Pallas kernels, call(): pl.pallas_call(fn, out_shape=[jax.ShapeDtypeStruct(s, F32) for s in outs]...  10.5 us
  transfers between devices with their start and end apart: 16, of which 5 were waited for; matrix products, arithmetic and copies ran while one was open for 0% of the time, Pallas kernels for 0%

profile of v4, /device:TPU:1, one launch (start us, length us, event | category | flops | bytes accessed | tf_op | source)
XLA Modules:
  0.0 140.8 jit_solution(9487948179985066441)
XLA Ops:
  0.7 0.1 stack.23
  0.8 0.0 copy-start
  0.8 0.9 copy-done
  1.7 0.0 copy-start.2
  1.7 0.9 copy-done.2
  2.7 0.0 copy-start.1
  2.7 0.7 shard_map.49
  3.4 5.2 %collective-permute-start.7 = (f32[2,64,256]{2,1,0:T(8,128)S(1)}, f32[2,64,256]{2,1,0:T(8,128)S(1)}, u32[]{:S(2)}, u32[]{:S(2)}) collective-permute-start(f32[2,64,256]{2,1,0:T(8,128)S(1)} %get-tuple-element.20), channel_id=1, source_target_pairs={{248,56},{249,57},{250,58},{251,59},{252,60},{253,61},{254,62},{25... | collective-permute-start | bytes 393224 | tf_op jit(solution)/shard_map/ppermute | solution.py:452
  8.6 2.0 %collective-permute-start.9 = (f32[2,64,256]{2,1,0:T(8,128)S(1)}, f32[2,64,256]{2,1,0:T(8,128)S(1)}, u32[]{:S(2)}, u32[]{:S(2)}) collective-permute-start(f32[2,64,256]{2,1,0:T(8,128)S(1)} %get-tuple-element.21), channel_id=1, source_target_pairs={{248,192},{249,193},{250,194},{251,195},{252,196},{253,197},{254,1... | collective-permute-start | bytes 393224 | tf_op jit(solution)/shard_map/ppermute | solution.py:452
  10.6 1.3 collective-permute-start.11
  11.9 1.9 %collective-permute-start.2 = (f32[3,64,256]{2,1,0:T(8,128)S(1)}, f32[3,64,256]{2,1,0:T(8,128)S(1)}, u32[]{:S(2)}, u32[]{:S(2)}) collective-permute-start(f32[3,64,256]{2,1,0:T(8,128)S(1)} %get-tuple-element.18), channel_id=1, source_target_pairs={{0,16},{1,17},{2,18},{3,19},{4,20},{5,21},{6,22},{7,23},{8,24},{9,... | collective-permute-start | bytes 589832 | tf_op jit(solution)/shard_map/ppermute | solution.py:452
  13.8 16.4 %collective-permute-start.13 = (f32[2,64,256]{2,1,0:T(8,128)S(1)}, f32[2,64,256]{2,1,0:T(8,128)S(1)}, u32[]{:S(2)}, u32[]{:S(2)}) collective-permute-start(f32[2,64,256]{2,1,0:T(8,128)S(1)} %get-tuple-element.23), channel_id=1, source_target_pairs={{248,256},{249,257},{250,258},{251,259},{252,260},{253,261},{254,2... | collective-permute-start | bytes 393224 | tf_op jit(solution)/shard_map/ppermute | solution.py:452
  30.2 0.0 collective-permute-done.7
  30.2 0.7 collective-permute-start.1
  31.0 0.0 collective-permute-done.9
  31.0 1.9 %collective-permute-start = (f32[8,64,256]{2,1,0:T(8,128)S(1)}, f32[8,64,256]{2,1,0:T(8,128)S(1)}, u32[]{:S(2)}, u32[]{:S(2)}) collective-permute-start(f32[8,64,256]{2,1,0:T(8,128)S(1)} %get-tuple-element.17.own), channel_id=1, source_target_pairs={{0,8},{1,9},{2,10},{3,11},{4,12},{5,13},{6,14},{7,15},{8,0},{9,1},... | collective-permute-start | bytes 1572872 | tf_op jit(solution)/shard_map/ppermute | solution.py:452
  32.9 0.0 collective-permute-done.11
  32.9 1.3 collective-permute-start.5
  34.2 0.0 collective-permute-done.13.d3
  34.2 1.3 collective-permute-start.4
  35.5 0.0 collective-permute-done.2.low2
  35.5 0.7 collective-permute-start.3
  36.2 1.3 collective-permute-done.5
  37.5 1.3 collective-permute-start.8
  38.8 10.9 %collective-permute-done.4.across = f32[3,64,256]{2,1,0:T(8,128)S(1)} collective-permute-done((f32[3,64,256]{2,1,0:T(8,128)S(1)}, f32[3,64,256]{2,1,0:T(8,128)S(1)}, u32[]{:S(2)}, u32[]{:S(2)}) %collective-permute-start.4) | collective-permute-done | bytes 196640 | tf_op jit(solution)/shard_map/ppermute | solution.py:452
  49.7 0.7 collective-permute-start.6
  50.3 0.0 collective-permute-done.3.high2
  50.3 1.3 collective-permute-start.10
  51.6 0.0 collective-permute-done.8.d0
  51.7 1.3 collective-permute-start.12
  53.0 9.4 %collective-permute-done.10.d1 = f32[2,64,256]{2,1,0:T(8,128)S(1)} collective-permute-done((f32[2,64,256]{2,1,0:T(8,128)S(1)}, f32[2,64,256]{2,1,0:T(8,128)S(1)}, u32[]{:S(2)}, u32[]{:S(2)}) %collective-permute-start.10) | collective-permute-done | bytes 131104 | tf_op jit(solution)/shard_map/ppermute | solution.py:452
  62.4 3.7 %collective-permute-done.12.d2 = f32[2,64,256]{2,1,0:T(8,128)S(1)} collective-permute-done((f32[2,64,256]{2,1,0:T(8,128)S(1)}, f32[2,64,256]{2,1,0:T(8,128)S(1)}, u32[]{:S(2)}, u32[]{:S(2)}) %collective-permute-start.12) | collective-permute-done | bytes 131104 | tf_op jit(solution)/shard_map/ppermute | solution.py:452
  66.1 0.0 collective-permute-done.6.ahead
  66.1 0.0 collective-permute-done.1.odd
  66.1 0.0 collective-permute-done.even
  66.1 0.8 shard_map.50
  66.9 0.0 copy-start.3
  66.9 25.4 %collective-permute-start.14 = (f32[26,8,256]{2,1,0:T(8,128)S(1)}, f32[26,8,256]{2,1,0:T(8,128)S(1)}, u32[]{:S(2)}, u32[]{:S(2)}) collective-permute-start(f32[26,8,256]{2,1,0:T(8,128)S(1)} %get-tuple-element.25), channel_id=1, source_target_pairs={{0,1},{1,0},{2,3},{3,2},{4,5},{5,4},{6,7},{7,6},{8,9},{9,8},{10,11... | collective-permute-start | bytes 638984 | tf_op jit(solution)/shard_map/ppermute | solution.py:452
  92.3 1.9 %collective-permute-start.15 = (f32[26,8,256]{2,1,0:T(8,128)S(1)}, f32[26,8,256]{2,1,0:T(8,128)S(1)}, u32[]{:S(2)}, u32[]{:S(2)}) collective-permute-start(f32[26,8,256]{2,1,0:T(8,128)S(1)} %get-tuple-element.26), channel_id=1, source_target_pairs={{0,7},{1,2},{2,1},{3,4},{4,3},{5,6},{6,5},{7,0},{8,15},{9,10},{10,... | collective-permute-start | bytes 638984 | tf_op jit(solution)/shard_map/ppermute | solution.py:452
  94.2 0.0 collective-permute-done.14.even
  94.3 7.5 %collective-permute-done.15.odd = f32[26,8,256]{2,1,0:T(8,128)S(1)} collective-permute-done((f32[26,8,256]{2,1,0:T(8,128)S(1)}, f32[26,8,256]{2,1,0:T(8,128)S(1)}, u32[]{:S(2)}, u32[]{:S(2)}) %collective-permute-start.15) | collective-permute-done | bytes 213024 | tf_op jit(solution)/shard_map/ppermute | solution.py:452
  101.8 0.0 copy-done.1
  101.8 7.4 %shard_map.51 = (f32[4,64,256]{2,1,0:T(8,128)S(1)}, f32[4,64,256]{2,1,0:T(8,128)S(1)}, f32[4,64,256]{2,1,0:T(8,128)S(1)}, f32[32,128]{1,0:T(8,128)S(1)}) custom-call(s32[5]{0:T(128)S(1)} %convert_element_type.3.flags, f32[4,64,256]{2,1,0:T(8,128)S(1)} %copy-done.1, f32[30,64,256]{2,1,0:T(8,128)S(1)} %get-tuple-element.24.center, ...), custom_call_target="tpu_custom_call" | custom-call | flops 20000000 | bytes 2501024 | tf_op jit(solution)/shard_map/pallas_call | solution.py:435
  109.1 11.6 %all_to_all.10 = f32[32,1,128]{2,1,0:T(1,128)S(1)} all-to-all(f32[32,1,128]{2,1,0:T(1,128)S(1)} %bitcast.16), channel_id=1, replica_groups=mesh['gx_0'=3,'gx_1'=4,'gx_2'=8,'gy_0'=4,'gy_1'=2] {'gx_1','gx_2'}, dimensions={0} | all-to-all | bytes 32768 | tf_op jit(solution)/shard_map/all_to_all | solution.py:495
  120.8 0.1 shard_map.52
  120.8 18.4 %all_to_all.11 = f32[24,1,128]{2,1,0:T(1,128)S(1)} all-to-all(f32[24,1,128]{2,1,0:T(1,128)S(1)} %bitcast.15), channel_id=1, replica_groups=mesh['gx_0'=3,'gx_1'=4,'gx_2'=8,'gy_0'=4,'gy_1'=2] {'gx_0','gy_0','gy_1'}, dimensions={0} | all-to-all | bytes 24576 | tf_op jit(solution)/shard_map/all_to_all | solution.py:497
  139.3 0.0 copy-done.3
  139.3 1.5 %shard_map.53 = (f32[4,64,256]{2,1,0:T(8,128)}, f32[4,64,256]{2,1,0:T(8,128)}, f32[3]{0:T(128)}) custom-call(f32[24,128]{1,0:T(8,128)S(1)} %bitcast.14, f32[4,64,256]{2,1,0:T(8,128)S(1)} %copy-done.1, f32[4,64,256]{2,1,0:T(8,128)S(1)} %copy-done.3, f32[4,64,256]{2,1,0:T(8,128)S(1)} %get-tuple-element.28.y1, f32[4,64,256]{2,1,0:T(8,128)S(1)} %get-tuple-element.29.y2, ...), custom_call_target="tpu_custom_call" | custom-call | flops 2000000 | bytes 251024 | tf_op jit(solution)/shard_map/pallas_call | solution.py:435
  (1 shorter events, 0.0 us)
Async XLA Ops:
  0.8 1.0 copy-start
  1.7 0.9 copy-start.2
  2.7 99.1 %copy-start.1 = (f32[4,64,256]{2,1,0:T(8,128)S(1)}, f32[4,64,256]{2,1,0:T(8,128)}, u32[]{:S(2)}) copy-start(f32[4,64,256]{2,1,0:T(8,128)} %rhs.3) | copy-start | bytes 786436
  3.4 26.9 %collective-permute-start.7 = (f32[2,64,256]{2,1,0:T(8,128)S(1)}, f32[2,64,256]{2,1,0:T(8,128)S(1)}, u32[]{:S(2)}, u32[]{:S(2)}) collective-permute-start(f32[2,64,256]{2,1,0:T(8,128)S(1)} %get-tuple-element.20), channel_id=1, source_target_pairs={{248,56},{249,57},{250,58},{251,59},{252,60},{253,61},{254,62},{25... | collective-permute-start | bytes 393224 | tf_op jit(solution)/shard_map/ppermute | solution.py:452
  8.6 22.3 %collective-permute-start.9 = (f32[2,64,256]{2,1,0:T(8,128)S(1)}, f32[2,64,256]{2,1,0:T(8,128)S(1)}, u32[]{:S(2)}, u32[]{:S(2)}) collective-permute-start(f32[2,64,256]{2,1,0:T(8,128)S(1)} %get-tuple-element.21), channel_id=1, source_target_pairs={{248,192},{249,193},{250,194},{251,195},{252,196},{253,197},{254,1... | collective-permute-start | bytes 393224 | tf_op jit(solution)/shard_map/ppermute | solution.py:452
  10.6 22.3 %collective-permute-start.11 = (f32[2,64,256]{2,1,0:T(8,128)S(1)}, f32[2,64,256]{2,1,0:T(8,128)S(1)}, u32[]{:S(2)}, u32[]{:S(2)}) collective-permute-start(f32[2,64,256]{2,1,0:T(8,128)S(1)} %get-tuple-element.22), channel_id=1, source_target_pairs={{248,184},{249,185},{250,186},{251,187},{252,188},{253,189},{254,1... | collective-permute-start | bytes 393224 | tf_op jit(solution)/shard_map/ppermute | solution.py:452
  11.9 23.6 %collective-permute-start.2 = (f32[3,64,256]{2,1,0:T(8,128)S(1)}, f32[3,64,256]{2,1,0:T(8,128)S(1)}, u32[]{:S(2)}, u32[]{:S(2)}) collective-permute-start(f32[3,64,256]{2,1,0:T(8,128)S(1)} %get-tuple-element.18), channel_id=1, source_target_pairs={{0,16},{1,17},{2,18},{3,19},{4,20},{5,21},{6,22},{7,23},{8,24},{9,... | collective-permute-start | bytes 589832 | tf_op jit(solution)/shard_map/ppermute | solution.py:452
  13.8 20.4 %collective-permute-start.13 = (f32[2,64,256]{2,1,0:T(8,128)S(1)}, f32[2,64,256]{2,1,0:T(8,128)S(1)}, u32[]{:S(2)}, u32[]{:S(2)}) collective-permute-start(f32[2,64,256]{2,1,0:T(8,128)S(1)} %get-tuple-element.23), channel_id=1, source_target_pairs={{248,256},{249,257},{250,258},{251,259},{252,260},{253,261},{254,2... | collective-permute-start | bytes 393224 | tf_op jit(solution)/shard_map/ppermute | solution.py:452
  30.2 35.8 %collective-permute-start.1 = (f32[8,64,256]{2,1,0:T(8,128)S(1)}, f32[8,64,256]{2,1,0:T(8,128)S(1)}, u32[]{:S(2)}, u32[]{:S(2)}) collective-permute-start(f32[8,64,256]{2,1,0:T(8,128)S(1)} %get-tuple-element.17.own), channel_id=1, source_target_pairs={{8,16},{9,17},{10,18},{11,19},{12,20},{13,21},{14,22},{15,23},{16,... | collective-permute-start | bytes 1572872 | tf_op jit(solution)/shard_map/ppermute | solution.py:452
  31.0 35.1 %collective-permute-start = (f32[8,64,256]{2,1,0:T(8,128)S(1)}, f32[8,64,256]{2,1,0:T(8,128)S(1)}, u32[]{:S(2)}, u32[]{:S(2)}) collective-permute-start(f32[8,64,256]{2,1,0:T(8,128)S(1)} %get-tuple-element.17.own), channel_id=1, source_target_pairs={{0,8},{1,9},{2,10},{3,11},{4,12},{5,13},{6,14},{7,15},{8,0},{9,1},... | collective-permute-start | bytes 1572872 | tf_op jit(solution)/shard_map/ppermute | solution.py:452
  32.9 4.6 %collective-permute-start.5 = (f32[3,64,256]{2,1,0:T(8,128)S(1)}, f32[3,64,256]{2,1,0:T(8,128)S(1)}, u32[]{:S(2)}, u32[]{:S(2)}) collective-permute-start(f32[3,64,256]{2,1,0:T(8,128)S(1)} %get-tuple-element.19), channel_id=1, source_target_pairs={{248,200},{249,201},{250,202},{251,203},{252,204},{253,205},{254,2... | collective-permute-start | bytes 589832 | tf_op jit(solution)/shard_map/ppermute | solution.py:452
  34.2 15.4 %collective-permute-start.4 = (f32[3,64,256]{2,1,0:T(8,128)S(1)}, f32[3,64,256]{2,1,0:T(8,128)S(1)}, u32[]{:S(2)}, u32[]{:S(2)}) collective-permute-start(f32[3,64,256]{2,1,0:T(8,128)S(1)} %get-tuple-element.19), channel_id=1, source_target_pairs={{240,256},{241,257},{242,258},{243,259},{244,260},{245,261},{246,2... | collective-permute-start | bytes 589832 | tf_op jit(solution)/shard_map/ppermute | solution.py:452
  35.5 14.8 %collective-permute-start.3 = (f32[3,64,256]{2,1,0:T(8,128)S(1)}, f32[3,64,256]{2,1,0:T(8,128)S(1)}, u32[]{:S(2)}, u32[]{:S(2)}) collective-permute-start(f32[3,64,256]{2,1,0:T(8,128)S(1)} %get-tuple-element.19), channel_id=1, source_target_pairs={{16,32},{17,33},{18,34},{19,35},{20,36},{21,37},{22,38},{23,39},{2... | collective-permute-start | bytes 589832 | tf_op jit(solution)/shard_map/ppermute | solution.py:452
  37.5 14.2 %collective-permute-start.8 = (f32[2,64,256]{2,1,0:T(8,128)S(1)}, f32[2,64,256]{2,1,0:T(8,128)S(1)}, u32[]{:S(2)}, u32[]{:S(2)}) collective-permute-start(f32[2,64,256]{2,1,0:T(8,128)S(1)} %collective-permute-done.7), channel_id=1, source_target_pairs={{56,256},{57,257},{58,258},{59,259},{60,260},{61,261},{62,262},{63... | collective-permute-start | bytes 393224 | tf_op jit(solution)/shard_map/ppermute | solution.py:452
  49.7 16.4 %collective-permute-start.6 = (f32[3,64,256]{2,1,0:T(8,128)S(1)}, f32[3,64,256]{2,1,0:T(8,128)S(1)}, u32[]{:S(2)}, u32[]{:S(2)}) collective-permute-start(f32[3,64,256]{2,1,0:T(8,128)S(1)} %collective-permute-done.5), channel_id=1, source_target_pairs={{200,264},{201,265},{202,266},{203,267},{204,268},{205,269},{206,2... | collective-permute-start | bytes 589832 | tf_op jit(solution)/shard_map/ppermute | solution.py:452
  50.3 12.0 %collective-permute-start.10 = (f32[2,64,256]{2,1,0:T(8,128)S(1)}, f32[2,64,256]{2,1,0:T(8,128)S(1)}, u32[]{:S(2)}, u32[]{:S(2)}) collective-permute-start(f32[2,64,256]{2,1,0:T(8,128)S(1)} %collective-permute-done.9), channel_id=1, source_target_pairs={{192,256},{193,257},{194,258},{195,259},{196,260},{197,261},{198,2... | collective-permute-start | bytes 393224 | tf_op jit(solution)/shard_map/ppermute | solution.py:452
  51.7 14.4 %collective-permute-start.12 = (f32[2,64,256]{2,1,0:T(8,128)S(1)}, f32[2,64,256]{2,1,0:T(8,128)S(1)}, u32[]{:S(2)}, u32[]{:S(2)}) collective-permute-start(f32[2,64,256]{2,1,0:T(8,128)S(1)} %collective-permute-done.11), channel_id=1, source_target_pairs={{184,256},{185,257},{186,258},{187,259},{188,260},{189,261},{190,2... | collective-permute-start | bytes 393224 | tf_op jit(solution)/shard_map/ppermute | solution.py:452
  66.9 72.4 %copy-start.3 = (f32[4,64,256]{2,1,0:T(8,128)S(1)}, f32[4,64,256]{2,1,0:T(8,128)}, u32[]{:S(2)}) copy-start(f32[4,64,256]{2,1,0:T(8,128)} %kappa.1) | copy-start | bytes 786436
  66.9 27.3 %collective-permute-start.14 = (f32[26,8,256]{2,1,0:T(8,128)S(1)}, f32[26,8,256]{2,1,0:T(8,128)S(1)}, u32[]{:S(2)}, u32[]{:S(2)}) collective-permute-start(f32[26,8,256]{2,1,0:T(8,128)S(1)} %get-tuple-element.25), channel_id=1, source_target_pairs={{0,1},{1,0},{2,3},{3,2},{4,5},{5,4},{6,7},{7,6},{8,9},{9,8},{10,11... | collective-permute-start | bytes 638984 | tf_op jit(solution)/shard_map/ppermute | solution.py:452
  92.3 9.4 %collective-permute-start.15 = (f32[26,8,256]{2,1,0:T(8,128)S(1)}, f32[26,8,256]{2,1,0:T(8,128)S(1)}, u32[]{:S(2)}, u32[]{:S(2)}) collective-permute-start(f32[26,8,256]{2,1,0:T(8,128)S(1)} %get-tuple-element.26), channel_id=1, source_target_pairs={{0,7},{1,2},{2,1},{3,4},{4,3},{5,6},{6,5},{7,0},{8,15},{9,10},{10,... | collective-permute-start | bytes 638984 | tf_op jit(solution)/shard_map/ppermute | solution.py:452

commit v5 on v4

--- a/solution.py
+++ b/solution.py
@@ -301,76 +301,96 @@
             lay(by_high, ahead)
 
 
-def powers_kernel(
-    flags, rhs, center, even, odd,
+def powers(v, k, t1, w1, t2, w2, t3, y1s, y2s):
+    def apply(src, dst, shift, count, scaled=None):
+        for i in range(count):
+            c, near = around(src, i + 1)
+            kk = k[i + shift]
+            y = kk * c - near
+            dst[i] = y
+            if scaled is not None:
+                scaled[i] = (1.0 / (kk * kk + 6.0)) * y
+
+    apply(v, t1, 0, 14)
+    apply(t1, y1s, 1, 12, w1)
+    apply(w1, t2, 2, 10)
+    apply(t2, y2s, 3, 8, w2)
+    apply(w2, t3, 4, 6)
+
+
+def folded(a, b):
+    prod = a * b
+    prod = prod[:, :128] + prod[:, 128:]
+    out = [prod[8 * j : 8 * j + 8] for j in range(prod.shape[0] // 8)]
+    while len(out) > 1:
+        out = [out[j] + out[j + 1] for j in range(0, len(out) - 1, 2)] + out[len(out) & ~1 :]
+    return out[0]
+
+
+def reduce_plane(i, cut, rhs, v, k, w1, w2, t3, y1s, y2s, outs, rows):
+    c, near = around(t3, i + 1)
+    y3 = cut(k[i + 5] * c - near)
+    y0, y1, y2, g = rhs(i), cut(y1s[i + 4]), cut(y2s[i + 2]), cut(c)
+    for out, y in zip(outs, (y1, y2, y3)):
+        out[i] = y
+    v0, v1, v2 = cut(v[i + 6]), cut(w1[i + 4]), cut(w2[i + 2])
+    pairs = (
+        (y0, v0), (y1, v0), (y1, v1), (y2, v1), (y2, v2), (g, g),
+        (y0, y0), (y0, y1), (y0, y2), (y1, y1), (y1, y2), (y2, y2),
+    )
+    for d, (a, b) in enumerate(pairs):
+        rows[8 * d : 8 * d + 8] += folded(a, b)
+
+
+def inner_kernel(rhs, center, y1_out, y2_out, y3_out, rows, v, k, t1, w1, t2, w2, t3, y1s, y2s):
+    for j in range(16):
+        v[j] = center[j]
+    for j in range(14):
+        k[j] = 6.0 + center[j + 16]
+
+    powers(v, k, t1, w1, t2, w2, t3, y1s, y2s)
+    rows[...] = jnp.zeros_like(rows)
+
+    for i in range(4):
+        reduce_plane(
+            i, lambda x: x[8:56], lambda p: rhs[p, 8:56], v, k, w1, w2, t3, y1s, y2s,
+            (y1_out, y2_out, y3_out), rows,
+        )
+
+
+def outer_kernel(
+    flags, rhs, center, even, odd, inner_rows,
     y1_out, y2_out, y3_out, sums_out,
     v, k, t1, w1, t2, w2, t3, y1s, y2s, rows,
 ):
-    even_side = pl.multiple_of((1 - flags[2]) * 72, 8)
-    odd_side = pl.multiple_of(flags[2] * 72, 8)
+    even_side = pl.multiple_of((1 - flags[2]) * 40, 8)
+    odd_side = pl.multiple_of(flags[2] * 40, 8)
     for j in range(30):
         ref, at, base = (v, j, 0.0) if j < 16 else (k, j - 16, 6.0)
         put = lambda plane: plane if ref is v else base + plane
-        ref[at, 8:72] = put(center[j])
+        ref[at, 8:24] = put(center[j, 0:16])
+        ref[at, 24:40] = put(center[j, 48:64])
         if j in WIDE:
             ref[at, pl.ds(even_side, 8)] = put(even[WIDE.index(j)])
             ref[at, pl.ds(odd_side, 8)] = put(odd[WIDE.index(j)])
         else:
             ref[at, 0:8] = jnp.zeros((8, ref.shape[2]), F32)
-            ref[at, 72:80] = jnp.zeros((8, ref.shape[2]), F32)
-
-    def apply(src, dst, shift, count):
-        @pl.loop(0, count)
-        def _(i):
-            c, near = around(src, i + 1)
-            dst[i] = k[i + shift] * c - near
-
-    def apply_scaled(src, plain, scaled, shift, count):
-        @pl.loop(0, count)
-        def _(i):
-            c, near = around(src, i + 1)
-            kk = k[i + shift]
-            y = kk * c - near
-            plain[i] = y
-            scaled[i] = (1.0 / (kk * kk + 6.0)) * y
-
-    apply(v, t1, 0, 14)
-    apply_scaled(t1, y1s, w1, 1, 12)
-    apply(w1, t2, 2, 10)
-    apply_scaled(t2, y2s, w2, 3, 8)
-    apply(w2, t3, 4, 6)
-
-    def folded(a, b):
-        prod = a * b
-        prod = prod[:, :128] + prod[:, 128:]
-        out = [prod[8 * j : 8 * j + 8] for j in range(8)]
-        while len(out) > 1:
-            out = [out[2 * j] + out[2 * j + 1] for j in range(len(out) // 2)]
-        return out[0]
-
-    rows[...] = jnp.zeros_like(rows)
-
-    @pl.loop(0, 4)
-    def _(i):
-        c, near = around(t3, i + 1)
-        y3_out[i] = (k[i + 5] * c - near)[8:72]
-        y0 = rhs[i]
-        y1 = y1s[i + 4, 8:72]
-        y2 = y2s[i + 2, 8:72]
-        y1_out[i] = y1
-        y2_out[i] = y2
-        v0, v1, v2, g = v[i + 6, 8:72], w1[i + 4, 8:72], w2[i + 2, 8:72], c[8:72]
-        pairs = (
-            (y0, v0), (y1, v0), (y1, v1), (y2, v1), (y2, v2), (g, g),
-            (y0, y0), (y0, y1), (y0, y2), (y1, y1), (y1, y2), (y2, y2),
+            ref[at, 40:48] = jnp.zeros((8, ref.shape[2]), F32)
+
+    powers(v, k, t1, w1, t2, w2, t3, y1s, y2s)
+    rows[...] = inner_rows[...]
+    ends = lambda x, a, b: jnp.concatenate([x[a : a + 8], x[b : b + 8]], axis=0)
+
+    for i in range(4):
+        reduce_plane(
+            i, lambda x: ends(x, 8, 32), lambda p: ends(rhs[p], 0, 56), v, k, w1, w2, t3, y1s, y2s,
+            (y1_out, y2_out, y3_out), rows,
         )
-        for d, (a, b) in enumerate(pairs):
-            rows[8 * d : 8 * d + 8] += folded(a, b)
-
-    terms = [(rows[pl.ds(s, 16, stride=8), :], None) for s in range(8)]
-    hi, lo = terms[0][0], jnp.zeros((16, 128), F32)
-    for s in range(1, 8):
-        hi, e = two_sum(hi, terms[s][0])
+
+    terms = [rows[pl.ds(s, 16, stride=8), :] for s in range(8)]
+    hi, lo = terms[0], jnp.zeros((16, 128), F32)
+    for term in terms[1:]:
+        hi, e = two_sum(hi, term)
         lo = lo + e
     for shift in (64, 32, 16, 8, 4, 2, 1):
         hi, e = two_sum(hi, pltpu.roll(hi, shift, 1))
@@ -398,7 +418,7 @@
     out[...] = jnp.broadcast_to(added(parts[...])[0:1], out.shape)
 
 
-def finish_kernel(cells, parts, rhs, kappa, y1, y2, y3, x_out, r_out, rms_out):
+def finish_kernel(cells, parts, rhs, kappa, i1, i2, i3, o1, o2, o3, x_out, r_out, rms_out):
     total = added(parts[...])[0:1]
     lane = lanes_of((1, 128))
 
@@ -412,14 +432,16 @@
     c, rr = coefficients(mu, lambda a, b: table[place[a, b]])
     for i in range(3):
         rms_out[i] = jnp.sqrt(rr[i] / F32(cells))[0, 0]
-    wide = [jnp.broadcast_to(a, rhs.shape[1:]) for a in c]
-
-    @pl.loop(0, 4)
-    def _(i):
-        a0, a1, a2 = rhs[i], y1[i], y2[i]
-        kk = 6.0 + kappa[i]
-        x_out[i] = (1.0 / (kk * kk + 6.0)) * (wide[0] * a0 + wide[1] * a1 + wide[2] * a2)
-        r_out[i] = a0 - (wide[0] * a1 + wide[1] * a2 + wide[2] * y3[i])
+    for i in range(4):
+        for at, size, (y1, y2, y3), own in (
+            (8, 48, (i1, i2, i3), 0), (0, 8, (o1, o2, o3), 0), (56, 8, (o1, o2, o3), 8)
+        ):
+            rows = slice(at, at + size)
+            take = lambda ref: ref[i, own : own + size]
+            a0, a1, a2, a3 = rhs[i, rows], take(y1), take(y2), take(y3)
+            kk = 6.0 + kappa[i, rows]
+            x_out[i, rows] = (1.0 / (kk * kk + 6.0)) * (c[0] * a0 + c[1] * a1 + c[2] * a2)
+            r_out[i, rows] = a0 - (c[0] * a1 + c[1] * a2 + c[2] * a3)
 
 
 def kernel(fn, outs, scratch=(), flops=0, flagged=False, scalars=False, fetched=0, limit=24):
@@ -482,22 +504,28 @@
     center, to_even, to_odd = extended(flags, right_side, kappa_sq)
     even = send(to_even, GY_EVEN)
     odd = send(to_odd, GY_ODD)
-    block, wide = right_side.shape, (80, 256)
+    block, lanes = right_side.shape, right_side.shape[2]
     n_plane, n_column = lax.axis_size(PLANE), lax.axis_size(COLUMN)
     counts = (16, 14, 14, 12, 10, 8, 6, 12, 8)
-    y1, y2, y3, sums = kernel(
-        powers_kernel,
-        [block] * 3 + [(n_plane, 128)],
-        [(n, *wide) for n in counts] + [(128, 128)],
+    *inner, rows = kernel(
+        inner_kernel,
+        [(4, 48, lanes)] * 3 + [(128, 128)],
+        [(n, 64, lanes) for n in counts],
         flops=20_000_000,
+    )(right_side, center)
+    *outer, sums = kernel(
+        outer_kernel,
+        [(4, 16, lanes)] * 3 + [(n_plane, 128)],
+        [(n, 48, lanes) for n in counts] + [(128, 128)],
+        flops=12_000_000,
         flagged=True,
-    )(flags, right_side, center, even, odd)
+    )(flags, right_side, center, even, odd, rows)
     sums = lax.all_to_all(sums.reshape(n_plane, 1, 128), PLANE, 0, 0).reshape(n_plane, 128)
     (sums,) = kernel(add_kernel, [(n_column, 128)], flops=20000)(sums)
     sums = lax.all_to_all(sums.reshape(n_column, 1, 128), COLUMN, 0, 0).reshape(n_column, 128)
     return kernel(
         functools.partial(finish_kernel, cells), [block, block, (3,)], flops=2_000_000, scalars=True
-    )(sums, right_side, kappa_sq, y1, y2, y3)
+    )(sums, right_side, kappa_sq, *inner, *outer)
 
 
 def solution(mesh):

time: 141 us -> 136 us (0.965)
  Pallas kernels: 10.5 us -> 7.74 us
  waiting for transfers between devices: 32.8 us -> 30.5 us
    pallas_call x5 -> x6, Pallas kernels: 10.5 us -> 7.74 us  [call(): pl.pallas_call(fn, out_shape=[jax.ShapeDtypeStruct(s, F32) for s in outs]...]
    ppermute x16, waiting for transfers between devices: 32.8 us -> 30.5 us  [send(): return lax.ppermute(x, ALL, pairs)]
  transfers between devices with their start and end apart: 16 -> 16, of which waited for: 5 -> 5; matrix products, arithmetic and copies ran while one was open for 0% -> 0% of each run, Pallas kernels for 0% -> 2%
where the time goes in v5:
time: 136 us
  starting transfers between devices  64.4 us (47%)
  waiting for transfers between devices  30.5 us (22%)
  blocking collectives  30.1 us (22%)
  Pallas kernels  7.74 us (6%)
  local copies, waits for them, and re-layouts  2.02 us (1%)
    ppermute x16, starting transfers between devices, send(): return lax.ppermute(x, ALL, pairs)  64.4 us
    ppermute x16, waiting for transfers between devices, send(): return lax.ppermute(x, ALL, pairs)  30.5 us
    all_to_all x1, blocking collectives, steps(): lax.all_to_all(sums.reshape(n_column, 1, 128), COLUMN, 0, 0)  18.4 us
    all_to_all x1, blocking collectives, steps(): lax.all_to_all(sums.reshape(n_plane, 1, 128), PLANE, 0, 0)  11.6 us
    pallas_call x6, Pallas kernels, call(): pl.pallas_call(fn, out_shape=[jax.ShapeDtypeStruct(s, F32) for s in outs]...  7.74 us
  transfers between devices with their start and end apart: 16, of which 5 were waited for; matrix products, arithmetic and copies ran while one was open for 0% of the time, Pallas kernels for 2%

profile of v5, /device:TPU:1, one launch (start us, length us, event | category | flops | bytes accessed | tf_op | source)
XLA Modules:
  0.0 135.7 jit_solution(11828602809178638119)
XLA Ops:
  0.7 0.1 stack.23
  0.8 0.0 copy-start
  0.8 0.9 copy-done
  1.7 0.0 copy-start.2
  1.7 0.9 copy-done.2
  2.7 0.0 copy-start.1
  2.7 0.7 shard_map.49
  3.4 5.2 %collective-permute-start.7 = (f32[2,64,256]{2,1,0:T(8,128)S(1)}, f32[2,64,256]{2,1,0:T(8,128)S(1)}, u32[]{:S(2)}, u32[]{:S(2)}) collective-permute-start(f32[2,64,256]{2,1,0:T(8,128)S(1)} %get-tuple-element.24), channel_id=1, source_target_pairs={{248,56},{249,57},{250,58},{251,59},{252,60},{253,61},{254,62},{25... | collective-permute-start | bytes 393224 | tf_op jit(solution)/shard_map/ppermute | solution.py:474
  8.6 2.0 %collective-permute-start.9 = (f32[2,64,256]{2,1,0:T(8,128)S(1)}, f32[2,64,256]{2,1,0:T(8,128)S(1)}, u32[]{:S(2)}, u32[]{:S(2)}) collective-permute-start(f32[2,64,256]{2,1,0:T(8,128)S(1)} %get-tuple-element.25), channel_id=1, source_target_pairs={{248,192},{249,193},{250,194},{251,195},{252,196},{253,197},{254,1... | collective-permute-start | bytes 393224 | tf_op jit(solution)/shard_map/ppermute | solution.py:474
  10.6 1.3 collective-permute-start.11
  11.9 1.9 %collective-permute-start.2 = (f32[3,64,256]{2,1,0:T(8,128)S(1)}, f32[3,64,256]{2,1,0:T(8,128)S(1)}, u32[]{:S(2)}, u32[]{:S(2)}) collective-permute-start(f32[3,64,256]{2,1,0:T(8,128)S(1)} %get-tuple-element.22), channel_id=1, source_target_pairs={{0,16},{1,17},{2,18},{3,19},{4,20},{5,21},{6,22},{7,23},{8,24},{9,... | collective-permute-start | bytes 589832 | tf_op jit(solution)/shard_map/ppermute | solution.py:474
  13.8 16.4 %collective-permute-start.13 = (f32[2,64,256]{2,1,0:T(8,128)S(1)}, f32[2,64,256]{2,1,0:T(8,128)S(1)}, u32[]{:S(2)}, u32[]{:S(2)}) collective-permute-start(f32[2,64,256]{2,1,0:T(8,128)S(1)} %get-tuple-element.27), channel_id=1, source_target_pairs={{248,256},{249,257},{250,258},{251,259},{252,260},{253,261},{254,2... | collective-permute-start | bytes 393224 | tf_op jit(solution)/shard_map/ppermute | solution.py:474
  30.2 0.0 collective-permute-done.7
  30.2 0.7 collective-permute-start.1
  31.0 0.0 collective-permute-done.9
  31.0 1.9 %collective-permute-start = (f32[8,64,256]{2,1,0:T(8,128)S(1)}, f32[8,64,256]{2,1,0:T(8,128)S(1)}, u32[]{:S(2)}, u32[]{:S(2)}) collective-permute-start(f32[8,64,256]{2,1,0:T(8,128)S(1)} %get-tuple-element.21.own), channel_id=1, source_target_pairs={{0,8},{1,9},{2,10},{3,11},{4,12},{5,13},{6,14},{7,15},{8,0},{9,1},... | collective-permute-start | bytes 1572872 | tf_op jit(solution)/shard_map/ppermute | solution.py:474
  32.9 0.0 collective-permute-done.11
  32.9 1.3 collective-permute-start.5
  34.2 0.0 collective-permute-done.13.d3
  34.2 1.3 collective-permute-start.4
  35.5 0.0 collective-permute-done.2.low2
  35.5 0.7 collective-permute-start.3
  36.2 1.3 collective-permute-done.5
  37.5 1.3 collective-permute-start.8
  38.8 10.9 %collective-permute-done.4.across = f32[3,64,256]{2,1,0:T(8,128)S(1)} collective-permute-done((f32[3,64,256]{2,1,0:T(8,128)S(1)}, f32[3,64,256]{2,1,0:T(8,128)S(1)}, u32[]{:S(2)}, u32[]{:S(2)}) %collective-permute-start.4) | collective-permute-done | bytes 196640 | tf_op jit(solution)/shard_map/ppermute | solution.py:474
  49.7 0.7 collective-permute-start.6
  50.3 0.0 collective-permute-done.3.high2
  50.3 1.3 collective-permute-start.10
  51.6 0.0 collective-permute-done.8.d0
  51.7 1.3 collective-permute-start.12
  53.0 9.4 %collective-permute-done.10.d1 = f32[2,64,256]{2,1,0:T(8,128)S(1)} collective-permute-done((f32[2,64,256]{2,1,0:T(8,128)S(1)}, f32[2,64,256]{2,1,0:T(8,128)S(1)}, u32[]{:S(2)}, u32[]{:S(2)}) %collective-permute-start.10) | collective-permute-done | bytes 131104 | tf_op jit(solution)/shard_map/ppermute | solution.py:474
  62.4 3.7 %collective-permute-done.12.d2 = f32[2,64,256]{2,1,0:T(8,128)S(1)} collective-permute-done((f32[2,64,256]{2,1,0:T(8,128)S(1)}, f32[2,64,256]{2,1,0:T(8,128)S(1)}, u32[]{:S(2)}, u32[]{:S(2)}) %collective-permute-start.12) | collective-permute-done | bytes 131104 | tf_op jit(solution)/shard_map/ppermute | solution.py:474
  66.1 0.0 collective-permute-done.6.ahead
  66.1 0.0 collective-permute-done.1.odd
  66.1 0.0 collective-permute-done.even
  66.1 0.8 shard_map.50
  66.9 25.3 %collective-permute-start.14 = (f32[26,8,256]{2,1,0:T(8,128)S(1)}, f32[26,8,256]{2,1,0:T(8,128)S(1)}, u32[]{:S(2)}, u32[]{:S(2)}) collective-permute-start(f32[26,8,256]{2,1,0:T(8,128)S(1)} %get-tuple-element.29), channel_id=1, source_target_pairs={{0,1},{1,0},{2,3},{3,2},{4,5},{5,4},{6,7},{7,6},{8,9},{9,8},{10,11... | collective-permute-start | bytes 638984 | tf_op jit(solution)/shard_map/ppermute | solution.py:474
  92.2 1.9 %collective-permute-start.15 = (f32[26,8,256]{2,1,0:T(8,128)S(1)}, f32[26,8,256]{2,1,0:T(8,128)S(1)}, u32[]{:S(2)}, u32[]{:S(2)}) collective-permute-start(f32[26,8,256]{2,1,0:T(8,128)S(1)} %get-tuple-element.30), channel_id=1, source_target_pairs={{0,7},{1,2},{2,1},{3,4},{4,3},{5,6},{6,5},{7,0},{8,15},{9,10},{10,... | collective-permute-start | bytes 638984 | tf_op jit(solution)/shard_map/ppermute | solution.py:474
  94.1 0.0 copy-done.1
  94.1 2.3 %shard_map.51 = (f32[4,48,256]{2,1,0:T(8,128)S(1)}, f32[4,48,256]{2,1,0:T(8,128)S(1)}, f32[4,48,256]{2,1,0:T(8,128)S(1)}, f32[128,128]{1,0:T(8,128)S(1)}) custom-call(f32[4,64,256]{2,1,0:T(8,128)S(1)} %copy-done.1, f32[30,64,256]{2,1,0:T(8,128)S(1)} %get-tuple-element.28.center), custom_call_target="tpu_custom_call" | custom-call | flops 20000000 | bytes 2501024 | tf_op jit(solution)/shard_map/pallas_call | solution.py:457
  96.4 0.0 copy-start.3
  96.4 0.0 collective-permute-done.14.even
  96.4 5.2 %collective-permute-done.15.odd = f32[26,8,256]{2,1,0:T(8,128)S(1)} collective-permute-done((f32[26,8,256]{2,1,0:T(8,128)S(1)}, f32[26,8,256]{2,1,0:T(8,128)S(1)}, u32[]{:S(2)}, u32[]{:S(2)}) %collective-permute-start.15) | collective-permute-done | bytes 213024 | tf_op jit(solution)/shard_map/ppermute | solution.py:474
  101.6 2.4 %shard_map.52 = (f32[4,16,256]{2,1,0:T(8,128)S(1)}, f32[4,16,256]{2,1,0:T(8,128)S(1)}, f32[4,16,256]{2,1,0:T(8,128)S(1)}, f32[32,128]{1,0:T(8,128)S(1)}) custom-call(s32[5]{0:T(128)S(1)} %convert_element_type.3.flags, f32[4,64,256]{2,1,0:T(8,128)S(1)} %copy-done.1, f32[30,64,256]{2,1,0:T(8,128)S(1)} %get-tuple-element.28.center, ...), custom_call_target="tpu_custom_call" | custom-call | flops 12000000 | bytes 1501024 | tf_op jit(solution)/shard_map/pallas_call | solution.py:457
  104.0 11.6 %all_to_all.10 = f32[32,1,128]{2,1,0:T(1,128)S(1)} all-to-all(f32[32,1,128]{2,1,0:T(1,128)S(1)} %bitcast.16), channel_id=1, replica_groups=mesh['gx_0'=3,'gx_1'=4,'gx_2'=8,'gy_0'=4,'gy_1'=2] {'gx_1','gx_2'}, dimensions={0} | all-to-all | bytes 32768 | tf_op jit(solution)/shard_map/all_to_all | solution.py:523
  115.7 0.1 shard_map.53
  115.8 18.4 %all_to_all.11 = f32[24,1,128]{2,1,0:T(1,128)S(1)} all-to-all(f32[24,1,128]{2,1,0:T(1,128)S(1)} %bitcast.15), channel_id=1, replica_groups=mesh['gx_0'=3,'gx_1'=4,'gx_2'=8,'gy_0'=4,'gy_1'=2] {'gx_0','gy_0','gy_1'}, dimensions={0} | all-to-all | bytes 24576 | tf_op jit(solution)/shard_map/all_to_all | solution.py:525
  134.2 0.0 copy-done.3
  134.2 1.5 %shard_map.54 = (f32[4,64,256]{2,1,0:T(8,128)}, f32[4,64,256]{2,1,0:T(8,128)}, f32[3]{0:T(128)}) custom-call(f32[24,128]{1,0:T(8,128)S(1)} %bitcast.14, f32[4,64,256]{2,1,0:T(8,128)S(1)} %copy-done.1, f32[4,64,256]{2,1,0:T(8,128)S(1)} %copy-done.3, f32[4,48,256]{2,1,0:T(8,128)S(1)} %get-tuple-element.33.i1, f32[4,48,256]{2,1,0:T(8,128)S(1)} %get-tuple-element.34.i2, ...), custom_call_target="tpu_custom_call" | custom-call | flops 2000000 | bytes 251024 | tf_op jit(solution)/shard_map/pallas_call | solution.py:457
  (1 shorter events, 0.0 us)
Async XLA Ops:
  0.8 1.0 copy-start
  1.7 0.9 copy-start.2
  2.7 91.4 %copy-start.1 = (f32[4,64,256]{2,1,0:T(8,128)S(1)}, f32[4,64,256]{2,1,0:T(8,128)}, u32[]{:S(2)}) copy-start(f32[4,64,256]{2,1,0:T(8,128)} %rhs.5) | copy-start | bytes 786436
  3.4 26.9 %collective-permute-start.7 = (f32[2,64,256]{2,1,0:T(8,128)S(1)}, f32[2,64,256]{2,1,0:T(8,128)S(1)}, u32[]{:S(2)}, u32[]{:S(2)}) collective-permute-start(f32[2,64,256]{2,1,0:T(8,128)S(1)} %get-tuple-element.24), channel_id=1, source_target_pairs={{248,56},{249,57},{250,58},{251,59},{252,60},{253,61},{254,62},{25... | collective-permute-start | bytes 393224 | tf_op jit(solution)/shard_map/ppermute | solution.py:474
  8.6 22.3 %collective-permute-start.9 = (f32[2,64,256]{2,1,0:T(8,128)S(1)}, f32[2,64,256]{2,1,0:T(8,128)S(1)}, u32[]{:S(2)}, u32[]{:S(2)}) collective-permute-start(f32[2,64,256]{2,1,0:T(8,128)S(1)} %get-tuple-element.25), channel_id=1, source_target_pairs={{248,192},{249,193},{250,194},{251,195},{252,196},{253,197},{254,1... | collective-permute-start | bytes 393224 | tf_op jit(solution)/shard_map/ppermute | solution.py:474
  10.6 22.3 %collective-permute-start.11 = (f32[2,64,256]{2,1,0:T(8,128)S(1)}, f32[2,64,256]{2,1,0:T(8,128)S(1)}, u32[]{:S(2)}, u32[]{:S(2)}) collective-permute-start(f32[2,64,256]{2,1,0:T(8,128)S(1)} %get-tuple-element.26), channel_id=1, source_target_pairs={{248,184},{249,185},{250,186},{251,187},{252,188},{253,189},{254,1... | collective-permute-start | bytes 393224 | tf_op jit(solution)/shard_map/ppermute | solution.py:474
  11.9 23.6 %collective-permute-start.2 = (f32[3,64,256]{2,1,0:T(8,128)S(1)}, f32[3,64,256]{2,1,0:T(8,128)S(1)}, u32[]{:S(2)}, u32[]{:S(2)}) collective-permute-start(f32[3,64,256]{2,1,0:T(8,128)S(1)} %get-tuple-element.22), channel_id=1, source_target_pairs={{0,16},{1,17},{2,18},{3,19},{4,20},{5,21},{6,22},{7,23},{8,24},{9,... | collective-permute-start | bytes 589832 | tf_op jit(solution)/shard_map/ppermute | solution.py:474
  13.8 20.4 %collective-permute-start.13 = (f32[2,64,256]{2,1,0:T(8,128)S(1)}, f32[2,64,256]{2,1,0:T(8,128)S(1)}, u32[]{:S(2)}, u32[]{:S(2)}) collective-permute-start(f32[2,64,256]{2,1,0:T(8,128)S(1)} %get-tuple-element.27), channel_id=1, source_target_pairs={{248,256},{249,257},{250,258},{251,259},{252,260},{253,261},{254,2... | collective-permute-start | bytes 393224 | tf_op jit(solution)/shard_map/ppermute | solution.py:474
  30.2 35.8 %collective-permute-start.1 = (f32[8,64,256]{2,1,0:T(8,128)S(1)}, f32[8,64,256]{2,1,0:T(8,128)S(1)}, u32[]{:S(2)}, u32[]{:S(2)}) collective-permute-start(f32[8,64,256]{2,1,0:T(8,128)S(1)} %get-tuple-element.21.own), channel_id=1, source_target_pairs={{8,16},{9,17},{10,18},{11,19},{12,20},{13,21},{14,22},{15,23},{16,... | collective-permute-start | bytes 1572872 | tf_op jit(solution)/shard_map/ppermute | solution.py:474
  31.0 35.1 %collective-permute-start = (f32[8,64,256]{2,1,0:T(8,128)S(1)}, f32[8,64,256]{2,1,0:T(8,128)S(1)}, u32[]{:S(2)}, u32[]{:S(2)}) collective-permute-start(f32[8,64,256]{2,1,0:T(8,128)S(1)} %get-tuple-element.21.own), channel_id=1, source_target_pairs={{0,8},{1,9},{2,10},{3,11},{4,12},{5,13},{6,14},{7,15},{8,0},{9,1},... | collective-permute-start | bytes 1572872 | tf_op jit(solution)/shard_map/ppermute | solution.py:474
  32.9 4.6 %collective-permute-start.5 = (f32[3,64,256]{2,1,0:T(8,128)S(1)}, f32[3,64,256]{2,1,0:T(8,128)S(1)}, u32[]{:S(2)}, u32[]{:S(2)}) collective-permute-start(f32[3,64,256]{2,1,0:T(8,128)S(1)} %get-tuple-element.23), channel_id=1, source_target_pairs={{248,200},{249,201},{250,202},{251,203},{252,204},{253,205},{254,2... | collective-permute-start | bytes 589832 | tf_op jit(solution)/shard_map/ppermute | solution.py:474
  34.2 15.4 %collective-permute-start.4 = (f32[3,64,256]{2,1,0:T(8,128)S(1)}, f32[3,64,256]{2,1,0:T(8,128)S(1)}, u32[]{:S(2)}, u32[]{:S(2)}) collective-permute-start(f32[3,64,256]{2,1,0:T(8,128)S(1)} %get-tuple-element.23), channel_id=1, source_target_pairs={{240,256},{241,257},{242,258},{243,259},{244,260},{245,261},{246,2... | collective-permute-start | bytes 589832 | tf_op jit(solution)/shard_map/ppermute | solution.py:474
  35.5 14.8 %collective-permute-start.3 = (f32[3,64,256]{2,1,0:T(8,128)S(1)}, f32[3,64,256]{2,1,0:T(8,128)S(1)}, u32[]{:S(2)}, u32[]{:S(2)}) collective-permute-start(f32[3,64,256]{2,1,0:T(8,128)S(1)} %get-tuple-element.23), channel_id=1, source_target_pairs={{16,32},{17,33},{18,34},{19,35},{20,36},{21,37},{22,38},{23,39},{2... | collective-permute-start | bytes 589832 | tf_op jit(solution)/shard_map/ppermute | solution.py:474
  37.5 14.2 %collective-permute-start.8 = (f32[2,64,256]{2,1,0:T(8,128)S(1)}, f32[2,64,256]{2,1,0:T(8,128)S(1)}, u32[]{:S(2)}, u32[]{:S(2)}) collective-permute-start(f32[2,64,256]{2,1,0:T(8,128)S(1)} %collective-permute-done.7), channel_id=1, source_target_pairs={{56,256},{57,257},{58,258},{59,259},{60,260},{61,261},{62,262},{63... | collective-permute-start | bytes 393224 | tf_op jit(solution)/shard_map/ppermute | solution.py:474
  49.7 16.4 %collective-permute-start.6 = (f32[3,64,256]{2,1,0:T(8,128)S(1)}, f32[3,64,256]{2,1,0:T(8,128)S(1)}, u32[]{:S(2)}, u32[]{:S(2)}) collective-permute-start(f32[3,64,256]{2,1,0:T(8,128)S(1)} %collective-permute-done.5), channel_id=1, source_target_pairs={{200,264},{201,265},{202,266},{203,267},{204,268},{205,269},{206,2... | collective-permute-start | bytes 589832 | tf_op jit(solution)/shard_map/ppermute | solution.py:474
  50.3 12.0 %collective-permute-start.10 = (f32[2,64,256]{2,1,0:T(8,128)S(1)}, f32[2,64,256]{2,1,0:T(8,128)S(1)}, u32[]{:S(2)}, u32[]{:S(2)}) collective-permute-start(f32[2,64,256]{2,1,0:T(8,128)S(1)} %collective-permute-done.9), channel_id=1, source_target_pairs={{192,256},{193,257},{194,258},{195,259},{196,260},{197,261},{198,2... | collective-permute-start | bytes 393224 | tf_op jit(solution)/shard_map/ppermute | solution.py:474
  51.7 14.4 %collective-permute-start.12 = (f32[2,64,256]{2,1,0:T(8,128)S(1)}, f32[2,64,256]{2,1,0:T(8,128)S(1)}, u32[]{:S(2)}, u32[]{:S(2)}) collective-permute-start(f32[2,64,256]{2,1,0:T(8,128)S(1)} %collective-permute-done.11), channel_id=1, source_target_pairs={{184,256},{185,257},{186,258},{187,259},{188,260},{189,261},{190,2... | collective-permute-start | bytes 393224 | tf_op jit(solution)/shard_map/ppermute | solution.py:474
  66.9 29.5 %collective-permute-start.14 = (f32[26,8,256]{2,1,0:T(8,128)S(1)}, f32[26,8,256]{2,1,0:T(8,128)S(1)}, u32[]{:S(2)}, u32[]{:S(2)}) collective-permute-start(f32[26,8,256]{2,1,0:T(8,128)S(1)} %get-tuple-element.29), channel_id=1, source_target_pairs={{0,1},{1,0},{2,3},{3,2},{4,5},{5,4},{6,7},{7,6},{8,9},{9,8},{10,11... | collective-permute-start | bytes 638984 | tf_op jit(solution)/shard_map/ppermute | solution.py:474
  92.2 9.4 %collective-permute-start.15 = (f32[26,8,256]{2,1,0:T(8,128)S(1)}, f32[26,8,256]{2,1,0:T(8,128)S(1)}, u32[]{:S(2)}, u32[]{:S(2)}) collective-permute-start(f32[26,8,256]{2,1,0:T(8,128)S(1)} %get-tuple-element.30), channel_id=1, source_target_pairs={{0,7},{1,2},{2,1},{3,4},{4,3},{5,6},{6,5},{7,0},{8,15},{9,10},{10,... | collective-permute-start | bytes 638984 | tf_op jit(solution)/shard_map/ppermute | solution.py:474
  96.4 37.8 %copy-start.3 = (f32[4,64,256]{2,1,0:T(8,128)S(1)}, f32[4,64,256]{2,1,0:T(8,128)}, u32[]{:S(2)}) copy-start(f32[4,64,256]{2,1,0:T(8,128)} %kappa.1) | copy-start | bytes 786436

commit v6 on v5

--- a/solution.py
+++ b/solution.py
@@ -78,10 +78,10 @@
         over_gx([(NEAR_LAST(k), FIRST(k + 1)) for k in SEGS] + [(NEAR_FIRST(k), LAST(k - 1)) for k in SEGS]),
     ),
     (
-        over_gx([(LAST(k), corner(k, XS - 1, 1)) for k in SEGS] + [(FIRST(k), corner(k, 0, YS - 2)) for k in SEGS]),
+        over_gx([(LAST(k), corner(k, 1, YS - 1)) for k in SEGS] + [(FIRST(k), corner(k, 2, 0)) for k in SEGS]),
         over_gx(
-            [(corner(k, XS - 1, 1), FIRST(k + 1) + 1) for k in SEGS]
-            + [(corner(k, 0, YS - 2), LAST(k - 1) - 1) for k in SEGS]
+            [(corner(k, 1, YS - 1), FIRST(k + 1) + 1) for k in SEGS]
+            + [(corner(k, 2, 0), LAST(k - 1) - 1) for k in SEGS]
         ),
     ),
 ]
@@ -100,7 +100,10 @@
     + [("nn", 2)]
 )
 
-WIDE = tuple(j for j in range(len(PLANES)) if j not in (0, 15, 16, 29))
+WHOLE = (5, 6, 7, 8, 9, 10) + (21, 22, 23, 24)
+HALVES = ((1, 2), (3, 4), (11, 12), (13, 14), (17, 18), (19, 20), (25, 26), (27, 28))
+TILES = len(WHOLE) + len(HALVES)
+NONE = tuple(j for j in range(len(PLANES)) if j not in WHOLE + sum(HALVES, ()))
 
 
 def two_sum(a, b):
@@ -251,17 +254,11 @@
 def gather_kernel(
     flags, own, even, odd, low2, high2, across, ahead, d0, d1, d2, d3, center, to_even, to_odd
 ):
-    even_side = pl.multiple_of((1 - flags[2]) * 56, 8)
-    odd_side = pl.multiple_of(flags[2] * 56, 8)
-
     def lay(part, ref):
         for j, (name, at) in enumerate(PLANES):
             if name == part:
                 src, i = ((d0, d1, d2, d3)[at // 2], at % 2) if ref is None else (ref, at)
                 center[j] = src[i]
-                if j in WIDE:
-                    to_even[WIDE.index(j)] = src[i, pl.ds(even_side, 8)]
-                    to_odd[WIDE.index(j)] = src[i, pl.ds(odd_side, 8)]
 
     def when(*conditions):
         here = functools.reduce(lambda a, b: a & b, [flags[i] == value for i, value in conditions])
@@ -299,6 +296,19 @@
         @when((1, value), (3, 0), (4, 1))
         def _():
             lay(by_high, ahead)
+
+    upper = lax.broadcasted_iota(jnp.int32, (8, center.shape[2]), 0) < 4
+    for out, last in ((to_even, flags[2] == 0), (to_odd, flags[2] == 1)):
+        columns = pl.ds(pl.multiple_of(jnp.where(last, 56, 0), 8), 8)
+        for t, j in enumerate(WHOLE):
+            out[t] = center[j, columns]
+        for t, (a, b) in enumerate(HALVES):
+            a, b = center[a, columns], center[b, columns]
+            out[len(WHOLE) + t] = jnp.where(
+                last,
+                jnp.where(upper, pltpu.roll(a, 4, 0), b),
+                jnp.where(upper, a, pltpu.roll(b, 4, 0)),
+            )
 
 
 def powers(v, k, t1, w1, t2, w2, t3, y1s, y2s):
@@ -363,19 +373,27 @@
     y1_out, y2_out, y3_out, sums_out,
     v, k, t1, w1, t2, w2, t3, y1s, y2s, rows,
 ):
-    even_side = pl.multiple_of((1 - flags[2]) * 40, 8)
-    odd_side = pl.multiple_of(flags[2] * 40, 8)
+    def at(j):
+        return (v, j, 0.0) if j < 16 else (k, j - 16, 6.0)
+
     for j in range(30):
-        ref, at, base = (v, j, 0.0) if j < 16 else (k, j - 16, 6.0)
-        put = lambda plane: plane if ref is v else base + plane
-        ref[at, 8:24] = put(center[j, 0:16])
-        ref[at, 24:40] = put(center[j, 48:64])
-        if j in WIDE:
-            ref[at, pl.ds(even_side, 8)] = put(even[WIDE.index(j)])
-            ref[at, pl.ds(odd_side, 8)] = put(odd[WIDE.index(j)])
-        else:
-            ref[at, 0:8] = jnp.zeros((8, ref.shape[2]), F32)
-            ref[at, 40:48] = jnp.zeros((8, ref.shape[2]), F32)
+        ref, i, base = at(j)
+        ref[i, 8:24] = base + center[j, 0:16] if base else center[j, 0:16]
+        ref[i, 24:40] = base + center[j, 48:64] if base else center[j, 48:64]
+        if j in NONE:
+            ref[i, 0:8] = jnp.zeros((8, ref.shape[2]), F32)
+            ref[i, 40:48] = jnp.zeros((8, ref.shape[2]), F32)
+    for tiles, above in ((even, flags[2] == 0), (odd, flags[2] == 1)):
+        side = pl.ds(pl.multiple_of(jnp.where(above, 40, 0), 8), 8)
+        for t, j in enumerate(WHOLE):
+            ref, i, base = at(j)
+            ref[i, side] = base + tiles[t]
+        for t, (a, b) in enumerate(HALVES):
+            tile = tiles[len(WHOLE) + t]
+            turned = pltpu.roll(tile, 4, 0)
+            for j, first in ((a, True), (b, False)):
+                ref, i, base = at(j)
+                ref[i, side] = base + jnp.where(above == first, tile, turned)
 
     powers(v, k, t1, w1, t2, w2, t3, y1s, y2s)
     rows[...] = inner_rows[...]
@@ -484,7 +502,7 @@
         flops=10**6,
         flagged=True,
         fetched=2,
-    )(flags, right_side, kappa_sq)
+    )(flags, *[pltpu.with_memory_space_constraint(x, pltpu.HBM) for x in (right_side, kappa_sq)])
     relayed = [send(piece, spread) for piece, (spread, _) in zip((p0, p1, p2, high2), ROUTES)]
     swapped = [
         send(x, pairs)
@@ -492,7 +510,7 @@
     ]
     *pieces, ahead = [send(x, onward) for x, (_, onward) in zip(relayed, ROUTES)]
     pieces.append(send(p3, STEP))
-    edge = (len(WIDE), 8, lanes)
+    edge = (TILES, 8, lanes)
     return kernel(
         gather_kernel, [shape(len(PLANES)), edge, edge], flops=10**6, flagged=True
     )(flags, own, *swapped, ahead, *pieces)

time: 136 us -> 135 us (level)
  starting transfers between devices: 64.4 us -> 62.2 us
  local copies, waits for them, and re-layouts: 2.02 us -> 0.12 us
    ppermute x16, starting transfers between devices: 64.4 us -> 62.2 us  [send(): return lax.ppermute(x, ALL, pairs)]
    unnamed x8 -> x4, local copies, waits for them, and re-layouts: 1.91 us -> 0.01 us
  transfers between devices with their start and end apart: 16 -> 16, of which waited for: 5 -> 6; matrix products, arithmetic and copies ran while one was open for 0% -> 0% of each run, Pallas kernels for 2% -> 2%
where the time goes in v6:
time: 135 us
  starting transfers between devices  62.2 us (46%)
  waiting for transfers between devices  31.3 us (23%)
  blocking collectives  31.3 us (23%)
  Pallas kernels  8.7 us (6%)
    ppermute x16, starting transfers between devices, send(): return lax.ppermute(x, ALL, pairs)  62.2 us
    ppermute x16, waiting for transfers between devices, send(): return lax.ppermute(x, ALL, pairs)  31.3 us
    all_to_all x1, blocking collectives, steps(): lax.all_to_all(sums.reshape(n_column, 1, 128), COLUMN, 0, 0)  19.6 us
    all_to_all x1, blocking collectives, steps(): lax.all_to_all(sums.reshape(n_plane, 1, 128), PLANE, 0, 0)  11.6 us
    pallas_call x6, Pallas kernels, call(): pl.pallas_call(fn, out_shape=[jax.ShapeDtypeStruct(s, F32) for s in outs]...  8.7 us
  transfers between devices with their start and end apart: 16, of which 6 were waited for; matrix products, arithmetic and copies ran while one was open for 0% of the time, Pallas kernels for 2%

profile of v6, /device:TPU:1, one launch (start us, length us, event | category | flops | bytes accessed | tf_op | source)
XLA Modules:
  0.0 134.6 jit_solution(6462713457951758335)
XLA Ops:
  0.6 0.0 copy-start
  0.7 0.1 stack.23
  0.8 1.7 %shard_map.49 = (f32[8,64,256]{2,1,0:T(8,128)S(1)}, f32[2,64,256]{2,1,0:T(8,128)S(1)}, f32[2,64,256]{2,1,0:T(8,128)S(1)}, f32[2,64,256]{2,1,0:T(8,128)S(1)}, f32...) custom-call(s32[5]{0:T(128)S(1)} %convert_element_type.3.flags, f32[4,64,256]{2,1,0:T(8,128)} %rhs.5, ...), custom_call_target="tpu_custom_call" | custom-call | flops 1000000 | bytes 126024 | tf_op jit(solution)/shard_map/pallas_call | solution.py:475
  2.5 5.2 %collective-permute-start.7 = (f32[2,64,256]{2,1,0:T(8,128)S(1)}, f32[2,64,256]{2,1,0:T(8,128)S(1)}, u32[]{:S(2)}, u32[]{:S(2)}) collective-permute-start(f32[2,64,256]{2,1,0:T(8,128)S(1)} %get-tuple-element.24), channel_id=1, source_target_pairs={{248,56},{249,57},{250,58},{251,59},{252,60},{253,61},{254,62},{25... | collective-permute-start | bytes 393224 | tf_op jit(solution)/shard_map/ppermute | solution.py:492
  7.7 2.0 %collective-permute-start.9 = (f32[2,64,256]{2,1,0:T(8,128)S(1)}, f32[2,64,256]{2,1,0:T(8,128)S(1)}, u32[]{:S(2)}, u32[]{:S(2)}) collective-permute-start(f32[2,64,256]{2,1,0:T(8,128)S(1)} %get-tuple-element.25), channel_id=1, source_target_pairs={{248,192},{249,193},{250,194},{251,195},{252,196},{253,197},{254,1... | collective-permute-start | bytes 393224 | tf_op jit(solution)/shard_map/ppermute | solution.py:492
  9.7 1.3 collective-permute-start.11
  11.0 1.9 %collective-permute-start.2 = (f32[3,64,256]{2,1,0:T(8,128)S(1)}, f32[3,64,256]{2,1,0:T(8,128)S(1)}, u32[]{:S(2)}, u32[]{:S(2)}) collective-permute-start(f32[3,64,256]{2,1,0:T(8,128)S(1)} %get-tuple-element.22), channel_id=1, source_target_pairs={{0,16},{1,17},{2,18},{3,19},{4,20},{5,21},{6,22},{7,23},{8,24},{9,... | collective-permute-start | bytes 589832 | tf_op jit(solution)/shard_map/ppermute | solution.py:492
  12.9 16.4 %collective-permute-start.13 = (f32[2,64,256]{2,1,0:T(8,128)S(1)}, f32[2,64,256]{2,1,0:T(8,128)S(1)}, u32[]{:S(2)}, u32[]{:S(2)}) collective-permute-start(f32[2,64,256]{2,1,0:T(8,128)S(1)} %get-tuple-element.27), channel_id=1, source_target_pairs={{248,256},{249,257},{250,258},{251,259},{252,260},{253,261},{254,2... | collective-permute-start | bytes 393224 | tf_op jit(solution)/shard_map/ppermute | solution.py:492
  29.3 0.0 collective-permute-done.7
  29.3 0.7 collective-permute-start.1
  30.0 0.0 collective-permute-done.9
  30.1 1.9 %collective-permute-start = (f32[8,64,256]{2,1,0:T(8,128)S(1)}, f32[8,64,256]{2,1,0:T(8,128)S(1)}, u32[]{:S(2)}, u32[]{:S(2)}) collective-permute-start(f32[8,64,256]{2,1,0:T(8,128)S(1)} %get-tuple-element.21.own), channel_id=1, source_target_pairs={{0,8},{1,9},{2,10},{3,11},{4,12},{5,13},{6,14},{7,15},{8,0},{9,1},... | collective-permute-start | bytes 1572872 | tf_op jit(solution)/shard_map/ppermute | solution.py:492
  32.0 0.0 collective-permute-done.11
  32.0 1.3 collective-permute-start.5
  33.3 0.0 collective-permute-done.13.d3
  33.3 1.3 collective-permute-start.4
  34.6 0.0 collective-permute-done.2.low2
  34.6 0.7 collective-permute-start.3
  35.3 5.8 %collective-permute-done.5 = f32[3,64,256]{2,1,0:T(8,128)S(1)} collective-permute-done((f32[3,64,256]{2,1,0:T(8,128)S(1)}, f32[3,64,256]{2,1,0:T(8,128)S(1)}, u32[]{:S(2)}, u32[]{:S(2)}) %collective-permute-start.5) | collective-permute-done | bytes 196640 | tf_op jit(solution)/shard_map/ppermute | solution.py:492
  41.1 1.3 collective-permute-start.8
  42.4 6.4 %collective-permute-done.4.across = f32[3,64,256]{2,1,0:T(8,128)S(1)} collective-permute-done((f32[3,64,256]{2,1,0:T(8,128)S(1)}, f32[3,64,256]{2,1,0:T(8,128)S(1)}, u32[]{:S(2)}, u32[]{:S(2)}) %collective-permute-start.4) | collective-permute-done | bytes 196640 | tf_op jit(solution)/shard_map/ppermute | solution.py:492
  48.8 0.7 collective-permute-start.6
  49.4 0.0 collective-permute-done.3.high2
  49.4 1.3 collective-permute-start.10
  50.7 2.2 %collective-permute-done.8.d0 = f32[2,64,256]{2,1,0:T(8,128)S(1)} collective-permute-done((f32[2,64,256]{2,1,0:T(8,128)S(1)}, f32[2,64,256]{2,1,0:T(8,128)S(1)}, u32[]{:S(2)}, u32[]{:S(2)}) %collective-permute-start.8) | collective-permute-done | bytes 131104 | tf_op jit(solution)/shard_map/ppermute | solution.py:492
  53.0 1.3 collective-permute-start.12
  54.2 7.2 %collective-permute-done.10.d1 = f32[2,64,256]{2,1,0:T(8,128)S(1)} collective-permute-done((f32[2,64,256]{2,1,0:T(8,128)S(1)}, f32[2,64,256]{2,1,0:T(8,128)S(1)}, u32[]{:S(2)}, u32[]{:S(2)}) %collective-permute-start.10) | collective-permute-done | bytes 131104 | tf_op jit(solution)/shard_map/ppermute | solution.py:492
  61.5 5.9 %collective-permute-done.12.d2 = f32[2,64,256]{2,1,0:T(8,128)S(1)} collective-permute-done((f32[2,64,256]{2,1,0:T(8,128)S(1)}, f32[2,64,256]{2,1,0:T(8,128)S(1)}, u32[]{:S(2)}, u32[]{:S(2)}) %collective-permute-start.12) | collective-permute-done | bytes 131104 | tf_op jit(solution)/shard_map/ppermute | solution.py:492
  67.4 0.0 collective-permute-done.6.ahead
  67.4 0.0 collective-permute-done.1.odd
  67.4 0.0 collective-permute-done.even
  67.4 0.8 shard_map.50
  68.2 23.1 %collective-permute-start.14 = (f32[18,8,256]{2,1,0:T(8,128)S(1)}, f32[18,8,256]{2,1,0:T(8,128)S(1)}, u32[]{:S(2)}, u32[]{:S(2)}) collective-permute-start(f32[18,8,256]{2,1,0:T(8,128)S(1)} %get-tuple-element.29), channel_id=1, source_target_pairs={{0,1},{1,0},{2,3},{3,2},{4,5},{5,4},{6,7},{7,6},{8,9},{9,8},{10,11... | collective-permute-start | bytes 442376 | tf_op jit(solution)/shard_map/ppermute | solution.py:492
  91.3 1.9 %collective-permute-start.15 = (f32[18,8,256]{2,1,0:T(8,128)S(1)}, f32[18,8,256]{2,1,0:T(8,128)S(1)}, u32[]{:S(2)}, u32[]{:S(2)}) collective-permute-start(f32[18,8,256]{2,1,0:T(8,128)S(1)} %get-tuple-element.30), channel_id=1, source_target_pairs={{0,7},{1,2},{2,1},{3,4},{4,3},{5,6},{6,5},{7,0},{8,15},{9,10},{10,... | collective-permute-start | bytes 442376 | tf_op jit(solution)/shard_map/ppermute | solution.py:492
  93.2 0.0 copy-done
  93.2 0.0 copy-start.1
  93.2 2.3 %shard_map.51 = (f32[4,48,256]{2,1,0:T(8,128)S(1)}, f32[4,48,256]{2,1,0:T(8,128)S(1)}, f32[4,48,256]{2,1,0:T(8,128)S(1)}, f32[128,128]{1,0:T(8,128)S(1)}) custom-call(f32[4,64,256]{2,1,0:T(8,128)S(1)} %copy-done, f32[30,64,256]{2,1,0:T(8,128)S(1)} %get-tuple-element.28.center), custom_call_target="tpu_custom_call" | custom-call | flops 20000000 | bytes 2501024 | tf_op jit(solution)/shard_map/pallas_call | solution.py:475
  95.5 0.0 collective-permute-done.14.even
  95.5 3.8 %collective-permute-done.15.odd = f32[18,8,256]{2,1,0:T(8,128)S(1)} collective-permute-done((f32[18,8,256]{2,1,0:T(8,128)S(1)}, f32[18,8,256]{2,1,0:T(8,128)S(1)}, u32[]{:S(2)}, u32[]{:S(2)}) %collective-permute-start.15) | collective-permute-done | bytes 147488 | tf_op jit(solution)/shard_map/ppermute | solution.py:492
  99.3 2.4 %shard_map.52 = (f32[4,16,256]{2,1,0:T(8,128)S(1)}, f32[4,16,256]{2,1,0:T(8,128)S(1)}, f32[4,16,256]{2,1,0:T(8,128)S(1)}, f32[32,128]{1,0:T(8,128)S(1)}) custom-call(s32[5]{0:T(128)S(1)} %convert_element_type.3.flags, f32[4,64,256]{2,1,0:T(8,128)S(1)} %copy-done, f32[30,64,256]{2,1,0:T(8,128)S(1)} %get-tuple-element.28.center, ...), custom_call_target="tpu_custom_call" | custom-call | flops 12000000 | bytes 1501024 | tf_op jit(solution)/shard_map/pallas_call | solution.py:475
  101.7 11.6 %all_to_all.10 = f32[32,1,128]{2,1,0:T(1,128)S(1)} all-to-all(f32[32,1,128]{2,1,0:T(1,128)S(1)} %bitcast.16), channel_id=1, replica_groups=mesh['gx_0'=3,'gx_1'=4,'gx_2'=8,'gy_0'=4,'gy_1'=2] {'gx_1','gx_2'}, dimensions={0} | all-to-all | bytes 32768 | tf_op jit(solution)/shard_map/all_to_all | solution.py:541
  113.4 0.1 shard_map.53
  113.4 19.6 %all_to_all.11 = f32[24,1,128]{2,1,0:T(1,128)S(1)} all-to-all(f32[24,1,128]{2,1,0:T(1,128)S(1)} %bitcast.15), channel_id=1, replica_groups=mesh['gx_0'=3,'gx_1'=4,'gx_2'=8,'gy_0'=4,'gy_1'=2] {'gx_0','gy_0','gy_1'}, dimensions={0} | all-to-all | bytes 24576 | tf_op jit(solution)/shard_map/all_to_all | solution.py:543
  133.1 0.0 copy-done.1
  133.1 1.5 %shard_map.54 = (f32[4,64,256]{2,1,0:T(8,128)}, f32[4,64,256]{2,1,0:T(8,128)}, f32[3]{0:T(128)}) custom-call(f32[24,128]{1,0:T(8,128)S(1)} %bitcast.14, f32[4,64,256]{2,1,0:T(8,128)S(1)} %copy-done, f32[4,64,256]{2,1,0:T(8,128)S(1)} %copy-done.1, f32[4,48,256]{2,1,0:T(8,128)S(1)} %get-tuple-element.33.i1, f32[4,48,256]{2,1,0:T(8,128)S(1)} %get-tuple-element.34.i2, ...), custom_call_target="tpu_custom_call" | custom-call | flops 2000000 | bytes 251024 | tf_op jit(solution)/shard_map/pallas_call | solution.py:475
  (1 shorter events, 0.0 us)
Async XLA Ops:
  0.6 92.6 %copy-start = (f32[4,64,256]{2,1,0:T(8,128)S(1)}, f32[4,64,256]{2,1,0:T(8,128)}, u32[]{:S(2)}) copy-start(f32[4,64,256]{2,1,0:T(8,128)} %rhs.5) | copy-start | bytes 786436
  2.5 26.8 %collective-permute-start.7 = (f32[2,64,256]{2,1,0:T(8,128)S(1)}, f32[2,64,256]{2,1,0:T(8,128)S(1)}, u32[]{:S(2)}, u32[]{:S(2)}) collective-permute-start(f32[2,64,256]{2,1,0:T(8,128)S(1)} %get-tuple-element.24), channel_id=1, source_target_pairs={{248,56},{249,57},{250,58},{251,59},{252,60},{253,61},{254,62},{25... | collective-permute-start | bytes 393224 | tf_op jit(solution)/shard_map/ppermute | solution.py:492
  7.7 22.3 %collective-permute-start.9 = (f32[2,64,256]{2,1,0:T(8,128)S(1)}, f32[2,64,256]{2,1,0:T(8,128)S(1)}, u32[]{:S(2)}, u32[]{:S(2)}) collective-permute-start(f32[2,64,256]{2,1,0:T(8,128)S(1)} %get-tuple-element.25), channel_id=1, source_target_pairs={{248,192},{249,193},{250,194},{251,195},{252,196},{253,197},{254,1... | collective-permute-start | bytes 393224 | tf_op jit(solution)/shard_map/ppermute | solution.py:492
  9.7 22.3 %collective-permute-start.11 = (f32[2,64,256]{2,1,0:T(8,128)S(1)}, f32[2,64,256]{2,1,0:T(8,128)S(1)}, u32[]{:S(2)}, u32[]{:S(2)}) collective-permute-start(f32[2,64,256]{2,1,0:T(8,128)S(1)} %get-tuple-element.26), channel_id=1, source_target_pairs={{248,184},{249,185},{250,186},{251,187},{252,188},{253,189},{254,1... | collective-permute-start | bytes 393224 | tf_op jit(solution)/shard_map/ppermute | solution.py:492
  11.0 23.6 %collective-permute-start.2 = (f32[3,64,256]{2,1,0:T(8,128)S(1)}, f32[3,64,256]{2,1,0:T(8,128)S(1)}, u32[]{:S(2)}, u32[]{:S(2)}) collective-permute-start(f32[3,64,256]{2,1,0:T(8,128)S(1)} %get-tuple-element.22), channel_id=1, source_target_pairs={{0,16},{1,17},{2,18},{3,19},{4,20},{5,21},{6,22},{7,23},{8,24},{9,... | collective-permute-start | bytes 589832 | tf_op jit(solution)/shard_map/ppermute | solution.py:492
  12.9 20.4 %collective-permute-start.13 = (f32[2,64,256]{2,1,0:T(8,128)S(1)}, f32[2,64,256]{2,1,0:T(8,128)S(1)}, u32[]{:S(2)}, u32[]{:S(2)}) collective-permute-start(f32[2,64,256]{2,1,0:T(8,128)S(1)} %get-tuple-element.27), channel_id=1, source_target_pairs={{248,256},{249,257},{250,258},{251,259},{252,260},{253,261},{254,2... | collective-permute-start | bytes 393224 | tf_op jit(solution)/shard_map/ppermute | solution.py:492
  29.3 38.0 %collective-permute-start.1 = (f32[8,64,256]{2,1,0:T(8,128)S(1)}, f32[8,64,256]{2,1,0:T(8,128)S(1)}, u32[]{:S(2)}, u32[]{:S(2)}) collective-permute-start(f32[8,64,256]{2,1,0:T(8,128)S(1)} %get-tuple-element.21.own), channel_id=1, source_target_pairs={{8,16},{9,17},{10,18},{11,19},{12,20},{13,21},{14,22},{15,23},{16,... | collective-permute-start | bytes 1572872 | tf_op jit(solution)/shard_map/ppermute | solution.py:492
  30.1 37.3 %collective-permute-start = (f32[8,64,256]{2,1,0:T(8,128)S(1)}, f32[8,64,256]{2,1,0:T(8,128)S(1)}, u32[]{:S(2)}, u32[]{:S(2)}) collective-permute-start(f32[8,64,256]{2,1,0:T(8,128)S(1)} %get-tuple-element.21.own), channel_id=1, source_target_pairs={{0,8},{1,9},{2,10},{3,11},{4,12},{5,13},{6,14},{7,15},{8,0},{9,1},... | collective-permute-start | bytes 1572872 | tf_op jit(solution)/shard_map/ppermute | solution.py:492
  32.0 9.1 %collective-permute-start.5 = (f32[3,64,256]{2,1,0:T(8,128)S(1)}, f32[3,64,256]{2,1,0:T(8,128)S(1)}, u32[]{:S(2)}, u32[]{:S(2)}) collective-permute-start(f32[3,64,256]{2,1,0:T(8,128)S(1)} %get-tuple-element.23), channel_id=1, source_target_pairs={{248,120},{249,121},{250,122},{251,123},{252,124},{253,125},{254,1... | collective-permute-start | bytes 589832 | tf_op jit(solution)/shard_map/ppermute | solution.py:492
  33.3 15.4 %collective-permute-start.4 = (f32[3,64,256]{2,1,0:T(8,128)S(1)}, f32[3,64,256]{2,1,0:T(8,128)S(1)}, u32[]{:S(2)}, u32[]{:S(2)}) collective-permute-start(f32[3,64,256]{2,1,0:T(8,128)S(1)} %get-tuple-element.23), channel_id=1, source_target_pairs={{240,256},{241,257},{242,258},{243,259},{244,260},{245,261},{246,2... | collective-permute-start | bytes 589832 | tf_op jit(solution)/shard_map/ppermute | solution.py:492
  34.6 14.8 %collective-permute-start.3 = (f32[3,64,256]{2,1,0:T(8,128)S(1)}, f32[3,64,256]{2,1,0:T(8,128)S(1)}, u32[]{:S(2)}, u32[]{:S(2)}) collective-permute-start(f32[3,64,256]{2,1,0:T(8,128)S(1)} %get-tuple-element.23), channel_id=1, source_target_pairs={{16,32},{17,33},{18,34},{19,35},{20,36},{21,37},{22,38},{23,39},{2... | collective-permute-start | bytes 589832 | tf_op jit(solution)/shard_map/ppermute | solution.py:492
  41.1 11.9 %collective-permute-start.8 = (f32[2,64,256]{2,1,0:T(8,128)S(1)}, f32[2,64,256]{2,1,0:T(8,128)S(1)}, u32[]{:S(2)}, u32[]{:S(2)}) collective-permute-start(f32[2,64,256]{2,1,0:T(8,128)S(1)} %collective-permute-done.7), channel_id=1, source_target_pairs={{56,256},{57,257},{58,258},{59,259},{60,260},{61,261},{62,262},{63... | collective-permute-start | bytes 393224 | tf_op jit(solution)/shard_map/ppermute | solution.py:492
  48.8 18.6 %collective-permute-start.6 = (f32[3,64,256]{2,1,0:T(8,128)S(1)}, f32[3,64,256]{2,1,0:T(8,128)S(1)}, u32[]{:S(2)}, u32[]{:S(2)}) collective-permute-start(f32[3,64,256]{2,1,0:T(8,128)S(1)} %collective-permute-done.5), channel_id=1, source_target_pairs={{120,264},{121,265},{122,266},{123,267},{124,268},{125,269},{126,2... | collective-permute-start | bytes 589832 | tf_op jit(solution)/shard_map/ppermute | solution.py:492
  49.4 12.0 %collective-permute-start.10 = (f32[2,64,256]{2,1,0:T(8,128)S(1)}, f32[2,64,256]{2,1,0:T(8,128)S(1)}, u32[]{:S(2)}, u32[]{:S(2)}) collective-permute-start(f32[2,64,256]{2,1,0:T(8,128)S(1)} %collective-permute-done.9), channel_id=1, source_target_pairs={{192,256},{193,257},{194,258},{195,259},{196,260},{197,261},{198,2... | collective-permute-start | bytes 393224 | tf_op jit(solution)/shard_map/ppermute | solution.py:492
  53.0 14.4 %collective-permute-start.12 = (f32[2,64,256]{2,1,0:T(8,128)S(1)}, f32[2,64,256]{2,1,0:T(8,128)S(1)}, u32[]{:S(2)}, u32[]{:S(2)}) collective-permute-start(f32[2,64,256]{2,1,0:T(8,128)S(1)} %collective-permute-done.11), channel_id=1, source_target_pairs={{184,256},{185,257},{186,258},{187,259},{188,260},{189,261},{190,2... | collective-permute-start | bytes 393224 | tf_op jit(solution)/shard_map/ppermute | solution.py:492
  68.2 27.3 %collective-permute-start.14 = (f32[18,8,256]{2,1,0:T(8,128)S(1)}, f32[18,8,256]{2,1,0:T(8,128)S(1)}, u32[]{:S(2)}, u32[]{:S(2)}) collective-permute-start(f32[18,8,256]{2,1,0:T(8,128)S(1)} %get-tuple-element.29), channel_id=1, source_target_pairs={{0,1},{1,0},{2,3},{3,2},{4,5},{5,4},{6,7},{7,6},{8,9},{9,8},{10,11... | collective-permute-start | bytes 442376 | tf_op jit(solution)/shard_map/ppermute | solution.py:492
  91.3 8.0 %collective-permute-start.15 = (f32[18,8,256]{2,1,0:T(8,128)S(1)}, f32[18,8,256]{2,1,0:T(8,128)S(1)}, u32[]{:S(2)}, u32[]{:S(2)}) collective-permute-start(f32[18,8,256]{2,1,0:T(8,128)S(1)} %get-tuple-element.30), channel_id=1, source_target_pairs={{0,7},{1,2},{2,1},{3,4},{4,3},{5,6},{6,5},{7,0},{8,15},{9,10},{10,... | collective-permute-start | bytes 442376 | tf_op jit(solution)/shard_map/ppermute | solution.py:492
  93.2 39.9 %copy-start.1 = (f32[4,64,256]{2,1,0:T(8,128)S(1)}, f32[4,64,256]{2,1,0:T(8,128)}, u32[]{:S(2)}) copy-start(f32[4,64,256]{2,1,0:T(8,128)} %kappa.1) | copy-start | bytes 786436

commit v7 on v6

--- a/solution.py
+++ b/solution.py
@@ -21,8 +21,8 @@
 F32 = jnp.float32
 
 
-def over_gx(moves):
-    return [(a % NGX * RANKS + h, b % NGX * RANKS + h) for a, b in moves for h in range(RANKS)]
+def over_gx(moves, ranks=range(RANKS)):
+    return [(a % NGX * RANKS + h, b % NGX * RANKS + h) for a, b in moves for h in ranks]
 
 
 def corner(hi, x, y):
@@ -35,22 +35,6 @@
 
 def LAST(k):
     return corner(k, XS - 1, YS - 1)
-
-
-def SIDE_A(k):
-    return corner(k, 0, YS - 1)
-
-
-def SIDE_B(k):
-    return corner(k, XS - 1, 0)
-
-
-def NEAR_LAST(k):
-    return corner(k, XS - 2, YS - 1)
-
-
-def NEAR_FIRST(k):
-    return corner(k, 1, 0)
 
 
 SEGS = range(HI)
@@ -64,27 +48,27 @@
 ACROSS = over_gx(
     [(LAST(k) - 1, FIRST(k + 1)) for k in SEGS] + [(FIRST(k) + 1, LAST(k - 1)) for k in SEGS]
 )
-ROUTES = [
-    (
-        over_gx([(LAST(k), SIDE_A(k)) for k in SEGS] + [(FIRST(k), SIDE_B(k)) for k in SEGS]),
-        over_gx([(SIDE_A(k), FIRST(k + 1)) for k in SEGS] + [(SIDE_B(k), LAST(k - 1)) for k in SEGS]),
-    ),
-    (
-        over_gx([(LAST(k), SIDE_B(k)) for k in SEGS] + [(FIRST(k), SIDE_A(k)) for k in SEGS]),
-        over_gx([(SIDE_B(k), FIRST(k + 1)) for k in SEGS] + [(SIDE_A(k), LAST(k - 1)) for k in SEGS]),
-    ),
-    (
-        over_gx([(LAST(k), NEAR_LAST(k)) for k in SEGS] + [(FIRST(k), NEAR_FIRST(k)) for k in SEGS]),
-        over_gx([(NEAR_LAST(k), FIRST(k + 1)) for k in SEGS] + [(NEAR_FIRST(k), LAST(k - 1)) for k in SEGS]),
-    ),
-    (
-        over_gx([(LAST(k), corner(k, 1, YS - 1)) for k in SEGS] + [(FIRST(k), corner(k, 2, 0)) for k in SEGS]),
-        over_gx(
-            [(corner(k, 1, YS - 1), FIRST(k + 1) + 1) for k in SEGS]
-            + [(corner(k, 2, 0), LAST(k - 1) - 1) for k in SEGS]
-        ),
-    ),
-]
+RELAYS = (
+    ((0, YS - 1), (XS - 1, 0), (0, YS - 2), (1, YS - 1)),
+    ((2, YS - 1), (1, 0), (2, YS - 2), (2, 2)),
+)
+
+
+def route(i, ends):
+    spread, onward = [], []
+    for core, relays in enumerate(RELAYS):
+        ranks = range(core, RANKS, 2)
+        x, y = relays[i]
+        for k in SEGS:
+            up, down = corner(k, x, y), corner(k, XS - 1 - x, YS - 1 - y)
+            spread += over_gx([(LAST(k), up), (FIRST(k), down)], ranks)
+            onward += over_gx([(up, FIRST(k + 1) + ends), (down, LAST(k - 1) - ends)], ranks)
+    return spread, onward
+
+
+ROUTES = [route(0, 0), route(1, 0), route(2, 0), route(3, 1)]
+CUTS = ((0, 3), (3, 5), (5, 7), (7, 8))
+
 GY_EVEN = [(g * RANKS + h, g * RANKS + (h ^ 1)) for g in range(NGX) for h in range(RANKS)]
 GY_ODD = [
     (g * RANKS + h, g * RANKS + (((h + 1) ^ 1) - 1) % RANKS) for g in range(NGX) for h in range(RANKS)
@@ -237,8 +221,8 @@
         shifted = 6.0 + k
         own[AT["v", i]] = (1.0 / (shifted * shifted + 6.0)) * rhs[i]
         own[AT["k", i]] = k
-    for i, piece in enumerate((p0, p1, p2, p3)):
-        piece[...] = own[2 * i : 2 * i + 2]
+    for (a, b), piece in zip(CUTS, (p0, p1, p2, p3)):
+        piece[...] = own[a:b]
 
     @pl.when(flags[1] == 0)
     def _():
@@ -254,10 +238,12 @@
 def gather_kernel(
     flags, own, even, odd, low2, high2, across, ahead, d0, d1, d2, d3, center, to_even, to_odd
 ):
+    cut = [(piece, i) for (a, b), piece in zip(CUTS, (d0, d1, d2, d3)) for i in range(b - a)]
+
     def lay(part, ref):
         for j, (name, at) in enumerate(PLANES):
             if name == part:
-                src, i = ((d0, d1, d2, d3)[at // 2], at % 2) if ref is None else (ref, at)
+                src, i = cut[at] if ref is None else (ref, at)
                 center[j] = src[i]
 
     def when(*conditions):
@@ -497,7 +483,7 @@
     shape = lambda n: (n, cols, lanes)
     own, p0, p1, p2, p3, low2, high2 = kernel(
         start_kernel,
-        [shape(8)] + [shape(2)] * 4 + [shape(3)] * 2,
+        [shape(8)] + [shape(b - a) for a, b in CUTS] + [shape(3)] * 2,
         [right_side.shape] * 2,
         flops=10**6,
         flagged=True,

time: 135 us -> 134 us (level)
  blocking collectives: 31.3 us -> 43.6 us
  starting transfers between devices: 62.2 us -> 52.9 us
  waiting for transfers between devices: 31.3 us -> 27.2 us
    ppermute x16, starting transfers between devices: 62.2 us -> 52.9 us  [send(): return lax.ppermute(x, ALL, pairs)]
    all_to_all x1, blocking collectives: 19.6 us -> 27 us  [steps(): lax.all_to_all(sums.reshape(n_column, 1, 128), COLUMN, 0, 0)]
    all_to_all x1, blocking collectives: 11.6 us -> 16.6 us  [steps(): lax.all_to_all(sums.reshape(n_plane, 1, 128), PLANE, 0, 0)]
    ppermute x16, waiting for transfers between devices: 31.3 us -> 27.2 us  [send(): return lax.ppermute(x, ALL, pairs)]
  transfers between devices with their start and end apart: 16 -> 16, of which waited for: 6 -> 4; matrix products, arithmetic and copies ran while one was open for 0% -> 0% of each run, Pallas kernels for 2% -> 2%
where the time goes in v7:
time: 134 us
  starting transfers between devices  52.9 us (39%)
  blocking collectives  43.6 us (33%)
  waiting for transfers between devices  27.2 us (20%)
  Pallas kernels  8.7 us (6%)
    ppermute x16, starting transfers between devices, send(): return lax.ppermute(x, ALL, pairs)  52.9 us
    ppermute x16, waiting for transfers between devices, send(): return lax.ppermute(x, ALL, pairs)  27.2 us
    all_to_all x1, blocking collectives, steps(): lax.all_to_all(sums.reshape(n_column, 1, 128), COLUMN, 0, 0)  27 us
    all_to_all x1, blocking collectives, steps(): lax.all_to_all(sums.reshape(n_plane, 1, 128), PLANE, 0, 0)  16.6 us
    pallas_call x6, Pallas kernels, call(): pl.pallas_call(fn, out_shape=[jax.ShapeDtypeStruct(s, F32) for s in outs]...  8.7 us
  transfers between devices with their start and end apart: 16, of which 4 were waited for; matrix products, arithmetic and copies ran while one was open for 0% of the time, Pallas kernels for 2%

profile of v7, /device:TPU:1, one launch (start us, length us, event | category | flops | bytes accessed | tf_op | source)
XLA Modules:
  0.0 133.5 jit_solution(4750787707643019859)
XLA Ops:
  0.6 0.0 copy-start
  0.7 0.1 stack.23
  0.8 1.7 %shard_map.49 = (f32[8,64,256]{2,1,0:T(8,128)S(1)}, f32[3,64,256]{2,1,0:T(8,128)S(1)}, f32[2,64,256]{2,1,0:T(8,128)S(1)}, f32[2,64,256]{2,1,0:T(8,128)S(1)}, f32...) custom-call(s32[5]{0:T(128)S(1)} %convert_element_type.3.flags, f32[4,64,256]{2,1,0:T(8,128)} %rhs.5, ...), custom_call_target="tpu_custom_call" | custom-call | flops 1000000 | bytes 126024 | tf_op jit(solution)/shard_map/pallas_call | solution.py:461
  2.5 8.4 %collective-permute-start.9 = (f32[2,64,256]{2,1,0:T(8,128)S(1)}, f32[2,64,256]{2,1,0:T(8,128)S(1)}, u32[]{:S(2)}, u32[]{:S(2)}) collective-permute-start(f32[2,64,256]{2,1,0:T(8,128)S(1)} %get-tuple-element.25), channel_id=1, source_target_pairs={{248,192},{250,194},{252,196},{254,198},{0,56},{2,58},{4,60},{6,62... | collective-permute-start | bytes 393224 | tf_op jit(solution)/shard_map/ppermute | solution.py:478
  10.9 14.1 %collective-permute-start.13 = (f32[1,64,256]{2,1,0:T(8,128)S(1)}, f32[1,64,256]{2,1,0:T(8,128)S(1)}, u32[]{:S(2)}, u32[]{:S(2)}) collective-permute-start(f32[1,64,256]{2,1,0:T(8,128)S(1)} %get-tuple-element.27), channel_id=1, source_target_pairs={{248,256},{249,257},{250,258},{251,259},{252,260},{253,261},{254,2... | collective-permute-start | bytes 196616 | tf_op jit(solution)/shard_map/ppermute | solution.py:478
  24.9 1.3 collective-permute-start.11
  26.2 1.9 %collective-permute-start.2 = (f32[3,64,256]{2,1,0:T(8,128)S(1)}, f32[3,64,256]{2,1,0:T(8,128)S(1)}, u32[]{:S(2)}, u32[]{:S(2)}) collective-permute-start(f32[3,64,256]{2,1,0:T(8,128)S(1)} %get-tuple-element.22), channel_id=1, source_target_pairs={{0,16},{1,17},{2,18},{3,19},{4,20},{5,21},{6,22},{7,23},{8,24},{9,... | collective-permute-start | bytes 589832 | tf_op jit(solution)/shard_map/ppermute | solution.py:478
  28.2 1.3 collective-permute-start.7
  29.5 0.0 collective-permute-done.13.d3
  29.5 0.7 collective-permute-start.1
  30.2 0.0 collective-permute-done.9
  30.2 5.1 %collective-permute-start = (f32[8,64,256]{2,1,0:T(8,128)S(1)}, f32[8,64,256]{2,1,0:T(8,128)S(1)}, u32[]{:S(2)}, u32[]{:S(2)}) collective-permute-start(f32[8,64,256]{2,1,0:T(8,128)S(1)} %get-tuple-element.21.own), channel_id=1, source_target_pairs={{0,8},{1,9},{2,10},{3,11},{4,12},{5,13},{6,14},{7,15},{8,0},{9,1},... | collective-permute-start | bytes 1572872 | tf_op jit(solution)/shard_map/ppermute | solution.py:478
  35.3 0.0 collective-permute-done.11
  35.3 1.3 collective-permute-start.5
  36.7 0.0 collective-permute-done.2.low2
  36.7 1.3 collective-permute-start.4
  38.0 0.0 collective-permute-done.7
  38.0 0.7 collective-permute-start.3
  38.7 0.6 collective-permute-done.5
  39.2 1.3 collective-permute-start.10
  40.5 12.4 %collective-permute-done.4.across = f32[3,64,256]{2,1,0:T(8,128)S(1)} collective-permute-done((f32[3,64,256]{2,1,0:T(8,128)S(1)}, f32[3,64,256]{2,1,0:T(8,128)S(1)}, u32[]{:S(2)}, u32[]{:S(2)}) %collective-permute-start.4) | collective-permute-done | bytes 196640 | tf_op jit(solution)/shard_map/ppermute | solution.py:478
  52.9 1.3 collective-permute-start.8
  54.2 0.0 collective-permute-done.3.high2
  54.2 0.7 collective-permute-start.6
  54.9 0.0 collective-permute-done.10.d1
  54.9 1.3 collective-permute-start.12
  56.2 13.7 %collective-permute-done.12.d2 = f32[2,64,256]{2,1,0:T(8,128)S(1)} collective-permute-done((f32[2,64,256]{2,1,0:T(8,128)S(1)}, f32[2,64,256]{2,1,0:T(8,128)S(1)}, u32[]{:S(2)}, u32[]{:S(2)}) %collective-permute-start.12) | collective-permute-done | bytes 131104 | tf_op jit(solution)/shard_map/ppermute | solution.py:478
  69.9 0.0 collective-permute-done.8.d0
  69.9 0.0 collective-permute-done.6.ahead
  69.9 0.0 collective-permute-done.1.odd
  69.9 0.0 collective-permute-done.even
  69.9 0.8 shard_map.50
  70.8 3.4 %collective-permute-start.14 = (f32[18,8,256]{2,1,0:T(8,128)S(1)}, f32[18,8,256]{2,1,0:T(8,128)S(1)}, u32[]{:S(2)}, u32[]{:S(2)}) collective-permute-start(f32[18,8,256]{2,1,0:T(8,128)S(1)} %get-tuple-element.29), channel_id=1, source_target_pairs={{0,1},{1,0},{2,3},{3,2},{4,5},{5,4},{6,7},{7,6},{8,9},{9,8},{10,11... | collective-permute-start | bytes 442376 | tf_op jit(solution)/shard_map/ppermute | solution.py:478
  74.2 9.0 %collective-permute-start.15 = (f32[18,8,256]{2,1,0:T(8,128)S(1)}, f32[18,8,256]{2,1,0:T(8,128)S(1)}, u32[]{:S(2)}, u32[]{:S(2)}) collective-permute-start(f32[18,8,256]{2,1,0:T(8,128)S(1)} %get-tuple-element.30), channel_id=1, source_target_pairs={{0,7},{1,2},{2,1},{3,4},{4,3},{5,6},{6,5},{7,0},{8,15},{9,10},{10,... | collective-permute-start | bytes 442376 | tf_op jit(solution)/shard_map/ppermute | solution.py:478
  83.2 0.0 copy-done
  83.2 0.0 copy-start.1
  83.2 2.3 %shard_map.51 = (f32[4,48,256]{2,1,0:T(8,128)S(1)}, f32[4,48,256]{2,1,0:T(8,128)S(1)}, f32[4,48,256]{2,1,0:T(8,128)S(1)}, f32[128,128]{1,0:T(8,128)S(1)}) custom-call(f32[4,64,256]{2,1,0:T(8,128)S(1)} %copy-done, f32[30,64,256]{2,1,0:T(8,128)S(1)} %get-tuple-element.28.center), custom_call_target="tpu_custom_call" | custom-call | flops 20000000 | bytes 2501024 | tf_op jit(solution)/shard_map/pallas_call | solution.py:461
  85.5 0.0 collective-permute-done.14.even
  85.5 0.5 collective-permute-done.15.odd
  86.0 2.4 %shard_map.52 = (f32[4,16,256]{2,1,0:T(8,128)S(1)}, f32[4,16,256]{2,1,0:T(8,128)S(1)}, f32[4,16,256]{2,1,0:T(8,128)S(1)}, f32[32,128]{1,0:T(8,128)S(1)}) custom-call(s32[5]{0:T(128)S(1)} %convert_element_type.3.flags, f32[4,64,256]{2,1,0:T(8,128)S(1)} %copy-done, f32[30,64,256]{2,1,0:T(8,128)S(1)} %get-tuple-element.28.center, ...), custom_call_target="tpu_custom_call" | custom-call | flops 12000000 | bytes 1501024 | tf_op jit(solution)/shard_map/pallas_call | solution.py:461
  88.4 16.6 %all_to_all.10 = f32[32,1,128]{2,1,0:T(1,128)S(1)} all-to-all(f32[32,1,128]{2,1,0:T(1,128)S(1)} %bitcast.16), channel_id=1, replica_groups=mesh['gx_0'=3,'gx_1'=4,'gx_2'=8,'gy_0'=4,'gy_1'=2] {'gx_1','gx_2'}, dimensions={0} | all-to-all | bytes 32768 | tf_op jit(solution)/shard_map/all_to_all | solution.py:527
  105.0 0.1 shard_map.53
  105.1 27.0 %all_to_all.11 = f32[24,1,128]{2,1,0:T(1,128)S(1)} all-to-all(f32[24,1,128]{2,1,0:T(1,128)S(1)} %bitcast.15), channel_id=1, replica_groups=mesh['gx_0'=3,'gx_1'=4,'gx_2'=8,'gy_0'=4,'gy_1'=2] {'gx_0','gy_0','gy_1'}, dimensions={0} | all-to-all | bytes 24576 | tf_op jit(solution)/shard_map/all_to_all | solution.py:529
  132.0 0.0 copy-done.1
  132.0 1.5 %shard_map.54 = (f32[4,64,256]{2,1,0:T(8,128)}, f32[4,64,256]{2,1,0:T(8,128)}, f32[3]{0:T(128)}) custom-call(f32[24,128]{1,0:T(8,128)S(1)} %bitcast.14, f32[4,64,256]{2,1,0:T(8,128)S(1)} %copy-done, f32[4,64,256]{2,1,0:T(8,128)S(1)} %copy-done.1, f32[4,48,256]{2,1,0:T(8,128)S(1)} %get-tuple-element.33.i1, f32[4,48,256]{2,1,0:T(8,128)S(1)} %get-tuple-element.34.i2, ...), custom_call_target="tpu_custom_call" | custom-call | flops 2000000 | bytes 251024 | tf_op jit(solution)/shard_map/pallas_call | solution.py:461
  (1 shorter events, 0.0 us)
Async XLA Ops:
  0.6 82.5 %copy-start = (f32[4,64,256]{2,1,0:T(8,128)S(1)}, f32[4,64,256]{2,1,0:T(8,128)}, u32[]{:S(2)}) copy-start(f32[4,64,256]{2,1,0:T(8,128)} %rhs.5) | copy-start | bytes 786436
  2.5 27.7 %collective-permute-start.9 = (f32[2,64,256]{2,1,0:T(8,128)S(1)}, f32[2,64,256]{2,1,0:T(8,128)S(1)}, u32[]{:S(2)}, u32[]{:S(2)}) collective-permute-start(f32[2,64,256]{2,1,0:T(8,128)S(1)} %get-tuple-element.25), channel_id=1, source_target_pairs={{248,192},{250,194},{252,196},{254,198},{0,56},{2,58},{4,60},{6,62... | collective-permute-start | bytes 393224 | tf_op jit(solution)/shard_map/ppermute | solution.py:478
  10.9 18.6 %collective-permute-start.13 = (f32[1,64,256]{2,1,0:T(8,128)S(1)}, f32[1,64,256]{2,1,0:T(8,128)S(1)}, u32[]{:S(2)}, u32[]{:S(2)}) collective-permute-start(f32[1,64,256]{2,1,0:T(8,128)S(1)} %get-tuple-element.27), channel_id=1, source_target_pairs={{248,256},{249,257},{250,258},{251,259},{252,260},{253,261},{254,2... | collective-permute-start | bytes 196616 | tf_op jit(solution)/shard_map/ppermute | solution.py:478
  24.9 10.4 %collective-permute-start.11 = (f32[2,64,256]{2,1,0:T(8,128)S(1)}, f32[2,64,256]{2,1,0:T(8,128)S(1)}, u32[]{:S(2)}, u32[]{:S(2)}) collective-permute-start(f32[2,64,256]{2,1,0:T(8,128)S(1)} %get-tuple-element.26), channel_id=1, source_target_pairs={{248,48},{250,50},{252,52},{254,54},{0,200},{2,202},{4,204},{6,206... | collective-permute-start | bytes 393224 | tf_op jit(solution)/shard_map/ppermute | solution.py:478
  26.2 10.4 %collective-permute-start.2 = (f32[3,64,256]{2,1,0:T(8,128)S(1)}, f32[3,64,256]{2,1,0:T(8,128)S(1)}, u32[]{:S(2)}, u32[]{:S(2)}) collective-permute-start(f32[3,64,256]{2,1,0:T(8,128)S(1)} %get-tuple-element.22), channel_id=1, source_target_pairs={{0,16},{1,17},{2,18},{3,19},{4,20},{5,21},{6,22},{7,23},{8,24},{9,... | collective-permute-start | bytes 589832 | tf_op jit(solution)/shard_map/ppermute | solution.py:478
  28.2 9.8 %collective-permute-start.7 = (f32[3,64,256]{2,1,0:T(8,128)S(1)}, f32[3,64,256]{2,1,0:T(8,128)S(1)}, u32[]{:S(2)}, u32[]{:S(2)}) collective-permute-start(f32[3,64,256]{2,1,0:T(8,128)S(1)} %get-tuple-element.24), channel_id=1, source_target_pairs={{248,56},{250,58},{252,60},{254,62},{0,192},{2,194},{4,196},{6,198... | collective-permute-start | bytes 589832 | tf_op jit(solution)/shard_map/ppermute | solution.py:478
  29.5 40.4 %collective-permute-start.1 = (f32[8,64,256]{2,1,0:T(8,128)S(1)}, f32[8,64,256]{2,1,0:T(8,128)S(1)}, u32[]{:S(2)}, u32[]{:S(2)}) collective-permute-start(f32[8,64,256]{2,1,0:T(8,128)S(1)} %get-tuple-element.21.own), channel_id=1, source_target_pairs={{8,16},{9,17},{10,18},{11,19},{12,20},{13,21},{14,22},{15,23},{16,... | collective-permute-start | bytes 1572872 | tf_op jit(solution)/shard_map/ppermute | solution.py:478
  30.2 39.7 %collective-permute-start = (f32[8,64,256]{2,1,0:T(8,128)S(1)}, f32[8,64,256]{2,1,0:T(8,128)S(1)}, u32[]{:S(2)}, u32[]{:S(2)}) collective-permute-start(f32[8,64,256]{2,1,0:T(8,128)S(1)} %get-tuple-element.21.own), channel_id=1, source_target_pairs={{0,8},{1,9},{2,10},{3,11},{4,12},{5,13},{6,14},{7,15},{8,0},{9,1},... | collective-permute-start | bytes 1572872 | tf_op jit(solution)/shard_map/ppermute | solution.py:478
  35.3 3.9 %collective-permute-start.5 = (f32[3,64,256]{2,1,0:T(8,128)S(1)}, f32[3,64,256]{2,1,0:T(8,128)S(1)}, u32[]{:S(2)}, u32[]{:S(2)}) collective-permute-start(f32[3,64,256]{2,1,0:T(8,128)S(1)} %get-tuple-element.23), channel_id=1, source_target_pairs={{248,120},{250,122},{252,124},{254,126},{0,128},{2,130},{4,132},{6... | collective-permute-start | bytes 589832 | tf_op jit(solution)/shard_map/ppermute | solution.py:478
  36.7 16.2 %collective-permute-start.4 = (f32[3,64,256]{2,1,0:T(8,128)S(1)}, f32[3,64,256]{2,1,0:T(8,128)S(1)}, u32[]{:S(2)}, u32[]{:S(2)}) collective-permute-start(f32[3,64,256]{2,1,0:T(8,128)S(1)} %get-tuple-element.23), channel_id=1, source_target_pairs={{240,256},{241,257},{242,258},{243,259},{244,260},{245,261},{246,2... | collective-permute-start | bytes 589832 | tf_op jit(solution)/shard_map/ppermute | solution.py:478
  38.0 16.2 %collective-permute-start.3 = (f32[3,64,256]{2,1,0:T(8,128)S(1)}, f32[3,64,256]{2,1,0:T(8,128)S(1)}, u32[]{:S(2)}, u32[]{:S(2)}) collective-permute-start(f32[3,64,256]{2,1,0:T(8,128)S(1)} %get-tuple-element.23), channel_id=1, source_target_pairs={{16,32},{17,33},{18,34},{19,35},{20,36},{21,37},{22,38},{23,39},{2... | collective-permute-start | bytes 589832 | tf_op jit(solution)/shard_map/ppermute | solution.py:478
  39.2 15.6 %collective-permute-start.10 = (f32[2,64,256]{2,1,0:T(8,128)S(1)}, f32[2,64,256]{2,1,0:T(8,128)S(1)}, u32[]{:S(2)}, u32[]{:S(2)}) collective-permute-start(f32[2,64,256]{2,1,0:T(8,128)S(1)} %collective-permute-done.9), channel_id=1, source_target_pairs={{192,256},{194,258},{196,260},{198,262},{56,760},{58,762},{60,764}... | collective-permute-start | bytes 393224 | tf_op jit(solution)/shard_map/ppermute | solution.py:478
  52.9 17.0 %collective-permute-start.8 = (f32[3,64,256]{2,1,0:T(8,128)S(1)}, f32[3,64,256]{2,1,0:T(8,128)S(1)}, u32[]{:S(2)}, u32[]{:S(2)}) collective-permute-start(f32[3,64,256]{2,1,0:T(8,128)S(1)} %collective-permute-done.7), channel_id=1, source_target_pairs={{56,256},{58,258},{60,260},{62,262},{192,760},{194,762},{196,764},... | collective-permute-start | bytes 589832 | tf_op jit(solution)/shard_map/ppermute | solution.py:478
  54.2 15.7 %collective-permute-start.6 = (f32[3,64,256]{2,1,0:T(8,128)S(1)}, f32[3,64,256]{2,1,0:T(8,128)S(1)}, u32[]{:S(2)}, u32[]{:S(2)}) collective-permute-start(f32[3,64,256]{2,1,0:T(8,128)S(1)} %collective-permute-done.5), channel_id=1, source_target_pairs={{120,264},{122,266},{124,268},{126,270},{128,752},{130,754},{132,7... | collective-permute-start | bytes 589832 | tf_op jit(solution)/shard_map/ppermute | solution.py:478
  54.9 15.0 %collective-permute-start.12 = (f32[2,64,256]{2,1,0:T(8,128)S(1)}, f32[2,64,256]{2,1,0:T(8,128)S(1)}, u32[]{:S(2)}, u32[]{:S(2)}) collective-permute-start(f32[2,64,256]{2,1,0:T(8,128)S(1)} %collective-permute-done.11), channel_id=1, source_target_pairs={{48,256},{50,258},{52,260},{54,262},{200,760},{202,762},{204,764},... | collective-permute-start | bytes 393224 | tf_op jit(solution)/shard_map/ppermute | solution.py:478
  70.8 14.7 %collective-permute-start.14 = (f32[18,8,256]{2,1,0:T(8,128)S(1)}, f32[18,8,256]{2,1,0:T(8,128)S(1)}, u32[]{:S(2)}, u32[]{:S(2)}) collective-permute-start(f32[18,8,256]{2,1,0:T(8,128)S(1)} %get-tuple-element.29), channel_id=1, source_target_pairs={{0,1},{1,0},{2,3},{3,2},{4,5},{5,4},{6,7},{7,6},{8,9},{9,8},{10,11... | collective-permute-start | bytes 442376 | tf_op jit(solution)/shard_map/ppermute | solution.py:478
  74.2 11.8 %collective-permute-start.15 = (f32[18,8,256]{2,1,0:T(8,128)S(1)}, f32[18,8,256]{2,1,0:T(8,128)S(1)}, u32[]{:S(2)}, u32[]{:S(2)}) collective-permute-start(f32[18,8,256]{2,1,0:T(8,128)S(1)} %get-tuple-element.30), channel_id=1, source_target_pairs={{0,7},{1,2},{2,1},{3,4},{4,3},{5,6},{6,5},{7,0},{8,15},{9,10},{10,... | collective-permute-start | bytes 442376 | tf_op jit(solution)/shard_map/ppermute | solution.py:478
  83.2 48.9 %copy-start.1 = (f32[4,64,256]{2,1,0:T(8,128)S(1)}, f32[4,64,256]{2,1,0:T(8,128)}, u32[]{:S(2)}) copy-start(f32[4,64,256]{2,1,0:T(8,128)} %kappa.1) | copy-start | bytes 786436
